TPU v7x, 32 devices: a whole 2x2x4 slice. The times are simulated.
32 devices in a mesh: leaf: 32 (over z, y, x, core).
Axes of the slice: x: 2, y: 2, z: 4, core: 2. Of those that a mesh axis runs over, the one named last changes fastest.
Arguments:
- features: bfloat16 [16384, 1024], P('leaf'), may hold values from -6 to 6
- probes: float32 [16384, 128], P('leaf'), may hold values from -6 to 6
- bases: float32 [16384, 256], P('leaf'), may hold values from -0.25 to 0.25
- transfers: float32 [32, 4, 256, 256], P('leaf'), may hold values from -1 to 1, as said below
- couplings: float32 [32, 5, 256, 256], P('leaf'), may hold values from -1 to 1, as said below
- near_list: int32 [32, 4], P('leaf'), may hold values from 0 to 31, as said below
- near_count: int32 [32], P('leaf'), may hold values from 1 to 4
Outputs:
- product: float32 [16384, 128], P('leaf')
Inputs may be any that keep to these rules, and one draw needn't show every extreme that they name: `near_list`: the first near_count[i] entries of row i are distinct leaves other than i, each at most 2 from i; the other entries equal i. Some leaf lists 4 leaves. transfers[i, l] is the same for all leaves i of one node of level l (an aligned block of 2^l leaves). couplings[i, l] is the same for all leaves i of one node of level l (an aligned block of 2^l leaves).
All inputs are finite; a program needn't handle non-finite values.
Results may differ from a plain program's by a relative error of at most 0.00095.
Values may be sent and summed in bfloat16 or wider, within the bound.
No kernel may reach another device: no remote copies, remote signals or barrier semaphores. Data moves between devices by JAX's collectives and lax.ppermute only.
A program may use at most 64 MiB of HBM per device.

v0:
```python
import jax
import jax.numpy as jnp
from jax import lax
from jax.sharding import PartitionSpec as P


def from_behind(array, axis, by):
    peers = lax.axis_size(axis)
    pairs = [(i, i + by) for i in range(peers) if 0 <= i + by < peers]
    return lax.ppermute(array, axis, pairs)


def partner(array, axis, distance):
    return lax.ppermute(array, axis, [(i, i ^ 1 << distance) for i in range(lax.axis_size(axis))])


def kernel_tile(rows_a, rows_b):
    gram_tile = lax.dot_general(
        rows_a, rows_b, (((1,), (1,)), ((), ())), preferred_element_type=jnp.float32
    )
    return gram_tile * gram_tile * (1.0 / (rows_a.shape[1] * rows_a.shape[0]))


def contract_first(matrix, values):
    return lax.dot_general(
        matrix,
        values,
        (((0,), (0,)), ((), ())),
        precision=lax.Precision.HIGHEST,
        preferred_element_type=jnp.float32,
    )


def apply_matrix(matrix, values):
    return jnp.dot(
        matrix, values, precision=lax.Precision.HIGHEST, preferred_element_type=jnp.float32
    )


def shards(features, probes, bases, transfers, couplings, near_list, near_count):
    leaf_index = lax.axis_index("leaf")
    tree_depth = transfers.shape[1]
    scale_g = (3.0 / transfers.shape[-1]) ** 0.5
    near_span = near_list.shape[1] // 2
    slot_ids = jnp.arange(near_list.shape[1], dtype=jnp.int32)
    is_live = slot_ids < near_count[0]

    def member(offset):
        return jnp.any((near_list[0] == leaf_index + offset) & is_live).astype(jnp.float32)

    near_sum = apply_matrix(kernel_tile(features, features), probes)
    for offset in range(1, near_span + 1):
        remote = from_behind(features, "leaf", -offset)
        remote_x = from_behind(probes.astype(jnp.bfloat16), "leaf", -offset).astype(probes.dtype)
        kernel = kernel_tile(features, remote)
        near_sum = near_sum + member(offset) * apply_matrix(kernel, remote_x)
        back_term = contract_first(kernel, probes)
        returned = from_behind(back_term, "leaf", offset)
        near_sum = near_sum + member(-offset) * returned
    skeleton = contract_first(bases, probes)
    levels = [skeleton]
    siblings = []
    for height in range(1, tree_depth + 1):
        factor = scale_g * 2.0 ** (-0.5 * height)
        pieces = factor * contract_first(transfers[0, height - 1], levels[-1])
        levels.append(
            pieces + partner(pieces.astype(jnp.bfloat16), "leaf", height - 1).astype(pieces.dtype)
        )
    for height in range(tree_depth + 1):
        siblings.append(partner(levels[height], "leaf", height))
    expansion = None
    for height in range(tree_depth, -1, -1):
        update = scale_g * apply_matrix(couplings[0, height], siblings[height])
        if height < tree_depth:
            update = update + scale_g * 2.0 ** (-0.5 * (height + 1)) * apply_matrix(
                transfers[0, height], expansion
            )
        expansion = update
    far_sum = apply_matrix(bases, expansion)
    return near_sum + far_sum


def solution(mesh):
    in_specs = (
        P("leaf", None),
        P("leaf", None),
        P("leaf", None),
        P("leaf", None, None, None),
        P("leaf", None, None, None),
        P("leaf", None),
        P("leaf"),
    )
    out_specs = P("leaf", None)
    return jax.shard_map(shards, mesh=mesh, in_specs=in_specs, out_specs=out_specs, check_vma=False)
```

profile of v0, /device:TPU:8, one launch (start us, length us, event | category | flops | bytes accessed | tf_op | source)
XLA Modules:
  0.0 109.1 jit_solution(5245317424175122447)
XLA Ops:
  0.0 1.0 copy-done
  1.0 1.9 %fusion.53 = f32[256,128]{1,0:T(8,128)S(1)} fusion(f32[512,256]{1,0:T(8,128)S(1)} %copy-done, f32[512,128]{1,0:T(8,128)} %param.8), kind=kOutput, calls=%fused_computation.81 | convolution fusion | flops 201326592 | bytes 917504 | tf_op jit(solution)/shard_map/dot_general | solution.py:25
  3.0 1.4 %fusion.46 = (bf16[256,128]{0,1:T(8,128)(2,1)S(1)}, f32[256,128]{0,1:T(8,128)S(1)}) fusion(f32[256,128]{1,0:T(8,128)S(1)} %fusion.53, f32[1,4,256,256]{3,2,1,0:T(8,128)} %param.10), kind=kOutput, calls=%fused_computation.74 | convolution fusion | flops 100728832 | bytes 589824 | tf_op jit(solution)/shard_map/dot_general | solution.py:25
  4.5 1.2 %collective-permute-done.7 = bf16[256,128]{0,1:T(8,128)(2,1)S(1)} collective-permute-done((bf16[256,128]{0,1:T(8,128)(2,1)S(1)}, bf16[256,128]{0,1:T(8,128)(2,1)S(1)}, u32[]{:S(2)}, u32[]{:S(2)}) %collective-permute-start.7) | collective-permute-done | bytes 65568 | tf_op jit(solution)/shard_map/ppermute | solution.py:14
  6.0 1.6 %collective-permute-start.9 = (bf16[256,128]{0,1:T(8,128)(2,1)S(1)}, bf16[256,128]{0,1:T(8,128)(2,1)S(1)}, u32[]{:S(2)}, u32[]{:S(2)}) collective-permute-start(bf16[256,128]{0,1:T(8,128)(2,1)S(1)} %get-tuple-element.11), channel_id=1, source_target_pairs={{0,2},{1,3},{2,0},{3,1},{4,6},{5,7},{6,4},{7,5},{8,10},{9,11},{10,... | collective-permute-start | bytes 196616 | tf_op jit(solution)/shard_map/ppermute | solution.py:14
  7.6 2.8 %collective-permute-done.9 = bf16[256,128]{0,1:T(8,128)(2,1)S(1)} collective-permute-done((bf16[256,128]{0,1:T(8,128)(2,1)S(1)}, bf16[256,128]{0,1:T(8,128)(2,1)S(1)}, u32[]{:S(2)}, u32[]{:S(2)}) %collective-permute-start.9) | collective-permute-done | bytes 65568 | tf_op jit(solution)/shard_map/ppermute | solution.py:14
  10.7 1.6 %collective-permute-start.11 = (bf16[256,128]{0,1:T(8,128)(2,1)S(1)}, bf16[256,128]{0,1:T(8,128)(2,1)S(1)}, u32[]{:S(2)}, u32[]{:S(2)}) collective-permute-start(bf16[256,128]{0,1:T(8,128)(2,1)S(1)} %get-tuple-element.13), channel_id=1, source_target_pairs={{0,4},{1,5},{2,6},{3,7},{4,0},{5,1},{6,2},{7,3},{8,12},{9,13},{10,... | collective-permute-start | bytes 196616 | tf_op jit(solution)/shard_map/ppermute | solution.py:14
  12.3 3.2 %collective-permute-start.3 = (bf16[512,1024]{1,0:T(8,128)(2,1)}, bf16[512,1024]{1,0:T(8,128)(2,1)}, u32[]{:S(2)}, u32[]{:S(2)}) collective-permute-start(bf16[512,1024]{1,0:T(8,128)(2,1)} %param.7), channel_id=1, source_target_pairs={{2,0},{3,1},{4,2},{5,3},{6,4},{7,5},{8,6},{9,7},{10,8},{11,9},{12,... | collective-permute-start | bytes 3145736 | tf_op jit(solution)/shard_map/ppermute | solution.py:10
  15.5 2.0 %collective-permute-start = (bf16[512,1024]{1,0:T(8,128)(2,1)}, bf16[512,1024]{1,0:T(8,128)(2,1)}, u32[]{:S(2)}, u32[]{:S(2)}) collective-permute-start(bf16[512,1024]{1,0:T(8,128)(2,1)} %param.7), channel_id=1, source_target_pairs={{1,0},{2,1},{3,2},{4,3},{5,4},{6,5},{7,6},{8,7},{9,8},{10,9},{11,1... | collective-permute-start | bytes 3145736 | tf_op jit(solution)/shard_map/ppermute | solution.py:10
  17.6 0.7 convert_element_type.43
  18.2 4.6 %collective-permute-start.4 = (bf16[512,128]{1,0:T(8,128)(2,1)}, bf16[512,128]{1,0:T(8,128)(2,1)}, u32[]{:S(2)}, u32[]{:S(2)}) collective-permute-start(bf16[512,128]{1,0:T(8,128)(2,1)} %convert_element_type.43), channel_id=1, source_target_pairs={{2,0},{3,1},{4,2},{5,3},{6,4},{7,5},{8,6},{9,7},{10,8},{11,9},{12,... | collective-permute-start | bytes 393224 | tf_op jit(solution)/shard_map/ppermute | solution.py:10
  23.5 2.6 %fusion = f32[512,512]{1,0:T(8,128)S(1)} fusion(bf16[512,1024]{1,0:T(8,128)(2,1)} %param.7), kind=kOutput, calls=%fused_computation.3 | convolution fusion | flops 537395200 | bytes 2097152 | tf_op jit(solution)/shard_map/dot_general | solution.py:18
  26.1 30.9 %collective-permute-done.13 = bf16[256,128]{0,1:T(8,128)(2,1)S(1)} collective-permute-done((bf16[256,128]{0,1:T(8,128)(2,1)S(1)}, bf16[256,128]{0,1:T(8,128)(2,1)S(1)}, u32[]{:S(2)}, u32[]{:S(2)}) %collective-permute-start.13) | collective-permute-done | bytes 65568 | tf_op jit(solution)/shard_map/ppermute | solution.py:14
  57.7 2.6 %collective-permute-start.14 = (f32[256,128]{0,1:T(8,128)}, f32[256,128]{0,1:T(8,128)}, u32[]{:S(2)}, u32[]{:S(2)}) collective-permute-start(f32[256,128]{0,1:T(8,128)} %convert_add_fusion), channel_id=1, source_target_pairs={{0,16},{1,17},{2,18},{3,19},{4,20},{5,21},{6,22},{7,23},{8,24},{9,... | collective-permute-start | bytes 393224 | tf_op jit(solution)/shard_map/ppermute | solution.py:14
  60.3 1.0 fusion.50
  62.0 0.7 fusion.45
  65.1 2.5 %collective-permute-start.12 = (f32[256,128]{0,1:T(8,128)}, f32[256,128]{0,1:T(8,128)S(1)}, u32[]{:S(2)}, u32[]{:S(2)}) collective-permute-start(f32[256,128]{0,1:T(8,128)} %copy-done.7), channel_id=1, source_target_pairs={{0,8},{1,9},{2,10},{3,11},{4,12},{5,13},{6,14},{7,15},{8,0},{9,1},... | collective-permute-start | bytes 393224 | tf_op jit(solution)/shard_map/ppermute | solution.py:14
  67.7 1.3 %convolution_multiply_fusion.9 = f32[128,256]{1,0:T(8,128)S(1)} fusion(f32[256,128]{0,1:T(8,128)} %collective-permute-done.14, f32[1,5,256,256]{3,2,1,0:T(8,128)S(1)} %copy-done.3), kind=kOutput, calls=%fused_computation.18 | convolution fusion | flops 100696064 | bytes 524288 | tf_op jit(solution)/shard_map/dot_general | solution.py:35
  69.4 1.4 %collective-permute-done.12 = f32[256,128]{0,1:T(8,128)S(1)} collective-permute-done((f32[256,128]{0,1:T(8,128)}, f32[256,128]{0,1:T(8,128)S(1)}, u32[]{:S(2)}, u32[]{:S(2)}) %collective-permute-start.12) | collective-permute-done | bytes 131104 | tf_op jit(solution)/shard_map/ppermute | solution.py:14
  71.7 4.4 %collective-permute-done.10 = f32[256,128]{0,1:T(8,128)S(1)} collective-permute-done((f32[256,128]{0,1:T(8,128)}, f32[256,128]{0,1:T(8,128)S(1)}, u32[]{:S(2)}, u32[]{:S(2)}) %collective-permute-start.10) | collective-permute-done | bytes 131104 | tf_op jit(solution)/shard_map/ppermute | solution.py:14
  76.8 4.1 %collective-permute-done.8 = f32[256,128]{0,1:T(8,128)S(1)} collective-permute-done((f32[256,128]{0,1:T(8,128)S(1)}, f32[256,128]{0,1:T(8,128)S(1)}, u32[]{:S(2)}, u32[]{:S(2)}) %collective-permute-start.8) | collective-permute-done | bytes 131104 | tf_op jit(solution)/shard_map/ppermute | solution.py:14
  81.0 1.9 %collective-permute-start.1 = (bf16[512,128]{1,0:T(8,128)(2,1)}, bf16[512,128]{1,0:T(8,128)(2,1)S(1)}, u32[]{:S(2)}, u32[]{:S(2)}) collective-permute-start(bf16[512,128]{1,0:T(8,128)(2,1)} %convert_element_type.43), channel_id=1, source_target_pairs={{1,0},{2,1},{3,2},{4,3},{5,4},{6,5},{7,6},{8,7},{9,8},{10,9},{11,1... | collective-permute-start | bytes 393224 | tf_op jit(solution)/shard_map/ppermute | solution.py:10
  83.7 1.3 %fusion.15 = f32[128,256]{1,0:T(8,128)S(1)} fusion(f32[128,256]{1,0:T(8,128)S(1)} %convolution_multiply_fusion.5, f32[256,128]{1,0:T(8,128)} %collective-permute-done.6, f32[1,5,256,256]{3,2,1,0:T(8,128)S(1)} %copy-done.3), kind=kOutput, calls=%fused_computation.34 | convolution fusion | flops 100728832 | bytes 655360 | tf_op jit(solution)/shard_map/dot_general | solution.py:35
  85.0 2.3 %fusion.1 = f32[512,512]{1,0:T(8,128)S(1)} fusion(bf16[512,1024]{1,0:T(8,128)(2,1)} %param.7, bf16[512,1024]{1,0:T(8,128)(2,1)} %collective-permute-done), kind=kOutput, calls=%fused_computation.4 | convolution fusion | flops 537395200 | bytes 3145728 | tf_op jit(solution)/shard_map/dot_general | solution.py:18
  87.3 1.8 %fusion.51 = f32[512,128]{1,0:T(8,128)S(1)} fusion(f32[512,512]{1,0:T(8,128)S(1)} %fusion.1, f32[512,128]{1,0:T(8,128)S(1)} %copy-done.1), kind=kOutput, calls=%fused_computation.79 | convolution fusion | flops 402653184 | bytes 1572864 | tf_op jit(solution)/shard_map/dot_general | solution.py:25
  89.1 2.6 %collective-permute-start.2 = (f32[512,128]{1,0:T(8,128)S(1)}, f32[512,128]{1,0:T(8,128)S(1)}, u32[]{:S(2)}, u32[]{:S(2)}) collective-permute-start(f32[512,128]{1,0:T(8,128)S(1)} %fusion.51), channel_id=1, source_target_pairs={{0,1},{1,2},{2,3},{3,4},{4,5},{5,6},{6,7},{7,8},{8,9},{9,10},{10,1... | collective-permute-start | bytes 786440 | tf_op jit(solution)/shard_map/ppermute | solution.py:10
  91.7 2.3 %fusion.2 = f32[512,512]{1,0:T(8,128)S(1)} fusion(bf16[512,1024]{1,0:T(8,128)(2,1)} %param.7, bf16[512,1024]{1,0:T(8,128)(2,1)} %collective-permute-done.3), kind=kOutput, calls=%fused_computation.5 | convolution fusion | flops 537395200 | bytes 3145728 | tf_op jit(solution)/shard_map/dot_general | solution.py:18
  94.0 1.8 %fusion.52 = f32[512,128]{1,0:T(8,128)S(1)} fusion(f32[512,512]{1,0:T(8,128)S(1)} %fusion.2, f32[512,128]{1,0:T(8,128)S(1)} %copy-done.1), kind=kOutput, calls=%fused_computation.80 | convolution fusion | flops 402653184 | bytes 1572864 | tf_op jit(solution)/shard_map/dot_general | solution.py:25
  95.9 1.9 %collective-permute-start.5 = (f32[512,128]{1,0:T(8,128)S(1)}, f32[512,128]{1,0:T(8,128)S(1)}, u32[]{:S(2)}, u32[]{:S(2)}) collective-permute-start(f32[512,128]{1,0:T(8,128)S(1)} %fusion.52), channel_id=1, source_target_pairs={{0,2},{1,3},{2,4},{3,5},{4,6},{5,7},{6,8},{7,9},{8,10},{9,11},{10,... | collective-permute-start | bytes 786440 | tf_op jit(solution)/shard_map/ppermute | solution.py:10
  98.4 1.5 %convolution_multiply_fusion.3 = f32[512,128]{1,0:T(8,128)S(1)} fusion(f32[512,512]{1,0:T(8,128)S(1)} %fusion.2, bf16[512,128]{1,0:T(8,128)(2,1)} %collective-permute-done.4, f32[]{:T(128)S(6)} %convert_element_type.45), kind=kOutput, calls=%fused_computation.7 | convolution fusion | flops 402718720 | bytes 1441796 | tf_op jit(solution)/shard_map/dot_general | solution.py:35
  99.9 7.9 %collective-permute-done.5 = f32[512,128]{1,0:T(8,128)S(1)} collective-permute-done((f32[512,128]{1,0:T(8,128)S(1)}, f32[512,128]{1,0:T(8,128)S(1)}, u32[]{:S(2)}, u32[]{:S(2)}) %collective-permute-start.5) | collective-permute-done | bytes 262176 | tf_op jit(solution)/shard_map/ppermute | solution.py:10
  107.8 1.3 %fusion.7 = f32[512,128]{1,0:T(8,128)} fusion(f32[512,128]{1,0:T(8,128)S(1)} %convolution_bitcast_fusion, f32[512,128]{1,0:T(8,128)S(1)} %convolution_multiply_fusion.3, f32[512,128]{1,0:T(8,128)S(1)} %fusion.50, f32[512,512]{1,0:T(8,128)S(1)} %fusion.1, bf16[512,128]{1,0:T(8,128)(2,1)S(1)} %collective-permute-done.1, ...), kind=kOutput, calls=%fused_computation.13 | convolution fusion | flops 403177472 | bytes 2752524 | tf_op jit(solution)/shard_map/dot_general | solution.py:35
  (45 shorter events, 5.4 us)
Async XLA Ops:
  0.0 1.0 copy-start
  0.0 5.7 %copy-start.2 = (f32[1,4,256,256]{3,2,1,0:T(8,128)S(1)}, f32[1,4,256,256]{3,2,1,0:T(8,128)}, u32[]{:S(2)}) copy-start(f32[1,4,256,256]{3,2,1,0:T(8,128)} %param.10) | copy-start | bytes 3145732
  3.0 14.6 %copy-start.1 = (f32[512,128]{1,0:T(8,128)S(1)}, f32[512,128]{1,0:T(8,128)}, u32[]{:S(2)}) copy-start(f32[512,128]{1,0:T(8,128)} %param.8) | copy-start | bytes 786436
  4.4 1.3 %collective-permute-start.7 = (bf16[256,128]{0,1:T(8,128)(2,1)S(1)}, bf16[256,128]{0,1:T(8,128)(2,1)S(1)}, u32[]{:S(2)}, u32[]{:S(2)}) collective-permute-start(bf16[256,128]{0,1:T(8,128)(2,1)S(1)} %get-tuple-element.9), channel_id=1, source_target_pairs={{0,1},{1,0},{2,3},{3,2},{4,5},{5,4},{6,7},{7,6},{8,9},{9,8},{10,11... | collective-permute-start | bytes 196616 | tf_op jit(solution)/shard_map/ppermute | solution.py:14
  5.7 17.4 %copy-start.4 = (f32[256,128]{0,1:T(8,128)}, f32[256,128]{0,1:T(8,128)S(1)}, u32[]{:S(2)}) copy-start(f32[256,128]{0,1:T(8,128)S(1)} %convert_add_fusion.3) | copy-start | bytes 393220
  6.0 4.3 %collective-permute-start.9 = (bf16[256,128]{0,1:T(8,128)(2,1)S(1)}, bf16[256,128]{0,1:T(8,128)(2,1)S(1)}, u32[]{:S(2)}, u32[]{:S(2)}) collective-permute-start(bf16[256,128]{0,1:T(8,128)(2,1)S(1)} %get-tuple-element.11), channel_id=1, source_target_pairs={{0,2},{1,3},{2,0},{3,1},{4,6},{5,7},{6,4},{7,5},{8,10},{9,11},{10,... | collective-permute-start | bytes 196616 | tf_op jit(solution)/shard_map/ppermute | solution.py:14
  10.4 15.7 %copy-start.6 = (f32[256,128]{0,1:T(8,128)}, f32[256,128]{0,1:T(8,128)S(1)}, u32[]{:S(2)}) copy-start(f32[256,128]{0,1:T(8,128)S(1)} %convert_add_fusion.2) | copy-start | bytes 393220
  10.7 12.1 %collective-permute-start.11 = (bf16[256,128]{0,1:T(8,128)(2,1)S(1)}, bf16[256,128]{0,1:T(8,128)(2,1)S(1)}, u32[]{:S(2)}, u32[]{:S(2)}) collective-permute-start(bf16[256,128]{0,1:T(8,128)(2,1)S(1)} %get-tuple-element.13), channel_id=1, source_target_pairs={{0,4},{1,5},{2,6},{3,7},{4,0},{5,1},{6,2},{7,3},{8,12},{9,13},{10,... | collective-permute-start | bytes 196616 | tf_op jit(solution)/shard_map/ppermute | solution.py:14
  12.3 71.4 %collective-permute-start.6 = (f32[256,128]{1,0:T(8,128)S(1)}, f32[256,128]{1,0:T(8,128)}, u32[]{:S(2)}, u32[]{:S(2)}) collective-permute-start(f32[256,128]{1,0:T(8,128)S(1)} %fusion.53), channel_id=1, source_target_pairs={{0,1},{1,0},{2,3},{3,2},{4,5},{5,4},{6,7},{7,6},{8,9},{9,8},{10,11... | collective-permute-start | bytes 393224 | tf_op jit(solution)/shard_map/ppermute | solution.py:14
  12.3 79.5 %collective-permute-start.3 = (bf16[512,1024]{1,0:T(8,128)(2,1)}, bf16[512,1024]{1,0:T(8,128)(2,1)}, u32[]{:S(2)}, u32[]{:S(2)}) collective-permute-start(bf16[512,1024]{1,0:T(8,128)(2,1)} %param.7), channel_id=1, source_target_pairs={{2,0},{3,1},{4,2},{5,3},{6,4},{7,5},{8,6},{9,7},{10,8},{11,9},{12,... | collective-permute-start | bytes 3145736 | tf_op jit(solution)/shard_map/ppermute | solution.py:10
  15.5 69.5 %collective-permute-start = (bf16[512,1024]{1,0:T(8,128)(2,1)}, bf16[512,1024]{1,0:T(8,128)(2,1)}, u32[]{:S(2)}, u32[]{:S(2)}) collective-permute-start(bf16[512,1024]{1,0:T(8,128)(2,1)} %param.7), channel_id=1, source_target_pairs={{1,0},{2,1},{3,2},{4,3},{5,4},{6,5},{7,6},{8,7},{9,8},{10,9},{11,1... | collective-permute-start | bytes 3145736 | tf_op jit(solution)/shard_map/ppermute | solution.py:10
  18.2 80.1 %collective-permute-start.4 = (bf16[512,128]{1,0:T(8,128)(2,1)}, bf16[512,128]{1,0:T(8,128)(2,1)}, u32[]{:S(2)}, u32[]{:S(2)}) collective-permute-start(bf16[512,128]{1,0:T(8,128)(2,1)} %convert_element_type.43), channel_id=1, source_target_pairs={{2,0},{3,1},{4,2},{5,3},{6,4},{7,5},{8,6},{9,7},{10,8},{11,9},{12,... | collective-permute-start | bytes 393224 | tf_op jit(solution)/shard_map/ppermute | solution.py:10
  22.9 0.7 copy-start.7
  23.5 33.5 %collective-permute-start.13 = (bf16[256,128]{0,1:T(8,128)(2,1)S(1)}, bf16[256,128]{0,1:T(8,128)(2,1)S(1)}, u32[]{:S(2)}, u32[]{:S(2)}) collective-permute-start(bf16[256,128]{0,1:T(8,128)(2,1)S(1)} %get-tuple-element.15), channel_id=1, source_target_pairs={{0,8},{1,9},{2,10},{3,11},{4,12},{5,13},{6,14},{7,15},{8,0},{9,1},... | collective-permute-start | bytes 196616 | tf_op jit(solution)/shard_map/ppermute | solution.py:14
  26.1 35.8 %copy-start.8 = (s32[1,4]{1,0:T(1,128)S(1)}, s32[1,4]{1,0:T(1,128)}, u32[]{:S(2)}) copy-start(s32[1,4]{1,0:T(1,128)} %param.12) | copy-start | bytes 52
  26.1 41.6 %copy-start.3 = (f32[1,5,256,256]{3,2,1,0:T(8,128)S(1)}, f32[1,5,256,256]{3,2,1,0:T(8,128)}, u32[]{:S(2)}) copy-start(f32[1,5,256,256]{3,2,1,0:T(8,128)} %param.11) | copy-start | bytes 3932164
  57.7 7.4 %collective-permute-start.14 = (f32[256,128]{0,1:T(8,128)}, f32[256,128]{0,1:T(8,128)}, u32[]{:S(2)}, u32[]{:S(2)}) collective-permute-start(f32[256,128]{0,1:T(8,128)} %convert_add_fusion), channel_id=1, source_target_pairs={{0,16},{1,17},{2,18},{3,19},{4,20},{5,21},{6,22},{7,23},{8,24},{9,... | collective-permute-start | bytes 393224 | tf_op jit(solution)/shard_map/ppermute | solution.py:14
  65.1 10.9 %copy-start.5 = (f32[256,128]{0,1:T(8,128)S(1)}, f32[256,128]{0,1:T(8,128)}, u32[]{:S(2)}) copy-start(f32[256,128]{0,1:T(8,128)} %copy-done.4) | copy-start | bytes 393220
  65.1 5.7 %collective-permute-start.12 = (f32[256,128]{0,1:T(8,128)}, f32[256,128]{0,1:T(8,128)S(1)}, u32[]{:S(2)}, u32[]{:S(2)}) collective-permute-start(f32[256,128]{0,1:T(8,128)} %copy-done.7), channel_id=1, source_target_pairs={{0,8},{1,9},{2,10},{3,11},{4,12},{5,13},{6,14},{7,15},{8,0},{9,1},... | collective-permute-start | bytes 393224 | tf_op jit(solution)/shard_map/ppermute | solution.py:14
  70.8 5.2 %collective-permute-start.10 = (f32[256,128]{0,1:T(8,128)}, f32[256,128]{0,1:T(8,128)S(1)}, u32[]{:S(2)}, u32[]{:S(2)}) collective-permute-start(f32[256,128]{0,1:T(8,128)} %copy-done.6), channel_id=1, source_target_pairs={{0,4},{1,5},{2,6},{3,7},{4,0},{5,1},{6,2},{7,3},{8,12},{9,13},{10,... | collective-permute-start | bytes 393224 | tf_op jit(solution)/shard_map/ppermute | solution.py:14
  76.0 5.0 %collective-permute-start.8 = (f32[256,128]{0,1:T(8,128)S(1)}, f32[256,128]{0,1:T(8,128)S(1)}, u32[]{:S(2)}, u32[]{:S(2)}) collective-permute-start(f32[256,128]{0,1:T(8,128)S(1)} %copy-done.5), channel_id=1, source_target_pairs={{0,2},{1,3},{2,0},{3,1},{4,6},{5,7},{6,4},{7,5},{8,10},{9,11},{10,... | collective-permute-start | bytes 393224 | tf_op jit(solution)/shard_map/ppermute | solution.py:14
  81.0 18.9 %collective-permute-start.1 = (bf16[512,128]{1,0:T(8,128)(2,1)}, bf16[512,128]{1,0:T(8,128)(2,1)S(1)}, u32[]{:S(2)}, u32[]{:S(2)}) collective-permute-start(bf16[512,128]{1,0:T(8,128)(2,1)} %convert_element_type.43), channel_id=1, source_target_pairs={{1,0},{2,1},{3,2},{4,3},{5,4},{6,5},{7,6},{8,7},{9,8},{10,9},{11,1... | collective-permute-start | bytes 393224 | tf_op jit(solution)/shard_map/ppermute | solution.py:10
  89.1 10.8 %collective-permute-start.2 = (f32[512,128]{1,0:T(8,128)S(1)}, f32[512,128]{1,0:T(8,128)S(1)}, u32[]{:S(2)}, u32[]{:S(2)}) collective-permute-start(f32[512,128]{1,0:T(8,128)S(1)} %fusion.51), channel_id=1, source_target_pairs={{0,1},{1,2},{2,3},{3,4},{4,5},{5,6},{6,7},{7,8},{8,9},{9,10},{10,1... | collective-permute-start | bytes 786440 | tf_op jit(solution)/shard_map/ppermute | solution.py:10
  95.9 11.9 %collective-permute-start.5 = (f32[512,128]{1,0:T(8,128)S(1)}, f32[512,128]{1,0:T(8,128)S(1)}, u32[]{:S(2)}, u32[]{:S(2)}) collective-permute-start(f32[512,128]{1,0:T(8,128)S(1)} %fusion.52), channel_id=1, source_target_pairs={{0,2},{1,3},{2,4},{3,5},{4,6},{5,7},{6,8},{7,9},{8,10},{9,11},{10,... | collective-permute-start | bytes 786440 | tf_op jit(solution)/shard_map/ppermute | solution.py:10
where the time goes:
time: 110 us; the launch traced here: 109 us
  waiting for transfers between devices  52.7 us (48%)
  matrix products  24.7 us (22%)
  starting transfers between devices  24.6 us (22%)
  between operations  3.51 us (3%)
  other arithmetic  2.09 us (2%)
  local copies, waits for them, and re-layouts  1.42 us (1%)
    ppermute x9, waiting for transfers between devices, partner(): lax.ppermute(array, axis, [(i, i ^ 1 << distance) for i in range(lax.axis...  44.9 us
    ppermute x6, starting transfers between devices, from_behind(): return lax.ppermute(array, axis, pairs)  16.3 us
    dot_general x13, matrix products, apply_matrix(): jnp.dot(matrix, values, precision=lax.Precision.HIGHEST, preferred_elemen...  9.81 us
    ppermute x9, starting transfers between devices, partner(): lax.ppermute(array, axis, [(i, i ^ 1 << distance) for i in range(lax.axis...  8.36 us
    ppermute x6, waiting for transfers between devices, from_behind(): return lax.ppermute(array, axis, pairs)  7.87 us
    dot_general x7, matrix products, contract_first(): lax.dot_general(matrix, values, (((0,), (0,)), ((), ())), precision=lax.P...  7.77 us
    dot_general x3, matrix products, kernel_tile(): lax.dot_general(rows_a, rows_b, (((1,), (1,)), ((), ())), preferred_eleme...  7.14 us
  transfers between devices with their start and end apart: 15, of which 7 were waited for; matrix products, arithmetic and copies ran while one was open for 20% of the time, Pallas kernels for 0%

commit v1 on v0

v1 whole, which is shorter than its diff:
```python
import functools

import jax
import jax.numpy as jnp
from jax import lax
from jax.experimental import pallas as pl
from jax.experimental.pallas import tpu as pltpu
from jax.sharding import PartitionSpec as P

BF16 = jnp.bfloat16
F32 = jnp.float32
VMEM = pl.BlockSpec(memory_space=pltpu.VMEM)
SMEM = pl.BlockSpec(memory_space=pltpu.SMEM)
NN = (((1,), (0,)), ((), ()))
NT = (((1,), (1,)), ((), ()))
TN = (((0,), (0,)), ((), ()))
FLAG_ROWS = 16
LIMIT = 16 << 20


def dot(a, b, dims):
    return lax.dot_general(a, b, dims, preferred_element_type=F32)


def halves(a):
    high = a.astype(BF16)
    return high, (a - high.astype(F32)).astype(BF16)


def dot_wide(a, b, dims):
    a_high, a_low = halves(a)
    b_high, b_low = halves(b)
    return dot(a_high, b_high, dims) + (dot(a_high, b_low, dims) + dot(a_low, b_high, dims))


def dot_half(a16, b, dims):
    b_high, b_low = halves(b)
    return dot(a16, b_high, dims) + dot(a16, b_low, dims)


def member(list_ref, count_ref, offset):
    index = lax.axis_index("leaf")
    found = jnp.float32(0.0)
    for slot in range(list_ref.shape[1]):
        hit = (list_ref[0, slot] == index + offset) & (slot < count_ref[0])
        found = jnp.where(hit, jnp.float32(1.0), found)
    return found


def call(kernel, name, outs, specs, flops, *args):
    out_bytes = sum(o.size * o.dtype.itemsize for o in outs)
    in_bytes = sum(a.size * a.dtype.itemsize for a in args)
    return pl.pallas_call(
        kernel,
        name=name,
        out_shape=outs,
        in_specs=specs,
        out_specs=[VMEM] * len(outs),
        compiler_params=pltpu.CompilerParams(vmem_limit_bytes=LIMIT),
        cost_estimate=pl.CostEstimate(flops=flops, bytes_accessed=in_bytes + out_bytes, transcendentals=0),
    )(*args)


def leaf_kernel(c1, bases_ref, x_ref, transfer_ref, list_ref, count_ref, message_ref, xmessage_ref):
    x = x_ref[...]
    rows, probes = x.shape
    skeleton = dot_wide(x, bases_ref[...], TN)
    message_ref[:probes] = skeleton
    message_ref[probes:] = c1 * dot_wide(skeleton, transfer_ref[0, 0], NN)
    xmessage_ref[:rows] = x.astype(BF16)
    for place, offset in ((0, -2), (1, -1)):
        flag = member(list_ref, count_ref, offset)
        xmessage_ref[rows + place * FLAG_ROWS : rows + (place + 1) * FLAG_ROWS] = jnp.full(
            (FLAG_ROWS, probes), flag, F32
        ).astype(BF16)


def up_kernel(level, factor, own_ref, got_ref, transfer_ref, message_ref, next_ref):
    probes = own_ref.shape[0]
    skeleton = own_ref[...] + got_ref[probes:].astype(F32)
    message_ref[:probes] = skeleton.astype(message_ref.dtype)
    if factor is not None:
        moved = factor * dot_wide(skeleton, transfer_ref[0, level], NN)
        message_ref[probes:] = moved.astype(message_ref.dtype)
        next_ref[...] = moved


def down_kernel(scale_g, factors, got0_ref, *refs):
    depth = len(factors)
    gots = [got0_ref, *refs[:depth]]
    coupling_ref, transfer_ref, bases_ref, out_ref = refs[depth:]
    probes = out_ref.shape[1]
    expansion = None
    for level in range(depth, -1, -1):
        got = gots[level][:probes]
        wide = dot_wide if got.dtype == F32 else dot_half
        update = scale_g * wide(got, coupling_ref[0, level], NT)
        if level < depth:
            update = update + factors[level] * dot_wide(expansion, transfer_ref[0, level], NT)
        expansion = update
    out_ref[...] = dot_wide(bases_ref[...], expansion, NT)


def tile(rows_a, rows_b, scale):
    gram = dot(rows_a, rows_b, NT)
    return halves(gram * gram * scale)


def self_kernel(scale, f_ref, x_ref, out_ref):
    high, low = tile(f_ref[...], f_ref[...], scale)
    x_high, x_low = halves(x_ref[...])
    out_ref[...] = dot(high, x_high, NN) + (dot(high, x_low, NN) + dot(low, x_high, NN))


def times(parts, x16):
    return dot(parts[0], x16, NN) + dot(parts[1], x16, NN)


def times_back(parts, x16):
    return (dot(x16, parts[0], TN) + dot(x16, parts[1], TN)).T


def pair_kernel(scale, f_ref, g_ref, near_ref, x_ref, xs_ref, list_ref, count_ref, out_ref, sib_ref):
    odd = lax.rem(lax.axis_index("leaf"), 2) == 1
    rows = near_ref.shape[0]

    @pl.when(odd)
    def _():
        parts = tile(g_ref[...], f_ref[...], scale)
        sib_ref[...] = times(parts, x_ref[:rows])
        flag = member(list_ref, count_ref, -1)
        out_ref[...] = near_ref[...] + flag * times_back(parts, xs_ref[:rows])

    @pl.when(jnp.logical_not(odd))
    def _():
        out_ref[...] = near_ref[...]
        sib_ref[...] = jnp.zeros_like(sib_ref)


def chunk_kernel(scale, first, f_ref, g_ref, h_ref, near_ref, sib_in_ref, x_ref, xs_ref, xh_ref, list_ref, count_ref, out_ref, sib_ref, back_ref):
    even = lax.rem(lax.axis_index("leaf"), 2) == 0
    rows = near_ref.shape[0]
    size = h_ref.shape[0]
    xh = xh_ref[first : first + size]
    parts = tile(f_ref[...], h_ref[...], scale)
    out_ref[...] = near_ref[...] + member(list_ref, count_ref, 2) * times(parts, xh)
    flag2 = xh_ref[rows : rows + 1].astype(F32)
    flag1 = xh_ref[rows + FLAG_ROWS : rows + FLAG_ROWS + 1].astype(F32)
    back = flag2 * times_back(parts, x_ref[:rows])

    @pl.when(even)
    def _():
        cross = tile(g_ref[...], h_ref[...], scale)
        sib_ref[...] = sib_in_ref[...] + times(cross, xh)
        back_ref[...] = (back + flag1 * times_back(cross, xs_ref[:rows])).astype(BF16)

    @pl.when(jnp.logical_not(even))
    def _():
        sib_ref[...] = sib_in_ref[...]
        back_ref[...] = back.astype(BF16)


def final_kernel(near_ref, far_ref, sib_ref, list_ref, count_ref, *refs):
    out_ref = refs[-1]
    flag = member(list_ref, count_ref, 1)
    at = 0
    for back_ref in refs[:-1]:
        rows = slice(at, at + back_ref.shape[0])
        out_ref[rows] = near_ref[rows] + far_ref[rows] + flag * sib_ref[rows].astype(F32) + back_ref[...].astype(F32)
        at += back_ref.shape[0]


def moved(array, by):
    peers = lax.axis_size("leaf")
    return lax.ppermute(array, "leaf", [(i, i + by) for i in range(peers) if 0 <= i + by < peers])


def partner(array, level):
    return lax.ppermute(array, "leaf", [(i, i ^ 1 << level) for i in range(lax.axis_size("leaf"))])


def chunks_of(rows):
    quarter = rows // 4
    return [(0, quarter), (quarter, quarter), (2 * quarter, quarter), (3 * quarter, quarter)]


def shards(features, probes, bases, transfers, couplings, near_list, near_count):
    rows, width = features.shape
    count = probes.shape[1]
    rank = bases.shape[1]
    depth = transfers.shape[1]
    scale = 1.0 / (rows * width)
    scale_g = (3.0 / rank) ** 0.5
    factors = [scale_g * 2.0 ** (-0.5 * (level + 1)) for level in range(depth)]
    shape = jax.ShapeDtypeStruct

    message, own_x = call(
        functools.partial(leaf_kernel, factors[0]),
        "leaf",
        [shape((2 * count, rank), F32), shape((rows + 2 * FLAG_ROWS, count), BF16)],
        [VMEM] * 3 + [SMEM] * 2,
        6 * rows * rank * count,
        bases, probes, transfers, near_list, near_count,
    )
    sib_features = partner(features, 0)
    sib_x = partner(own_x, 0)
    far_x = moved(own_x, -2)
    pieces = chunks_of(rows)
    far_features = [moved(features[a : a + n], -2) for a, n in pieces]

    gots = [partner(message, 0)]
    own = message[count:]
    for level in range(1, depth + 1):
        last = level == depth
        outs = [shape((count if last else 2 * count, rank), BF16), shape((count, rank), F32)]
        message, own = call(
            functools.partial(up_kernel, level, None if last else factors[level]),
            f"up{level}",
            outs,
            [VMEM] * 3,
            6 * rank * rank * count,
            own, gots[-1], transfers,
        )
        gots.append(partner(message, level))
    (far,) = call(
        functools.partial(down_kernel, scale_g, factors),
        "down",
        [shape((rows, count), F32)],
        [VMEM] * (depth + 4),
        6 * count * rank * (rank * (2 * depth + 1) + rows),
        *gots, couplings, transfers, bases,
    )

    tile_flops = 2 * rows * rows * (width + 4 * count)
    (near,) = call(
        functools.partial(self_kernel, scale),
        "self",
        [shape((rows, count), F32)],
        [VMEM, VMEM],
        tile_flops,
        features, probes,
    )
    near, sib = call(
        functools.partial(pair_kernel, scale),
        "pair",
        [shape((rows, count), F32)] * 2,
        [VMEM] * 5 + [SMEM] * 2,
        tile_flops,
        features, sib_features, near, own_x, sib_x, near_list, near_count,
    )
    backs = []
    for (first, size), part in zip(pieces, far_features):
        near, sib, back = call(
            functools.partial(chunk_kernel, scale, first),
            f"chunk{first}",
            [shape((rows, count), F32), shape((rows, count), F32), shape((size, count), BF16)],
            [VMEM] * 8 + [SMEM] * 2,
            tile_flops * 2 * size // rows,
            features, sib_features, part, near, sib, own_x, sib_x, far_x, near_list, near_count,
        )
        backs.append(moved(back, 2))
    sib_got = partner(sib.astype(BF16), 0)
    (out,) = call(
        final_kernel,
        "final",
        [shape((rows, count), F32)],
        [VMEM] * 3 + [SMEM] * 2 + [VMEM] * len(backs),
        6 * rows * count,
        near, far, sib_got, near_list, near_count, *backs,
    )
    return out


def solution(mesh):
    in_specs = (
        P("leaf", None),
        P("leaf", None),
        P("leaf", None),
        P("leaf", None, None, None),
        P("leaf", None, None, None),
        P("leaf", None),
        P("leaf"),
    )
    out_specs = P("leaf", None)
    return jax.shard_map(shards, mesh=mesh, in_specs=in_specs, out_specs=out_specs, check_vma=False)
```

time: 110 us -> 74.7 us (0.68)
  waiting for transfers between devices: 52.7 us -> 17 us
  matrix products: 24.7 us -> 0 us
  Pallas kernels: 0 us -> 17.7 us
  starting transfers between devices: 24.6 us -> 34.2 us
  local copies, waits for them, and re-layouts: 1.42 us -> 4.41 us
  between operations: 3.51 us -> 0.99 us
  other arithmetic: 2.09 us -> 0.02 us
    ppermute x15 -> x17, waiting for transfers between devices: 52.7 us -> 17 us  [the longest x9 11.7 us: moved(): lax.ppermute(array, 'leaf', [(i, i + by) for i in range(peers) if 0 <= i...]
    dot_general x23 -> x0, matrix products: 24.7 us -> none  [the longest x13 9.81 us: apply_matrix(): jnp.dot(matrix, values, precision=lax.Precision.HIGHEST, preferred_elemen...]
    pallas_call x0 -> x13, Pallas kernels: none -> 17.7 us  [call(): pl.pallas_call(kernel, name=name, out_shape=outs, in_specs=specs, out_spe...]
    ppermute x15 -> x17, starting transfers between devices: 24.6 us -> 34.2 us  [the longest x9 27.3 us: moved(): lax.ppermute(array, 'leaf', [(i, i + by) for i in range(peers) if 0 <= i...]
    unnamed x18, local copies, waits for them, and re-layouts: 1.42 us -> 4.31 us
  transfers between devices with their start and end apart: 15 -> 17, of which waited for: 7 -> 4; matrix products, arithmetic and copies ran while one was open for 20% -> 0% of each run, Pallas kernels for 0% -> 22%
where the time goes in v1:
time: 74.7 us; the launch traced here: 74.3 us
  starting transfers between devices  34.2 us (46%)
  Pallas kernels  17.7 us (24%)
  waiting for transfers between devices  17 us (23%)
  local copies, waits for them, and re-layouts  4.41 us (6%)
  between operations  0.99 us (1%)
    ppermute x9, starting transfers between devices, moved(): lax.ppermute(array, 'leaf', [(i, i + by) for i in range(peers) if 0 <= i...  27.3 us
    pallas_call x13, Pallas kernels, call(): pl.pallas_call(kernel, name=name, out_shape=outs, in_specs=specs, out_spe...  17.7 us
    ppermute x9, waiting for transfers between devices, moved(): lax.ppermute(array, 'leaf', [(i, i + by) for i in range(peers) if 0 <= i...  11.7 us
    ppermute x8, starting transfers between devices, partner(): lax.ppermute(array, 'leaf', [(i, i ^ 1 << level) for i in range(lax.axis_...  6.91 us
    ppermute x8, waiting for transfers between devices, partner(): lax.ppermute(array, 'leaf', [(i, i ^ 1 << level) for i in range(lax.axis_...  5.34 us
    unnamed x18, local copies, waits for them, and re-layouts  4.31 us
  transfers between devices with their start and end apart: 17, of which 4 were waited for; matrix products, arithmetic and copies ran while one was open for 0% of the time, Pallas kernels for 22%

profile of v1, /device:TPU:8, one launch (start us, length us, event | category | flops | bytes accessed | tf_op | source)
XLA Modules:
  0.0 74.3 jit_solution(3581343387274086705)
XLA Ops:
  0.7 1.2 %copy-done = f32[1,4,256,256]{3,2,1,0:T(8,128)S(1)} copy-done((f32[1,4,256,256]{3,2,1,0:T(8,128)S(1)}, f32[1,4,256,256]{3,2,1,0:T(8,128)}, u32[]{:S(2)}) %copy-start) | copy-done | bytes 1048600
  1.9 1.0 %copy-done.3 = f32[512,256]{1,0:T(8,128)S(1)} copy-done((f32[512,256]{1,0:T(8,128)S(1)}, f32[512,256]{1,0:T(8,128)}, u32[]{:S(2)}) %copy-start.3) | copy-done | bytes 524312
  2.9 0.9 %copy-done.5 = f32[512,128]{1,0:T(8,128)S(1)} copy-done((f32[512,128]{1,0:T(8,128)S(1)}, f32[512,128]{1,0:T(8,128)}, u32[]{:S(2)}) %copy-start.5) | copy-done | bytes 262168
  3.9 0.7 copy-done.7
  4.5 1.1 %leaf.1 = (f32[256,256]{1,0:T(8,128)S(1)}, bf16[544,128]{1,0:T(8,128)(2,1)S(1)}) custom-call(f32[512,256]{1,0:T(8,128)S(1)} %copy-done.3, f32[512,128]{1,0:T(8,128)S(1)} %copy-done.5, f32[1,4,256,256]{3,2,1,0:T(8,128)S(1)} %copy-done, s32[1,4]{1,0:T(1,128)S(1)} %copy-done.7, s32[1]{0:T(128)S(6)} %copy.8.count_ref), custom_call_target="tpu_custom_call" | custom-call | flops 100663296 | bytes 2236436 | tf_op jit(solution)/shard_map/leaf/pallas_call | solution.py:53
  5.6 0.6 collective-permute-start.7
  6.2 1.1 %collective-permute-done.7.got_ref.got0_ref = f32[256,256]{1,0:T(8,128)S(1)} collective-permute-done((f32[256,256]{1,0:T(8,128)S(1)}, f32[256,256]{1,0:T(8,128)S(1)}, u32[]{:S(2)}, u32[]{:S(2)}) %collective-permute-start.7) | collective-permute-done | bytes 262176 | tf_op jit(solution)/shard_map/ppermute | solution.py:179
  7.6 1.6 %collective-permute-start.8 = (bf16[256,256]{1,0:T(8,128)(2,1)S(1)}, bf16[256,256]{1,0:T(8,128)(2,1)S(1)}, u32[]{:S(2)}, u32[]{:S(2)}) collective-permute-start(bf16[256,256]{1,0:T(8,128)(2,1)S(1)} %get-tuple-element.39), channel_id=1, source_target_pairs={{0,2},{1,3},{2,0},{3,1},{4,6},{5,7},{6,4},{7,5},{8,10},{9,11},{10,... | collective-permute-start | bytes 393224 | tf_op jit(solution)/shard_map/ppermute | solution.py:179
  9.2 4.2 %collective-permute-done.8.got_ref.refs_0_ = bf16[256,256]{1,0:T(8,128)(2,1)S(1)} collective-permute-done((bf16[256,256]{1,0:T(8,128)(2,1)S(1)}, bf16[256,256]{1,0:T(8,128)(2,1)S(1)}, u32[]{:S(2)}, u32[]{:S(2)}) %collective-permute-start.8) | collective-permute-done | bytes 131104 | tf_op jit(solution)/shard_map/ppermute | solution.py:179
  13.7 1.6 %collective-permute-start.9 = (bf16[256,256]{1,0:T(8,128)(2,1)S(1)}, bf16[256,256]{1,0:T(8,128)(2,1)S(1)}, u32[]{:S(2)}, u32[]{:S(2)}) collective-permute-start(bf16[256,256]{1,0:T(8,128)(2,1)S(1)} %get-tuple-element.41), channel_id=1, source_target_pairs={{0,4},{1,5},{2,6},{3,7},{4,0},{5,1},{6,2},{7,3},{8,12},{9,13},{10,... | collective-permute-start | bytes 393224 | tf_op jit(solution)/shard_map/ppermute | solution.py:179
  15.3 3.2 %collective-permute-start.4 = (bf16[128,1024]{1,0:T(8,128)(2,1)S(1)}, bf16[128,1024]{1,0:T(8,128)(2,1)S(1)}, u32[]{:S(2)}, u32[]{:S(2)}) collective-permute-start(bf16[128,1024]{1,0:T(8,128)(2,1)S(1)} %get-tuple-element.51), channel_id=1, source_target_pairs={{2,0},{3,1},{4,2},{5,3},{6,4},{7,5},{8,6},{9,7},{10,8},{11,9},{12,... | collective-permute-start | bytes 786440 | tf_op jit(solution)/shard_map/ppermute | solution.py:175
  18.6 2.2 %collective-permute-start.3 = (bf16[128,1024]{1,0:T(8,128)(2,1)S(1)}, bf16[128,1024]{1,0:T(8,128)(2,1)S(1)}, u32[]{:S(2)}, u32[]{:S(2)}) collective-permute-start(bf16[128,1024]{1,0:T(8,128)(2,1)S(1)} %get-tuple-element.52), channel_id=1, source_target_pairs={{2,0},{3,1},{4,2},{5,3},{6,4},{7,5},{8,6},{9,7},{10,8},{11,9},{12,... | collective-permute-start | bytes 786440 | tf_op jit(solution)/shard_map/ppermute | solution.py:175
  20.8 4.6 %collective-permute-start.2 = (bf16[128,1024]{1,0:T(8,128)(2,1)S(1)}, bf16[128,1024]{1,0:T(8,128)(2,1)S(1)}, u32[]{:S(2)}, u32[]{:S(2)}) collective-permute-start(bf16[128,1024]{1,0:T(8,128)(2,1)S(1)} %get-tuple-element.53), channel_id=1, source_target_pairs={{2,0},{3,1},{4,2},{5,3},{6,4},{7,5},{8,6},{9,7},{10,8},{11,9},{12,... | collective-permute-start | bytes 786440 | tf_op jit(solution)/shard_map/ppermute | solution.py:175
  25.4 2.4 %collective-permute-start.6 = (bf16[544,128]{1,0:T(8,128)(2,1)S(1)}, bf16[544,128]{1,0:T(8,128)(2,1)S(1)}, u32[]{:S(2)}, u32[]{:S(2)}) collective-permute-start(bf16[544,128]{1,0:T(8,128)(2,1)S(1)} %get-tuple-element.28.x_ref), channel_id=1, source_target_pairs={{2,0},{3,1},{4,2},{5,3},{6,4},{7,5},{8,6},{9,7},{10,8},{11,9},{12,... | collective-permute-start | bytes 417800 | tf_op jit(solution)/shard_map/ppermute | solution.py:175
  27.9 1.9 %collective-permute-start.1 = (bf16[128,1024]{1,0:T(8,128)(2,1)S(1)}, bf16[128,1024]{1,0:T(8,128)(2,1)S(1)}, u32[]{:S(2)}, u32[]{:S(2)}) collective-permute-start(bf16[128,1024]{1,0:T(8,128)(2,1)S(1)} %get-tuple-element.54), channel_id=1, source_target_pairs={{2,0},{3,1},{4,2},{5,3},{6,4},{7,5},{8,6},{9,7},{10,8},{11,9},{12,... | collective-permute-start | bytes 786440 | tf_op jit(solution)/shard_map/ppermute | solution.py:175
  29.8 1.8 %self.1.near_ref = f32[512,128]{1,0:T(8,128)S(1)} custom-call(bf16[512,1024]{1,0:T(8,128)(2,1)S(1)} %copy-done.2, f32[512,128]{1,0:T(8,128)S(1)} %copy-done.6), custom_call_target="tpu_custom_call" | custom-call | flops 805306368 | bytes 1572864 | tf_op jit(solution)/shard_map/self/pallas_call | solution.py:53
  32.3 0.6 pair.1
  32.9 7.8 %collective-permute-done.6.xh_ref = bf16[544,128]{1,0:T(8,128)(2,1)S(1)} collective-permute-done((bf16[544,128]{1,0:T(8,128)(2,1)S(1)}, bf16[544,128]{1,0:T(8,128)(2,1)S(1)}, u32[]{:S(2)}, u32[]{:S(2)}) %collective-permute-start.6) | collective-permute-done | bytes 139296 | tf_op jit(solution)/shard_map/ppermute | solution.py:175
  40.6 0.4 collective-permute-start.10
  41.1 2.4 %chunk0.1 = (f32[512,128]{1,0:T(8,128)S(1)}, f32[512,128]{1,0:T(8,128)S(1)}, bf16[128,128]{1,0:T(8,128)(2,1)S(1)}) custom-call(bf16[512,1024]{1,0:T(8,128)(2,1)S(1)} %copy-done.2, bf16[512,1024]{1,0:T(8,128)(2,1)S(1)} %collective-permute-done.g_ref, bf16[128,1024]{1,0:T(8,128)(2,1)S(1)} %collective-permute-done.4.h_ref, ...), custom_call_target="tpu_custom_call" | custom-call | flops 402653184 | bytes 3858452 | tf_op jit(solution)/shard_map/chunk0/pallas_call | solution.py:53
  43.6 2.5 %chunk128.1 = (f32[512,128]{1,0:T(8,128)S(1)}, f32[512,128]{1,0:T(8,128)S(1)}, bf16[128,128]{1,0:T(8,128)(2,1)S(1)}) custom-call(bf16[512,1024]{1,0:T(8,128)(2,1)S(1)} %copy-done.2, bf16[512,1024]{1,0:T(8,128)(2,1)S(1)} %collective-permute-done.g_ref, bf16[128,1024]{1,0:T(8,128)(2,1)S(1)} %collective-permute-done.3.h_ref, ...), custom_call_target="tpu_custom_call" | custom-call | flops 402653184 | bytes 3858452 | tf_op jit(solution)/shard_map/chunk128/pallas_call | solution.py:53
  46.0 2.5 %chunk256.1 = (f32[512,128]{1,0:T(8,128)S(1)}, f32[512,128]{1,0:T(8,128)S(1)}, bf16[128,128]{1,0:T(8,128)(2,1)S(1)}) custom-call(bf16[512,1024]{1,0:T(8,128)(2,1)S(1)} %copy-done.2, bf16[512,1024]{1,0:T(8,128)(2,1)S(1)} %collective-permute-done.g_ref, bf16[128,1024]{1,0:T(8,128)(2,1)S(1)} %collective-permute-done.2.h_ref, ...), custom_call_target="tpu_custom_call" | custom-call | flops 402653184 | bytes 3858452 | tf_op jit(solution)/shard_map/chunk256/pallas_call | solution.py:53
  48.5 2.5 %chunk384.1 = (f32[512,128]{1,0:T(8,128)S(1)}, f32[512,128]{1,0:T(8,128)S(1)}, bf16[128,128]{1,0:T(8,128)(2,1)S(1)}) custom-call(bf16[512,1024]{1,0:T(8,128)(2,1)S(1)} %copy-done.2, bf16[512,1024]{1,0:T(8,128)(2,1)S(1)} %collective-permute-done.g_ref, bf16[128,1024]{1,0:T(8,128)(2,1)S(1)} %collective-permute-done.1.h_ref, ...), custom_call_target="tpu_custom_call" | custom-call | flops 402653184 | bytes 3858452 | tf_op jit(solution)/shard_map/chunk384/pallas_call | solution.py:53
  51.1 0.7 up4.1
  51.8 2.6 %collective-permute-start.11 = (bf16[128,256]{1,0:T(8,128)(2,1)S(1)}, bf16[128,256]{1,0:T(8,128)(2,1)S(1)}, u32[]{:S(2)}, u32[]{:S(2)}) collective-permute-start(bf16[128,256]{1,0:T(8,128)(2,1)S(1)} %get-tuple-element.45), channel_id=1, source_target_pairs={{0,16},{1,17},{2,18},{3,19},{4,20},{5,21},{6,22},{7,23},{8,24},{9,... | collective-permute-start | bytes 196616 | tf_op jit(solution)/shard_map/ppermute | solution.py:179
  54.3 4.3 %collective-permute-start.16 = (bf16[128,128]{1,0:T(8,128)(2,1)S(1)}, bf16[128,128]{1,0:T(8,128)(2,1)S(1)}, u32[]{:S(2)}, u32[]{:S(2)}) collective-permute-start(bf16[128,128]{1,0:T(8,128)(2,1)S(1)} %get-tuple-element.50), channel_id=1, source_target_pairs={{0,2},{1,3},{2,4},{3,5},{4,6},{5,7},{6,8},{7,9},{8,10},{9,11},{10,... | collective-permute-start | bytes 98312 | tf_op jit(solution)/shard_map/ppermute | solution.py:175
  58.6 1.9 %collective-permute-start.15 = (bf16[128,128]{1,0:T(8,128)(2,1)S(1)}, bf16[128,128]{1,0:T(8,128)(2,1)S(1)}, u32[]{:S(2)}, u32[]{:S(2)}) collective-permute-start(bf16[128,128]{1,0:T(8,128)(2,1)S(1)} %get-tuple-element.49), channel_id=1, source_target_pairs={{0,2},{1,3},{2,4},{3,5},{4,6},{5,7},{6,8},{7,9},{8,10},{9,11},{10,... | collective-permute-start | bytes 98312 | tf_op jit(solution)/shard_map/ppermute | solution.py:175
  60.6 4.8 %collective-permute-start.14 = (bf16[128,128]{1,0:T(8,128)(2,1)S(1)}, bf16[128,128]{1,0:T(8,128)(2,1)S(1)}, u32[]{:S(2)}, u32[]{:S(2)}) collective-permute-start(bf16[128,128]{1,0:T(8,128)(2,1)S(1)} %get-tuple-element.48), channel_id=1, source_target_pairs={{0,2},{1,3},{2,4},{3,5},{4,6},{5,7},{6,8},{7,9},{8,10},{9,11},{10,... | collective-permute-start | bytes 98312 | tf_op jit(solution)/shard_map/ppermute | solution.py:175
  65.4 1.9 %collective-permute-start.13 = (bf16[128,128]{1,0:T(8,128)(2,1)S(1)}, bf16[128,128]{1,0:T(8,128)(2,1)S(1)}, u32[]{:S(2)}, u32[]{:S(2)}) collective-permute-start(bf16[128,128]{1,0:T(8,128)(2,1)S(1)} %get-tuple-element.47), channel_id=1, source_target_pairs={{0,2},{1,3},{2,4},{3,5},{4,6},{5,7},{6,8},{7,9},{8,10},{9,11},{10,... | collective-permute-start | bytes 98312 | tf_op jit(solution)/shard_map/ppermute | solution.py:175
  67.3 1.8 %down.1.far_ref = f32[512,128]{1,0:T(8,128)S(1)} custom-call(f32[256,256]{1,0:T(8,128)S(1)} %collective-permute-done.7.got_ref.got0_ref, bf16[256,256]{1,0:T(8,128)(2,1)S(1)} %collective-permute-done.8.got_ref.refs_0_, bf16[256,256]{1,0:T(8,128)(2,1)S(1)} %collective-permute-done.9.got_ref.refs_1_, ...), custom_call_target="tpu_custom_call" | custom-call | flops 553648128 | bytes 3866624 | tf_op jit(solution)/shard_map/down/pallas_call | solution.py:53
  69.1 3.9 %collective-permute-done.13.refs_0_ = bf16[128,128]{1,0:T(8,128)(2,1)S(1)} collective-permute-done((bf16[128,128]{1,0:T(8,128)(2,1)S(1)}, bf16[128,128]{1,0:T(8,128)(2,1)S(1)}, u32[]{:S(2)}, u32[]{:S(2)}) %collective-permute-start.13) | collective-permute-done | bytes 32800 | tf_op jit(solution)/shard_map/ppermute | solution.py:175
  73.0 1.3 %final.1 = f32[512,128]{1,0:T(8,128)} custom-call(f32[512,128]{1,0:T(8,128)S(1)} %get-tuple-element.37.near_ref, f32[512,128]{1,0:T(8,128)S(1)} %down.1.far_ref, bf16[512,128]{1,0:T(8,128)(2,1)S(1)} %collective-permute-done.12.sib_ref, s32[1,4]{1,0:T(1,128)S(1)} %copy-done.8, s32[1]{0:T(128)S(6)} %copy.8.count_ref, ...), custom_call_target="tpu_custom_call" | custom-call | flops 393216 | bytes 1048596 | tf_op jit(solution)/shard_map/final/pallas_call | solution.py:53
  (36 shorter events, 1.4 us)
Async XLA Ops:
  0.0 27.9 %collective-permute-start = (bf16[512,1024]{1,0:T(8,128)(2,1)}, bf16[512,1024]{1,0:T(8,128)(2,1)S(1)}, u32[]{:S(2)}, u32[]{:S(2)}) collective-permute-start(bf16[512,1024]{1,0:T(8,128)(2,1)} %f_ref.11), channel_id=1, source_target_pairs={{0,1},{1,0},{2,3},{3,2},{4,5},{5,4},{6,7},{7,6},{8,9},{9,8},{10,11... | collective-permute-start | bytes 3145736 | tf_op jit(solution)/shard_map/ppermute | solution.py:179
  0.7 1.2 %copy-start = (f32[1,4,256,256]{3,2,1,0:T(8,128)S(1)}, f32[1,4,256,256]{3,2,1,0:T(8,128)}, u32[]{:S(2)}) copy-start(f32[1,4,256,256]{3,2,1,0:T(8,128)} %refs_5_.1) | copy-start | bytes 3145732
  1.9 1.0 %copy-start.3 = (f32[512,256]{1,0:T(8,128)S(1)}, f32[512,256]{1,0:T(8,128)}, u32[]{:S(2)}) copy-start(f32[512,256]{1,0:T(8,128)} %refs_6_.1) | copy-start | bytes 1572868
  2.9 0.9 %copy-start.5 = (f32[512,128]{1,0:T(8,128)S(1)}, f32[512,128]{1,0:T(8,128)}, u32[]{:S(2)}) copy-start(f32[512,128]{1,0:T(8,128)} %x_ref.3) | copy-start | bytes 786436
  3.9 0.7 copy-start.7
  4.5 2.8 %copy-start.1 = (f32[1,4,256,256]{3,2,1,0:T(8,128)S(1)}, f32[1,4,256,256]{3,2,1,0:T(8,128)}, u32[]{:S(2)}) copy-start(f32[1,4,256,256]{3,2,1,0:T(8,128)} %refs_5_.1) | copy-start | bytes 3145732
  5.6 1.7 %collective-permute-start.7 = (f32[256,256]{1,0:T(8,128)S(1)}, f32[256,256]{1,0:T(8,128)S(1)}, u32[]{:S(2)}, u32[]{:S(2)}) collective-permute-start(f32[256,256]{1,0:T(8,128)S(1)} %get-tuple-element.38), channel_id=1, source_target_pairs={{0,1},{1,0},{2,3},{3,2},{4,5},{5,4},{6,7},{7,6},{8,9},{9,8},{10,11... | collective-permute-start | bytes 786440 | tf_op jit(solution)/shard_map/ppermute | solution.py:179
  6.2 9.0 %copy-start.2 = (bf16[512,1024]{1,0:T(8,128)(2,1)S(1)}, bf16[512,1024]{1,0:T(8,128)(2,1)}, u32[]{:S(2)}) copy-start(bf16[512,1024]{1,0:T(8,128)(2,1)} %f_ref.11) | copy-start | bytes 3145732
  7.6 5.8 %collective-permute-start.8 = (bf16[256,256]{1,0:T(8,128)(2,1)S(1)}, bf16[256,256]{1,0:T(8,128)(2,1)S(1)}, u32[]{:S(2)}, u32[]{:S(2)}) collective-permute-start(bf16[256,256]{1,0:T(8,128)(2,1)S(1)} %get-tuple-element.39), channel_id=1, source_target_pairs={{0,2},{1,3},{2,0},{3,1},{4,6},{5,7},{6,4},{7,5},{8,10},{9,11},{10,... | collective-permute-start | bytes 393224 | tf_op jit(solution)/shard_map/ppermute | solution.py:179
  9.1 11.7 %collective-permute-start.5 = (bf16[544,128]{1,0:T(8,128)(2,1)S(1)}, bf16[544,128]{1,0:T(8,128)(2,1)S(1)}, u32[]{:S(2)}, u32[]{:S(2)}) collective-permute-start(bf16[544,128]{1,0:T(8,128)(2,1)S(1)} %get-tuple-element.28.x_ref), channel_id=1, source_target_pairs={{0,1},{1,0},{2,3},{3,2},{4,5},{5,4},{6,7},{7,6},{8,9},{9,8},{10,11... | collective-permute-start | bytes 417800 | tf_op jit(solution)/shard_map/ppermute | solution.py:179
  13.7 16.2 %copy-start.6 = (f32[512,128]{1,0:T(8,128)S(1)}, f32[512,128]{1,0:T(8,128)}, u32[]{:S(2)}) copy-start(f32[512,128]{1,0:T(8,128)} %x_ref.3) | copy-start | bytes 786436
  13.7 11.7 %collective-permute-start.9 = (bf16[256,256]{1,0:T(8,128)(2,1)S(1)}, bf16[256,256]{1,0:T(8,128)(2,1)S(1)}, u32[]{:S(2)}, u32[]{:S(2)}) collective-permute-start(bf16[256,256]{1,0:T(8,128)(2,1)S(1)} %get-tuple-element.41), channel_id=1, source_target_pairs={{0,4},{1,5},{2,6},{3,7},{4,0},{5,1},{6,2},{7,3},{8,12},{9,13},{10,... | collective-permute-start | bytes 393224 | tf_op jit(solution)/shard_map/ppermute | solution.py:179
  15.3 25.7 %collective-permute-start.4 = (bf16[128,1024]{1,0:T(8,128)(2,1)S(1)}, bf16[128,1024]{1,0:T(8,128)(2,1)S(1)}, u32[]{:S(2)}, u32[]{:S(2)}) collective-permute-start(bf16[128,1024]{1,0:T(8,128)(2,1)S(1)} %get-tuple-element.51), channel_id=1, source_target_pairs={{2,0},{3,1},{4,2},{5,3},{6,4},{7,5},{8,6},{9,7},{10,8},{11,9},{12,... | collective-permute-start | bytes 786440 | tf_op jit(solution)/shard_map/ppermute | solution.py:175
  18.6 25.0 %collective-permute-start.3 = (bf16[128,1024]{1,0:T(8,128)(2,1)S(1)}, bf16[128,1024]{1,0:T(8,128)(2,1)S(1)}, u32[]{:S(2)}, u32[]{:S(2)}) collective-permute-start(bf16[128,1024]{1,0:T(8,128)(2,1)S(1)} %get-tuple-element.52), channel_id=1, source_target_pairs={{2,0},{3,1},{4,2},{5,3},{6,4},{7,5},{8,6},{9,7},{10,8},{11,9},{12,... | collective-permute-start | bytes 786440 | tf_op jit(solution)/shard_map/ppermute | solution.py:175
  20.8 25.2 %collective-permute-start.2 = (bf16[128,1024]{1,0:T(8,128)(2,1)S(1)}, bf16[128,1024]{1,0:T(8,128)(2,1)S(1)}, u32[]{:S(2)}, u32[]{:S(2)}) collective-permute-start(bf16[128,1024]{1,0:T(8,128)(2,1)S(1)} %get-tuple-element.53), channel_id=1, source_target_pairs={{2,0},{3,1},{4,2},{5,3},{6,4},{7,5},{8,6},{9,7},{10,8},{11,9},{12,... | collective-permute-start | bytes 786440 | tf_op jit(solution)/shard_map/ppermute | solution.py:175
  25.4 15.2 %collective-permute-start.6 = (bf16[544,128]{1,0:T(8,128)(2,1)S(1)}, bf16[544,128]{1,0:T(8,128)(2,1)S(1)}, u32[]{:S(2)}, u32[]{:S(2)}) collective-permute-start(bf16[544,128]{1,0:T(8,128)(2,1)S(1)} %get-tuple-element.28.x_ref), channel_id=1, source_target_pairs={{2,0},{3,1},{4,2},{5,3},{6,4},{7,5},{8,6},{9,7},{10,8},{11,9},{12,... | collective-permute-start | bytes 417800 | tf_op jit(solution)/shard_map/ppermute | solution.py:175
  27.9 20.6 %collective-permute-start.1 = (bf16[128,1024]{1,0:T(8,128)(2,1)S(1)}, bf16[128,1024]{1,0:T(8,128)(2,1)S(1)}, u32[]{:S(2)}, u32[]{:S(2)}) collective-permute-start(bf16[128,1024]{1,0:T(8,128)(2,1)S(1)} %get-tuple-element.54), channel_id=1, source_target_pairs={{2,0},{3,1},{4,2},{5,3},{6,4},{7,5},{8,6},{9,7},{10,8},{11,9},{12,... | collective-permute-start | bytes 786440 | tf_op jit(solution)/shard_map/ppermute | solution.py:175
  31.6 0.7 copy-start.8
  40.6 10.4 %collective-permute-start.10 = (bf16[256,256]{1,0:T(8,128)(2,1)S(1)}, bf16[256,256]{1,0:T(8,128)(2,1)S(1)}, u32[]{:S(2)}, u32[]{:S(2)}) collective-permute-start(bf16[256,256]{1,0:T(8,128)(2,1)S(1)} %get-tuple-element.43), channel_id=1, source_target_pairs={{0,8},{1,9},{2,10},{3,11},{4,12},{5,13},{6,14},{7,15},{8,0},{9,1},... | collective-permute-start | bytes 393224 | tf_op jit(solution)/shard_map/ppermute | solution.py:179
  51.0 16.3 %copy-start.4 = (f32[1,5,256,256]{3,2,1,0:T(8,128)S(1)}, f32[1,5,256,256]{3,2,1,0:T(8,128)}, u32[]{:S(2)}) copy-start(f32[1,5,256,256]{3,2,1,0:T(8,128)} %refs_4_.1) | copy-start | bytes 3932164
  51.0 22.0 %collective-permute-start.12 = (bf16[512,128]{1,0:T(8,128)(2,1)S(1)}, bf16[512,128]{1,0:T(8,128)(2,1)S(1)}, u32[]{:S(2)}, u32[]{:S(2)}) collective-permute-start(bf16[512,128]{1,0:T(8,128)(2,1)S(1)} %convert_element_type.3), channel_id=1, source_target_pairs={{0,1},{1,0},{2,3},{3,2},{4,5},{5,4},{6,7},{7,6},{8,9},{9,8},{10,11... | collective-permute-start | bytes 393224 | tf_op jit(solution)/shard_map/ppermute | solution.py:179
  51.8 13.6 %collective-permute-start.11 = (bf16[128,256]{1,0:T(8,128)(2,1)S(1)}, bf16[128,256]{1,0:T(8,128)(2,1)S(1)}, u32[]{:S(2)}, u32[]{:S(2)}) collective-permute-start(bf16[128,256]{1,0:T(8,128)(2,1)S(1)} %get-tuple-element.45), channel_id=1, source_target_pairs={{0,16},{1,17},{2,18},{3,19},{4,20},{5,21},{6,22},{7,23},{8,24},{9,... | collective-permute-start | bytes 196616 | tf_op jit(solution)/shard_map/ppermute | solution.py:179
  54.3 14.7 %collective-permute-start.16 = (bf16[128,128]{1,0:T(8,128)(2,1)S(1)}, bf16[128,128]{1,0:T(8,128)(2,1)S(1)}, u32[]{:S(2)}, u32[]{:S(2)}) collective-permute-start(bf16[128,128]{1,0:T(8,128)(2,1)S(1)} %get-tuple-element.50), channel_id=1, source_target_pairs={{0,2},{1,3},{2,4},{3,5},{4,6},{5,7},{6,8},{7,9},{8,10},{9,11},{10,... | collective-permute-start | bytes 98312 | tf_op jit(solution)/shard_map/ppermute | solution.py:175
  58.6 10.4 %collective-permute-start.15 = (bf16[128,128]{1,0:T(8,128)(2,1)S(1)}, bf16[128,128]{1,0:T(8,128)(2,1)S(1)}, u32[]{:S(2)}, u32[]{:S(2)}) collective-permute-start(bf16[128,128]{1,0:T(8,128)(2,1)S(1)} %get-tuple-element.49), channel_id=1, source_target_pairs={{0,2},{1,3},{2,4},{3,5},{4,6},{5,7},{6,8},{7,9},{8,10},{9,11},{10,... | collective-permute-start | bytes 98312 | tf_op jit(solution)/shard_map/ppermute | solution.py:175
  60.6 8.5 %collective-permute-start.14 = (bf16[128,128]{1,0:T(8,128)(2,1)S(1)}, bf16[128,128]{1,0:T(8,128)(2,1)S(1)}, u32[]{:S(2)}, u32[]{:S(2)}) collective-permute-start(bf16[128,128]{1,0:T(8,128)(2,1)S(1)} %get-tuple-element.48), channel_id=1, source_target_pairs={{0,2},{1,3},{2,4},{3,5},{4,6},{5,7},{6,8},{7,9},{8,10},{9,11},{10,... | collective-permute-start | bytes 98312 | tf_op jit(solution)/shard_map/ppermute | solution.py:175
  65.4 7.6 %collective-permute-start.13 = (bf16[128,128]{1,0:T(8,128)(2,1)S(1)}, bf16[128,128]{1,0:T(8,128)(2,1)S(1)}, u32[]{:S(2)}, u32[]{:S(2)}) collective-permute-start(bf16[128,128]{1,0:T(8,128)(2,1)S(1)} %get-tuple-element.47), channel_id=1, source_target_pairs={{0,2},{1,3},{2,4},{3,5},{4,6},{5,7},{6,8},{7,9},{8,10},{9,11},{10,... | collective-permute-start | bytes 98312 | tf_op jit(solution)/shard_map/ppermute | solution.py:175

commit v2 on v1

v2 whole, which is shorter than its diff:
```python
import functools

import jax
import jax.numpy as jnp
from jax import lax
from jax.experimental import pallas as pl
from jax.experimental.pallas import tpu as pltpu
from jax.sharding import PartitionSpec as P

BF16 = jnp.bfloat16
F32 = jnp.float32
VMEM = pl.BlockSpec(memory_space=pltpu.VMEM)
SMEM = pl.BlockSpec(memory_space=pltpu.SMEM)
HBM = pl.BlockSpec(memory_space=pltpu.HBM)
ANY = pl.BlockSpec(memory_space=pl.ANY)
NN = (((1,), (0,)), ((), ()))
NT = (((1,), (1,)), ((), ()))
TN = (((0,), (0,)), ((), ()))
FLAG_ROWS = 16
LIMIT = 16 << 20
LOAD_LIMIT = 54800000


def dot(a, b, dims):
    return lax.dot_general(a, b, dims, preferred_element_type=F32)


def halves(a):
    high = a.astype(BF16)
    return high, (a - high.astype(F32)).astype(BF16)


def dot_wide(a, b, dims):
    a_high, a_low = halves(a)
    b_high, b_low = halves(b)
    return dot(a_high, b_high, dims) + (dot(a_high, b_low, dims) + dot(a_low, b_high, dims))


def dot_half(a16, b, dims):
    b_high, b_low = halves(b)
    return dot(a16, b_high, dims) + dot(a16, b_low, dims)


def member(list_ref, count_ref, offset):
    index = lax.axis_index("leaf")
    found = jnp.float32(0.0)
    for slot in range(list_ref.shape[1]):
        hit = (list_ref[0, slot] == index + offset) & (slot < count_ref[0])
        found = jnp.where(hit, jnp.float32(1.0), found)
    return found


def call(kernel, outs, specs, flops, *args, scratch=(), limit=LIMIT):
    out_bytes = sum(o.size * o.dtype.itemsize for o in outs)
    in_bytes = sum(a.size * a.dtype.itemsize for a in args)
    return pl.pallas_call(
        kernel,
        out_shape=outs,
        in_specs=specs,
        out_specs=[VMEM] * len(outs),
        scratch_shapes=list(scratch),
        compiler_params=pltpu.CompilerParams(vmem_limit_bytes=limit),
        cost_estimate=pl.CostEstimate(flops=flops, bytes_accessed=in_bytes + out_bytes, transcendentals=0),
    )(*args)


def load_kernel(f_hbm, x_hbm, bases_hbm, transfers_hbm, far_ref, x_ref, bases_ref, transfer_ref, sems):
    size = far_ref.shape[0]
    width = f_hbm.shape[1]
    copies = [
        pltpu.make_async_copy(x_hbm, x_ref, sems.at[0]),
        pltpu.make_async_copy(f_hbm.at[:size], far_ref.at[:, :width], sems.at[1]),
        pltpu.make_async_copy(bases_hbm, bases_ref, sems.at[2]),
        pltpu.make_async_copy(transfers_hbm.at[0, 0], transfer_ref, sems.at[3]),
    ]
    for copy in copies:
        copy.start()
    copies[0].wait()
    far_ref[:, width:] = x_ref[:size].astype(BF16)
    for copy in copies[1:]:
        copy.wait()


def leaf_kernel(c1, bases_ref, x_ref, transfer_ref, message_ref):
    x = x_ref[...]
    rows, probes = x.shape
    skeleton = dot_wide(x, bases_ref[...], TN)
    message_ref[:probes] = skeleton
    message_ref[probes : 2 * probes] = c1 * dot_wide(skeleton, transfer_ref[...], NN)
    message_ref[2 * probes :, :probes] = x[: rows // 2]
    message_ref[2 * probes :, probes:] = x[rows // 2 :]


def pack_kernel(sizes, first, f_ref, x_ref, after_ref, list_ref, count_ref, *far_refs):
    width = f_ref.shape[1]
    probes = x_ref.shape[1]
    for size, far_ref in zip(sizes, far_refs):
        far_ref[:size, :width] = f_ref[first : first + size]
        far_ref[:size, width:] = x_ref[first : first + size].astype(BF16)
        first += size
    flags = [jnp.full((FLAG_ROWS, probes), member(list_ref, count_ref, offset), F32) for offset in (-2, -1)]
    flags.append(jnp.zeros((FLAG_ROWS, width - probes), F32))
    far_refs[0][sizes[0] :] = jnp.concatenate(flags, axis=1).astype(BF16)


def up_kernel(level, factor, own_ref, got_ref, transfer_ref, message_ref, next_ref):
    probes = next_ref.shape[0]
    own = own_ref[probes : 2 * probes] if own_ref.shape[0] > probes else own_ref[...]
    skeleton = own + got_ref[probes : 2 * probes].astype(F32)
    message_ref[:probes] = skeleton.astype(message_ref.dtype)
    if factor is not None:
        moved = factor * dot_wide(skeleton, transfer_ref[0, level], NN)
        message_ref[probes:] = moved.astype(message_ref.dtype)
        next_ref[...] = moved
    else:
        next_ref[...] = skeleton


def down_kernel(scale_g, factors, got0_ref, *refs):
    depth = len(factors)
    gots = [got0_ref, *refs[:depth]]
    coupling_ref, transfer_ref, bases_ref, out_ref = refs[depth:]
    probes = out_ref.shape[1]
    expansion = None
    for level in range(depth, -1, -1):
        got = gots[level][:probes]
        wide = dot_wide if got.dtype == F32 else dot_half
        update = scale_g * wide(got, coupling_ref[0, level], NT)
        if level < depth:
            update = update + factors[level] * dot_wide(expansion, transfer_ref[0, level], NT)
        expansion = update
    out_ref[...] = dot_wide(bases_ref[...], expansion, NT)


def tile(rows_a, rows_b, scale):
    gram = dot(rows_a, rows_b, NT)
    return halves(gram * gram * scale)


def self_kernel(scale, f_ref, x_ref, out_ref):
    high, low = tile(f_ref[...], f_ref[...], scale)
    x_high, x_low = halves(x_ref[...])
    out_ref[...] = dot(high, x_high, NN) + (dot(high, x_low, NN) + dot(low, x_high, NN))


def times(parts, x16):
    return dot(parts[0], x16, NN) + dot(parts[1], x16, NN)


def times_back(parts, xt16):
    return (dot(xt16, parts[0], NN) + dot(xt16, parts[1], NN)).T


def pair_kernel(scale, f_ref, g_ref, near_ref, x_ref, got_ref, list_ref, count_ref, out_ref, sib_ref, xt_ref, xst_ref):
    odd = lax.rem(lax.axis_index("leaf"), 2) == 1
    rows, probes = near_ref.shape
    xt_ref[...] = x_ref[...].T.astype(BF16)
    for half in range(2):
        part = got_ref[2 * probes :, half * probes : (half + 1) * probes]
        xst_ref[:, half * (rows // 2) : (half + 1) * (rows // 2)] = part.T.astype(BF16)

    @pl.when(odd)
    def _():
        parts = tile(g_ref[...], f_ref[...], scale)
        sib_ref[...] = times(parts, x_ref[...].astype(BF16))
        flag = member(list_ref, count_ref, -1)
        out_ref[...] = near_ref[...] + flag * times_back(parts, xst_ref[...])

    @pl.when(jnp.logical_not(odd))
    def _():
        out_ref[...] = near_ref[...]
        sib_ref[...] = jnp.zeros_like(sib_ref)


def chunk_kernel(scale, size, head, stage, f_ref, g_ref, h_ref, near_ref, sib_in_ref, xt_ref, xst_ref, list_ref, count_ref, *refs):
    even = lax.rem(lax.axis_index("leaf"), 2) == 0
    width = f_ref.shape[1]
    probes = near_ref.shape[1]
    h = h_ref[:size, :width]
    xh = h_ref[:size, width:]
    extra = 0
    if stage:
        flags_ref = refs[0]
        extra = 1
        at = flags_ref.shape[0] - FLAG_ROWS
        flag2 = flags_ref[at : at + 1, :probes].astype(F32)
        flag1 = flags_ref[at : at + 1, probes : 2 * probes].astype(F32)
    if stage == 1:
        far_head, near_head = refs[1:3]
        extra = 3
    out_ref, sib_ref, *back_refs = refs[extra:]
    parts = tile(f_ref[...], h, scale)
    out_ref[...] = near_ref[...] + member(list_ref, count_ref, 2) * times(parts, xh)
    back = times_back(parts, xt_ref[...])
    if stage == 0:
        back_refs[0][...] = back
    else:
        back = flag2 * back
    if stage == 1:
        back_refs[0][:head] = (flag2 * far_head[...] + flag1 * near_head[...]).astype(BF16)

    @pl.when(even)
    def _():
        cross = tile(g_ref[...], h, scale)
        sib_ref[...] = (sib_in_ref[...] + times(cross, xh)).astype(sib_ref.dtype)
        cross_back = times_back(cross, xst_ref[...])
        if stage == 0:
            back_refs[1][...] = cross_back
        else:
            back_refs[0][head:] = (back + flag1 * cross_back).astype(BF16)

    @pl.when(jnp.logical_not(even))
    def _():
        sib_ref[...] = sib_in_ref[...].astype(sib_ref.dtype)
        if stage == 0:
            back_refs[1][...] = jnp.zeros_like(back_refs[1])
        else:
            back_refs[0][head:] = back.astype(BF16)


def final_kernel(near_ref, far_ref, sib_ref, list_ref, count_ref, *refs):
    out_ref = refs[-1]
    flag = member(list_ref, count_ref, 1)
    at = 0
    for back_ref in refs[:-1]:
        rows = slice(at, at + back_ref.shape[0])
        out_ref[rows] = near_ref[rows] + far_ref[rows] + flag * sib_ref[rows].astype(F32) + back_ref[...].astype(F32)
        at += back_ref.shape[0]


def moved(array, by):
    peers = lax.axis_size("leaf")
    return lax.ppermute(array, "leaf", [(i, i + by) for i in range(peers) if 0 <= i + by < peers])


def partner(array, level):
    return lax.ppermute(array, "leaf", [(i, i ^ 1 << level) for i in range(lax.axis_size("leaf"))])


def body(features, probes, bases, transfers, couplings, near_list, near_count):
    rows, width = features.shape
    count = probes.shape[1]
    rank = bases.shape[1]
    depth = transfers.shape[1]
    scale = 1.0 / (rows * width)
    scale_g = (3.0 / rank) ** 0.5
    factors = [scale_g * 2.0 ** (-0.5 * (level + 1)) for level in range(depth)]
    shape = jax.ShapeDtypeStruct
    sizes = [rows // 4, rows // 2, rows // 4]

    sib_features = partner(features, 0)
    far0_out, x, bases_v, transfer0 = call(
        load_kernel,
        [
            shape((sizes[0], width + count), BF16),
            shape((rows, count), F32),
            shape((rows, rank), F32),
            shape((rank, rank), F32),
        ],
        [HBM] * 4,
        1000,
        features, probes, bases, transfers,
        scratch=[pltpu.SemaphoreType.DMA((4,))],
        limit=LOAD_LIMIT,
    )
    far = [moved(far0_out, -2)]
    (message,) = call(
        functools.partial(leaf_kernel, factors[0]),
        [shape((2 * count + rows // 2, rank), F32)],
        [VMEM] * 3,
        6 * rows * rank * count,
        bases_v, x, transfer0,
    )
    gots = [partner(message, 0)]
    own = message
    for level in range(1, depth + 1):
        last = level == depth
        outs = [shape((count if last else 2 * count, rank), BF16), shape((count, rank), F32)]
        message, own = call(
            functools.partial(up_kernel, level, None if last else factors[level]),
            outs,
            [VMEM] * 3,
            6 * rank * rank * count,
            own, gots[-1], transfers,
        )
        gots.append(partner(message, level))
        if level == 1:
            packed = call(
                functools.partial(pack_kernel, sizes[1:], sizes[0]),
                [shape((size + (0 if i else FLAG_ROWS), width + count), BF16) for i, size in enumerate(sizes[1:])],
                [VMEM, VMEM, ANY, SMEM, SMEM],
                1000,
                features, x, message, near_list, near_count,
            )
            far += [moved(part, -2) for part in packed]

    tile_flops = 2 * rows * rows * (width + 4 * count)
    (near,) = call(
        functools.partial(self_kernel, scale),
        [shape((rows, count), F32)],
        [VMEM, VMEM],
        tile_flops,
        features, x,
    )
    near, sib, xt, xst = call(
        functools.partial(pair_kernel, scale),
        [shape((rows, count), F32)] * 2 + [shape((count, rows), BF16)] * 2,
        [VMEM] * 5 + [SMEM] * 2,
        tile_flops,
        features, sib_features, near, x, gots[0], near_list, near_count,
    )
    backs = []
    heads = []
    for stage, (size, part) in enumerate(zip(sizes, far)):
        head = sizes[0] if stage == 1 else 0
        more = [[], [far[1], *heads], [far[1]]][stage]
        back_shapes = [shape((size, count), F32)] * 2 if stage == 0 else [shape((head + size, count), BF16)]
        near, sib, *heads = call(
            functools.partial(chunk_kernel, scale, size, head, stage),
            [shape((rows, count), F32), shape((rows, count), BF16 if stage == 2 else F32), *back_shapes],
            [VMEM] * 7 + [SMEM] * 2 + [VMEM] * len(more),
            tile_flops * 2 * size // rows,
            features, sib_features, part, near, sib, xt, xst, near_list, near_count, *more,
        )
        if stage:
            backs.append(moved(heads[0], 2))
    sib_got = partner(sib, 0)
    (far_sum,) = call(
        functools.partial(down_kernel, scale_g, factors),
        [shape((rows, count), F32)],
        [VMEM] * (depth + 4),
        6 * count * rank * (rank * (2 * depth + 1) + rows),
        *gots, couplings, transfers, bases_v,
    )
    (out,) = call(
        final_kernel,
        [shape((rows, count), F32)],
        [VMEM] * 3 + [SMEM] * 2 + [VMEM] * len(backs),
        6 * rows * count,
        near, far_sum, sib_got, near_list, near_count, *backs,
    )
    return out


def solution(mesh):
    in_specs = (
        P("leaf", None),
        P("leaf", None),
        P("leaf", None),
        P("leaf", None, None, None),
        P("leaf", None, None, None),
        P("leaf", None),
        P("leaf"),
    )
    out_specs = P("leaf", None)
    return jax.shard_map(body, mesh=mesh, in_specs=in_specs, out_specs=out_specs, check_vma=False)
```

time: 74.7 us -> 68 us (0.910)
  starting transfers between devices: 34.2 us -> 24.8 us
  waiting for transfers between devices: 17 us -> 24 us
  local copies, waits for them, and re-layouts: 4.41 us -> 0.98 us
    ppermute x8 -> x7, waiting for transfers between devices: 5.34 us -> 20.1 us  [partner(): lax.ppermute(array, 'leaf', [(i, i ^ 1 << level) for i in range(lax.axis_...]
    ppermute x9 -> x5, waiting for transfers between devices: 11.7 us -> 3.88 us  [moved(): lax.ppermute(array, 'leaf', [(i, i + by) for i in range(peers) if 0 <= i...]
    ppermute x9 -> x5, starting transfers between devices: 27.3 us -> 20.1 us  [moved(): lax.ppermute(array, 'leaf', [(i, i + by) for i in range(peers) if 0 <= i...]
    unnamed x18 -> x10, local copies, waits for them, and re-layouts: 4.31 us -> 0.98 us
    ppermute x8 -> x7, starting transfers between devices: 6.91 us -> 4.71 us  [partner(): lax.ppermute(array, 'leaf', [(i, i ^ 1 << level) for i in range(lax.axis_...]
    pallas_call x13 -> x14, Pallas kernels: 17.7 us -> 17 us  [call(): pl.pallas_call(kernel, out_shape=outs, in_specs=specs, out_specs=[VMEM] *...]
  transfers between devices with their start and end apart: 17 -> 12, of which waited for: 4 -> 3; matrix products, arithmetic and copies ran while one was open for 0% -> 0% of each run, Pallas kernels for 22% -> 23%
where the time goes in v2:
time: 68 us; the launch traced here: 67.7 us
  starting transfers between devices  24.8 us (36%)
  waiting for transfers between devices  24 us (35%)
  Pallas kernels  17 us (25%)
  local copies, waits for them, and re-layouts  0.98 us (1%)
  between operations  0.93 us (1%)
    ppermute x5, starting transfers between devices, moved(): lax.ppermute(array, 'leaf', [(i, i + by) for i in range(peers) if 0 <= i...  20.1 us
    ppermute x7, waiting for transfers between devices, partner(): lax.ppermute(array, 'leaf', [(i, i ^ 1 << level) for i in range(lax.axis_...  20.1 us
    pallas_call x14, Pallas kernels, call(): pl.pallas_call(kernel, out_shape=outs, in_specs=specs, out_specs=[VMEM] *...  17 us
    ppermute x7, starting transfers between devices, partner(): lax.ppermute(array, 'leaf', [(i, i ^ 1 << level) for i in range(lax.axis_...  4.71 us
    ppermute x5, waiting for transfers between devices, moved(): lax.ppermute(array, 'leaf', [(i, i + by) for i in range(peers) if 0 <= i...  3.88 us
  transfers between devices with their start and end apart: 12, of which 3 were waited for; matrix products, arithmetic and copies ran while one was open for 0% of the time, Pallas kernels for 23%

profile of v2, /device:TPU:8, one launch (start us, length us, event | category | flops | bytes accessed | tf_op | source)
XLA Modules:
  0.0 67.7 jit_solution(9752956654407738697)
XLA Ops:
  0.0 0.9 %copy-done.3 = f32[512,128]{1,0:T(8,128)S(1)} copy-done((f32[512,128]{1,0:T(8,128)S(1)}, f32[512,128]{1,0:T(8,128)}, u32[]{:S(2)}) %copy-start.3) | copy-done | bytes 262168
  1.0 1.2 %shard_map.73 = (bf16[128,1152]{1,0:T(8,128)(2,1)S(1)}, f32[512,128]{1,0:T(8,128)S(1)}, f32[512,256]{1,0:T(8,128)S(1)}, f32[256,256]{1,0:T(8,128)S(1)}) custom-call(bf16[512,1024]{1,0:T(8,128)(2,1)} %f_ref.11, f32[512,128]{1,0:T(8,128)S(1)} %copy-done.3, f32[512,256]{1,0:T(8,128)} %bases_hbm.1, f32[1,4,256,256]{3,2,1,0:T(8,128)} %refs_5_.1), custom_call_target="tpu_custom_call" | custom-call | flops 1000 | bytes 4227072 | tf_op jit(solution)/shard_map/pallas_call | solution.py:56
  2.2 0.0 copy-start.1
  2.2 0.5 shard_map.74.own_ref
  2.8 0.0 copy-start
  2.8 0.0 copy-start.4
  2.8 0.6 collective-permute-start.1
  4.0 0.9 %collective-permute-done.1.got_ref.got0_ref = f32[512,256]{1,0:T(8,128)S(1)} collective-permute-done((f32[512,256]{1,0:T(8,128)S(1)}, f32[512,256]{1,0:T(8,128)S(1)}, u32[]{:S(2)}, u32[]{:S(2)}) %collective-permute-start.1) | collective-permute-done | bytes 524320 | tf_op jit(solution)/shard_map/ppermute | solution.py:237
  4.9 0.2 shard_map.75
  5.2 0.6 shard_map.76
  5.8 4.2 %collective-permute-start.3 = (bf16[272,1152]{1,0:T(8,128)(2,1)S(1)}, bf16[272,1152]{1,0:T(8,128)(2,1)S(1)}, u32[]{:S(2)}, u32[]{:S(2)}) collective-permute-start(bf16[272,1152]{1,0:T(8,128)(2,1)S(1)} %get-tuple-element.37), channel_id=1, source_target_pairs={{2,0},{3,1},{4,2},{5,3},{6,4},{7,5},{8,6},{9,7},{10,8},{11,9},{12,... | collective-permute-start | bytes 1880072 | tf_op jit(solution)/shard_map/ppermute | solution.py:233
  10.0 0.1 collective-permute-start.5
  10.1 3.9 %collective-permute-start.4 = (bf16[128,1152]{1,0:T(8,128)(2,1)S(1)}, bf16[128,1152]{1,0:T(8,128)(2,1)S(1)}, u32[]{:S(2)}, u32[]{:S(2)}) collective-permute-start(bf16[128,1152]{1,0:T(8,128)(2,1)S(1)} %get-tuple-element.38), channel_id=1, source_target_pairs={{2,0},{3,1},{4,2},{5,3},{6,4},{7,5},{8,6},{9,7},{10,8},{11,9},{12,... | collective-permute-start | bytes 884744 | tf_op jit(solution)/shard_map/ppermute | solution.py:233
  14.0 19.2 %collective-permute-done.5.got_ref.refs_0_ = bf16[256,256]{1,0:T(8,128)(2,1)S(1)} collective-permute-done((bf16[256,256]{1,0:T(8,128)(2,1)S(1)}, bf16[256,256]{1,0:T(8,128)(2,1)S(1)}, u32[]{:S(2)}, u32[]{:S(2)}) %collective-permute-start.5) | collective-permute-done | bytes 131104 | tf_op jit(solution)/shard_map/ppermute | solution.py:237
  33.1 0.2 shard_map.82
  33.4 0.1 collective-permute-start.6
  33.4 4.9 %collective-permute-start.2 = (bf16[128,1152]{1,0:T(8,128)(2,1)S(1)}, bf16[128,1152]{1,0:T(8,128)(2,1)S(1)}, u32[]{:S(2)}, u32[]{:S(2)}) collective-permute-start(bf16[128,1152]{1,0:T(8,128)(2,1)S(1)} %get-tuple-element.36), channel_id=1, source_target_pairs={{2,0},{3,1},{4,2},{5,3},{6,4},{7,5},{8,6},{9,7},{10,8},{11,9},{12,... | collective-permute-start | bytes 884744 | tf_op jit(solution)/shard_map/ppermute | solution.py:233
  38.3 1.8 %shard_map.77.near_ref = f32[512,128]{1,0:T(8,128)S(1)} custom-call(bf16[512,1024]{1,0:T(8,128)(2,1)S(1)} %copy-done, f32[512,128]{1,0:T(8,128)S(1)} %get-tuple-element.32.x_ref), custom_call_target="tpu_custom_call" | custom-call | flops 805306368 | bytes 1572864 | tf_op jit(solution)/shard_map/pallas_call | solution.py:56
  40.1 0.2 shard_map.83
  40.4 0.1 collective-permute-start.7
  40.5 0.7 %shard_map.78 = (f32[512,128]{1,0:T(8,128)S(1)}, f32[512,128]{1,0:T(8,128)S(1)}, bf16[128,512]{1,0:T(8,128)(2,1)S(1)}, bf16[128,512]{1,0:T(8,128)(2,1)S(1)}) custom-call(bf16[512,1024]{1,0:T(8,128)(2,1)S(1)} %copy-done, bf16[512,1024]{1,0:T(8,128)(2,1)S(1)} %collective-permute-done.g_ref, f32[512,128]{1,0:T(8,128)S(1)} %shard_map.77.near_ref, ...), custom_call_target="tpu_custom_call" | custom-call | flops 805306368 | bytes 3932180 | tf_op jit(solution)/shard_map/pallas_call | solution.py:56
  41.2 2.4 %shard_map.79 = (f32[512,128]{1,0:T(8,128)S(1)}, f32[512,128]{1,0:T(8,128)S(1)}, f32[128,128]{1,0:T(8,128)S(1)}, f32[128,128]{1,0:T(8,128)S(1)}) custom-call(bf16[512,1024]{1,0:T(8,128)(2,1)S(1)} %copy-done, bf16[512,1024]{1,0:T(8,128)(2,1)S(1)} %collective-permute-done.g_ref, bf16[128,1152]{1,0:T(8,128)(2,1)S(1)} %collective-permute-done.4.h_ref, ...), custom_call_target="tpu_custom_call" | custom-call | flops 402653184 | bytes 3833876 | tf_op jit(solution)/shard_map/pallas_call | solution.py:56
  43.6 2.8 %shard_map.80 = (f32[512,128]{1,0:T(8,128)S(1)}, f32[512,128]{1,0:T(8,128)S(1)}, bf16[384,128]{1,0:T(8,128)(2,1)S(1)}) custom-call(bf16[512,1024]{1,0:T(8,128)(2,1)S(1)} %copy-done, bf16[512,1024]{1,0:T(8,128)(2,1)S(1)} %collective-permute-done.g_ref, bf16[272,1152]{1,0:T(8,128)(2,1)S(1)} %collective-permute-done.3.h_ref.refs_0_, ...), custom_call_target="tpu_custom_call" | custom-call | flops 805306368 | bytes 4890644 | tf_op jit(solution)/shard_map/pallas_call | solution.py:56
  46.5 2.5 %shard_map.81 = (f32[512,128]{1,0:T(8,128)S(1)}, bf16[512,128]{1,0:T(8,128)(2,1)S(1)}, bf16[128,128]{1,0:T(8,128)(2,1)S(1)}) custom-call(bf16[512,1024]{1,0:T(8,128)(2,1)S(1)} %copy-done, bf16[512,1024]{1,0:T(8,128)(2,1)S(1)} %collective-permute-done.g_ref, bf16[128,1152]{1,0:T(8,128)(2,1)S(1)} %collective-permute-done.2.h_ref, ...), custom_call_target="tpu_custom_call" | custom-call | flops 402653184 | bytes 4231188 | tf_op jit(solution)/shard_map/pallas_call | solution.py:56
  48.9 0.1 collective-permute-start.9
  49.0 0.7 shard_map.84
  49.7 3.9 %collective-permute-start.8 = (bf16[128,256]{1,0:T(8,128)(2,1)S(1)}, bf16[128,256]{1,0:T(8,128)(2,1)S(1)}, u32[]{:S(2)}, u32[]{:S(2)}) collective-permute-start(bf16[128,256]{1,0:T(8,128)(2,1)S(1)} %get-tuple-element.55), channel_id=1, source_target_pairs={{0,16},{1,17},{2,18},{3,19},{4,20},{5,21},{6,22},{7,23},{8,24},{9,... | collective-permute-start | bytes 196616 | tf_op jit(solution)/shard_map/ppermute | solution.py:237
  53.6 5.2 %collective-permute-start.10 = (bf16[384,128]{1,0:T(8,128)(2,1)S(1)}, bf16[384,128]{1,0:T(8,128)(2,1)S(1)}, u32[]{:S(2)}, u32[]{:S(2)}) collective-permute-start(bf16[384,128]{1,0:T(8,128)(2,1)S(1)} %get-tuple-element.57), channel_id=1, source_target_pairs={{0,2},{1,3},{2,4},{3,5},{4,6},{5,7},{6,8},{7,9},{8,10},{9,11},{10,... | collective-permute-start | bytes 294920 | tf_op jit(solution)/shard_map/ppermute | solution.py:233
  58.8 1.9 %collective-permute-start.11 = (bf16[128,128]{1,0:T(8,128)(2,1)S(1)}, bf16[128,128]{1,0:T(8,128)(2,1)S(1)}, u32[]{:S(2)}, u32[]{:S(2)}) collective-permute-start(bf16[128,128]{1,0:T(8,128)(2,1)S(1)} %get-tuple-element.58), channel_id=1, source_target_pairs={{0,2},{1,3},{2,4},{3,5},{4,6},{5,7},{6,8},{7,9},{8,10},{9,11},{10,... | collective-permute-start | bytes 98312 | tf_op jit(solution)/shard_map/ppermute | solution.py:233
  60.7 1.8 %shard_map.85.far_ref = f32[512,128]{1,0:T(8,128)S(1)} custom-call(f32[512,256]{1,0:T(8,128)S(1)} %collective-permute-done.1.got_ref.got0_ref, bf16[256,256]{1,0:T(8,128)(2,1)S(1)} %collective-permute-done.5.got_ref.refs_0_, bf16[256,256]{1,0:T(8,128)(2,1)S(1)} %collective-permute-done.6.got_ref.refs_1_, ...), custom_call_target="tpu_custom_call" | custom-call | flops 553648128 | bytes 4128768 | tf_op jit(solution)/shard_map/pallas_call | solution.py:56
  62.5 3.9 %collective-permute-done.11.refs_1_ = bf16[128,128]{1,0:T(8,128)(2,1)S(1)} collective-permute-done((bf16[128,128]{1,0:T(8,128)(2,1)S(1)}, bf16[128,128]{1,0:T(8,128)(2,1)S(1)}, u32[]{:S(2)}, u32[]{:S(2)}) %collective-permute-start.11) | collective-permute-done | bytes 32800 | tf_op jit(solution)/shard_map/ppermute | solution.py:233
  66.4 1.3 %shard_map.86 = f32[512,128]{1,0:T(8,128)} custom-call(f32[512,128]{1,0:T(8,128)S(1)} %get-tuple-element.49.near_ref, f32[512,128]{1,0:T(8,128)S(1)} %shard_map.85.far_ref, bf16[512,128]{1,0:T(8,128)(2,1)S(1)} %collective-permute-done.9.sib_ref, s32[1,4]{1,0:T(1,128)S(1)} %copy-done.4, s32[1]{0:T(128)S(6)} %copy.8.count_ref, ...), custom_call_target="tpu_custom_call" | custom-call | flops 393216 | bytes 1048596 | tf_op jit(solution)/shard_map/pallas_call | solution.py:56
  (16 shorter events, 0.0 us)
Async XLA Ops:
  0.0 40.4 %collective-permute-start = (bf16[512,1024]{1,0:T(8,128)(2,1)}, bf16[512,1024]{1,0:T(8,128)(2,1)S(1)}, u32[]{:S(2)}, u32[]{:S(2)}) collective-permute-start(bf16[512,1024]{1,0:T(8,128)(2,1)} %f_ref.11), channel_id=1, source_target_pairs={{0,1},{1,0},{2,3},{3,2},{4,5},{5,4},{6,7},{7,6},{8,9},{9,8},{10,11... | collective-permute-start | bytes 3145736 | tf_op jit(solution)/shard_map/ppermute | solution.py:237
  0.0 1.0 %copy-start.3 = (f32[512,128]{1,0:T(8,128)S(1)}, f32[512,128]{1,0:T(8,128)}, u32[]{:S(2)}) copy-start(f32[512,128]{1,0:T(8,128)} %x_hbm.1) | copy-start | bytes 786436
  2.2 2.7 %copy-start.1 = (f32[1,4,256,256]{3,2,1,0:T(8,128)S(1)}, f32[1,4,256,256]{3,2,1,0:T(8,128)}, u32[]{:S(2)}) copy-start(f32[1,4,256,256]{3,2,1,0:T(8,128)} %refs_5_.1) | copy-start | bytes 3145732
  2.8 2.4 %copy-start = (bf16[512,1024]{1,0:T(8,128)(2,1)S(1)}, bf16[512,1024]{1,0:T(8,128)(2,1)}, u32[]{:S(2)}) copy-start(bf16[512,1024]{1,0:T(8,128)(2,1)} %f_ref.11) | copy-start | bytes 3145732
  2.8 2.4 %copy-start.4 = (s32[1,4]{1,0:T(1,128)S(1)}, s32[1,4]{1,0:T(1,128)}, u32[]{:S(2)}) copy-start(s32[1,4]{1,0:T(1,128)} %list_ref.11) | copy-start | bytes 52
  2.8 2.1 %collective-permute-start.1 = (f32[512,256]{1,0:T(8,128)S(1)}, f32[512,256]{1,0:T(8,128)S(1)}, u32[]{:S(2)}, u32[]{:S(2)}) collective-permute-start(f32[512,256]{1,0:T(8,128)S(1)} %shard_map.74.own_ref), channel_id=1, source_target_pairs={{0,1},{1,0},{2,3},{3,2},{4,5},{5,4},{6,7},{7,6},{8,9},{9,8},{10,11... | collective-permute-start | bytes 1572872 | tf_op jit(solution)/shard_map/ppermute | solution.py:237
  5.8 37.9 %collective-permute-start.3 = (bf16[272,1152]{1,0:T(8,128)(2,1)S(1)}, bf16[272,1152]{1,0:T(8,128)(2,1)S(1)}, u32[]{:S(2)}, u32[]{:S(2)}) collective-permute-start(bf16[272,1152]{1,0:T(8,128)(2,1)S(1)} %get-tuple-element.37), channel_id=1, source_target_pairs={{2,0},{3,1},{4,2},{5,3},{6,4},{7,5},{8,6},{9,7},{10,8},{11,9},{12,... | collective-permute-start | bytes 1880072 | tf_op jit(solution)/shard_map/ppermute | solution.py:233
  10.0 23.1 %collective-permute-start.5 = (bf16[256,256]{1,0:T(8,128)(2,1)S(1)}, bf16[256,256]{1,0:T(8,128)(2,1)S(1)}, u32[]{:S(2)}, u32[]{:S(2)}) collective-permute-start(bf16[256,256]{1,0:T(8,128)(2,1)S(1)} %get-tuple-element.35.after_ref), channel_id=1, source_target_pairs={{0,2},{1,3},{2,0},{3,1},{4,6},{5,7},{6,4},{7,5},{8,10},{9,11},{10,... | collective-permute-start | bytes 393224 | tf_op jit(solution)/shard_map/ppermute | solution.py:237
  10.1 31.1 %collective-permute-start.4 = (bf16[128,1152]{1,0:T(8,128)(2,1)S(1)}, bf16[128,1152]{1,0:T(8,128)(2,1)S(1)}, u32[]{:S(2)}, u32[]{:S(2)}) collective-permute-start(bf16[128,1152]{1,0:T(8,128)(2,1)S(1)} %get-tuple-element.38), channel_id=1, source_target_pairs={{2,0},{3,1},{4,2},{5,3},{6,4},{7,5},{8,6},{9,7},{10,8},{11,9},{12,... | collective-permute-start | bytes 884744 | tf_op jit(solution)/shard_map/ppermute | solution.py:233
  33.4 6.8 %collective-permute-start.6 = (bf16[256,256]{1,0:T(8,128)(2,1)S(1)}, bf16[256,256]{1,0:T(8,128)(2,1)S(1)}, u32[]{:S(2)}, u32[]{:S(2)}) collective-permute-start(bf16[256,256]{1,0:T(8,128)(2,1)S(1)} %get-tuple-element.51), channel_id=1, source_target_pairs={{0,4},{1,5},{2,6},{3,7},{4,0},{5,1},{6,2},{7,3},{8,12},{9,13},{10,... | collective-permute-start | bytes 393224 | tf_op jit(solution)/shard_map/ppermute | solution.py:237
  33.4 13.0 %collective-permute-start.2 = (bf16[128,1152]{1,0:T(8,128)(2,1)S(1)}, bf16[128,1152]{1,0:T(8,128)(2,1)S(1)}, u32[]{:S(2)}, u32[]{:S(2)}) collective-permute-start(bf16[128,1152]{1,0:T(8,128)(2,1)S(1)} %get-tuple-element.36), channel_id=1, source_target_pairs={{2,0},{3,1},{4,2},{5,3},{6,4},{7,5},{8,6},{9,7},{10,8},{11,9},{12,... | collective-permute-start | bytes 884744 | tf_op jit(solution)/shard_map/ppermute | solution.py:233
  40.4 8.7 %collective-permute-start.7 = (bf16[256,256]{1,0:T(8,128)(2,1)S(1)}, bf16[256,256]{1,0:T(8,128)(2,1)S(1)}, u32[]{:S(2)}, u32[]{:S(2)}) collective-permute-start(bf16[256,256]{1,0:T(8,128)(2,1)S(1)} %get-tuple-element.53), channel_id=1, source_target_pairs={{0,8},{1,9},{2,10},{3,11},{4,12},{5,13},{6,14},{7,15},{8,0},{9,1},... | collective-permute-start | bytes 393224 | tf_op jit(solution)/shard_map/ppermute | solution.py:237
  48.9 11.8 %copy-start.2 = (f32[1,5,256,256]{3,2,1,0:T(8,128)S(1)}, f32[1,5,256,256]{3,2,1,0:T(8,128)}, u32[]{:S(2)}) copy-start(f32[1,5,256,256]{3,2,1,0:T(8,128)} %refs_4_.1) | copy-start | bytes 3932164
  48.9 17.4 %collective-permute-start.9 = (bf16[512,128]{1,0:T(8,128)(2,1)S(1)}, bf16[512,128]{1,0:T(8,128)(2,1)S(1)}, u32[]{:S(2)}, u32[]{:S(2)}) collective-permute-start(bf16[512,128]{1,0:T(8,128)(2,1)S(1)} %get-tuple-element.56), channel_id=1, source_target_pairs={{0,1},{1,0},{2,3},{3,2},{4,5},{5,4},{6,7},{7,6},{8,9},{9,8},{10,11... | collective-permute-start | bytes 393224 | tf_op jit(solution)/shard_map/ppermute | solution.py:237
  49.7 11.0 %collective-permute-start.8 = (bf16[128,256]{1,0:T(8,128)(2,1)S(1)}, bf16[128,256]{1,0:T(8,128)(2,1)S(1)}, u32[]{:S(2)}, u32[]{:S(2)}) collective-permute-start(bf16[128,256]{1,0:T(8,128)(2,1)S(1)} %get-tuple-element.55), channel_id=1, source_target_pairs={{0,16},{1,17},{2,18},{3,19},{4,20},{5,21},{6,22},{7,23},{8,24},{9,... | collective-permute-start | bytes 196616 | tf_op jit(solution)/shard_map/ppermute | solution.py:237
  53.6 12.8 %collective-permute-start.10 = (bf16[384,128]{1,0:T(8,128)(2,1)S(1)}, bf16[384,128]{1,0:T(8,128)(2,1)S(1)}, u32[]{:S(2)}, u32[]{:S(2)}) collective-permute-start(bf16[384,128]{1,0:T(8,128)(2,1)S(1)} %get-tuple-element.57), channel_id=1, source_target_pairs={{0,2},{1,3},{2,4},{3,5},{4,6},{5,7},{6,8},{7,9},{8,10},{9,11},{10,... | collective-permute-start | bytes 294920 | tf_op jit(solution)/shard_map/ppermute | solution.py:233
  58.8 7.6 %collective-permute-start.11 = (bf16[128,128]{1,0:T(8,128)(2,1)S(1)}, bf16[128,128]{1,0:T(8,128)(2,1)S(1)}, u32[]{:S(2)}, u32[]{:S(2)}) collective-permute-start(bf16[128,128]{1,0:T(8,128)(2,1)S(1)} %get-tuple-element.58), channel_id=1, source_target_pairs={{0,2},{1,3},{2,4},{3,5},{4,6},{5,7},{6,8},{7,9},{8,10},{9,11},{10,... | collective-permute-start | bytes 98312 | tf_op jit(solution)/shard_map/ppermute | solution.py:233

commit v3 on v2

v3 whole, which is shorter than its diff:
```python
import functools

import jax
import jax.numpy as jnp
from jax import lax
from jax.experimental import pallas as pl
from jax.experimental.pallas import tpu as pltpu
from jax.sharding import PartitionSpec as P

BF16 = jnp.bfloat16
F32 = jnp.float32
VMEM = pl.BlockSpec(memory_space=pltpu.VMEM)
SMEM = pl.BlockSpec(memory_space=pltpu.SMEM)
HBM = pl.BlockSpec(memory_space=pltpu.HBM)
ANY = pl.BlockSpec(memory_space=pl.ANY)
NN = (((1,), (0,)), ((), ()))
NT = (((1,), (1,)), ((), ()))
TN = (((0,), (0,)), ((), ()))
FLAG_ROWS = 16
LIMIT = 16 << 20
LOAD_LIMIT = 55500000
SHARED = ((), ((0, 1),), ((0, 1), (1, 0)), ((0, 1), (1, 0), (2, 1)))


def dot(a, b, dims):
    return lax.dot_general(a, b, dims, preferred_element_type=F32)


def halves(a):
    high = a.astype(BF16)
    return high, (a - high.astype(F32)).astype(BF16)


def dot_wide(a, b, dims):
    a_high, a_low = halves(a)
    b_high, b_low = halves(b)
    return dot(a_high, b_high, dims) + (dot(a_high, b_low, dims) + dot(a_low, b_high, dims))


def dot_half(a16, b, dims):
    b_high, b_low = halves(b)
    return dot(a16, b_high, dims) + dot(a16, b_low, dims)


def member(list_ref, count_ref, offset):
    index = lax.axis_index("leaf")
    found = jnp.float32(0.0)
    for slot in range(list_ref.shape[1]):
        hit = (list_ref[0, slot] == index + offset) & (slot < count_ref[0])
        found = jnp.where(hit, jnp.float32(1.0), found)
    return found


def call(kernel, outs, specs, flops, *args, scratch=(), limit=LIMIT):
    out_bytes = sum(o.size * o.dtype.itemsize for o in outs)
    in_bytes = sum(a.size * a.dtype.itemsize for a in args)
    return pl.pallas_call(
        kernel,
        out_shape=outs,
        in_specs=specs,
        out_specs=[VMEM] * len(outs),
        scratch_shapes=list(scratch),
        compiler_params=pltpu.CompilerParams(vmem_limit_bytes=limit),
        cost_estimate=pl.CostEstimate(flops=flops, bytes_accessed=in_bytes + out_bytes, transcendentals=0),
    )(*args)


def leaf_kernel(c1, bases_hbm, x_hbm, transfers_hbm, message_ref, bases_ref, x_ref, transfer_ref, sems):
    copies = [
        pltpu.make_async_copy(x_hbm, x_ref, sems.at[0]),
        pltpu.make_async_copy(bases_hbm, bases_ref, sems.at[1]),
        pltpu.make_async_copy(transfers_hbm.at[0, 0], transfer_ref, sems.at[2]),
    ]
    for copy in copies:
        copy.start()
    for copy in copies:
        copy.wait()
    x = x_ref[...]
    rows, probes = x.shape
    skeleton = dot_wide(x, bases_ref[...], TN)
    message_ref[:probes] = skeleton
    message_ref[probes : 2 * probes] = c1 * dot_wide(skeleton, transfer_ref[...], NN)
    message_ref[2 * probes :, :probes] = x[: rows // 2]
    message_ref[2 * probes :, probes:] = x[rows // 2 :]


def pack_kernel(sizes, f_ref, x_ref, list_ref, count_ref, *far_refs):
    width = f_ref.shape[1]
    probes = x_ref.shape[1]
    first = 0
    for size, far_ref in zip(sizes, far_refs):
        far_ref[:size, :width] = f_ref[first : first + size]
        far_ref[:size, width:] = x_ref[first : first + size].astype(BF16)
        first += size
    flags = [jnp.full((FLAG_ROWS, probes), member(list_ref, count_ref, offset), F32) for offset in (-2, -1)]
    flags.append(jnp.zeros((FLAG_ROWS, width - probes), F32))
    far_refs[0][sizes[0] :] = jnp.concatenate(flags, axis=1).astype(BF16)


def up_kernel(level, factor, own_ref, got_ref, transfer_ref, message_ref, next_ref):
    probes = next_ref.shape[0]
    own = own_ref[probes : 2 * probes] if own_ref.shape[0] > probes else own_ref[...]
    skeleton = own + got_ref[probes : 2 * probes].astype(F32)
    message_ref[:probes] = skeleton.astype(message_ref.dtype)
    moved = factor * dot_wide(skeleton, transfer_ref[0, level], NN)
    if message_ref.shape[0] > probes:
        message_ref[probes:] = moved.astype(message_ref.dtype)
    next_ref[...] = moved.astype(next_ref.dtype)


def bit_of(level):
    return lax.rem(lax.axis_index("leaf") >> level, 2)


def descend(scale_g, factor, got, coupling, transfer, above):
    wide = dot_wide if got.dtype == F32 else dot_half
    update = scale_g * wide(got, coupling, NT)
    return update if above is None else update + factor * dot_wide(above, transfer, NT)


def top_kernel(scale_g, factor, coupling_ref, transfer_ref, got_ref, term_ref, other_ref, own_ref, message_ref):
    depth = transfer_ref.shape[1]
    sibling = term_ref[...].astype(F32) + other_ref[...].astype(F32)
    root = descend(scale_g, None, sibling, coupling_ref[0, depth], None, None)
    out = descend(scale_g, factor, got_ref[...], coupling_ref[0, depth - 1], transfer_ref[0, depth - 1], root)
    own_ref[...] = out
    message_ref[...] = out.astype(BF16)


def middle_kernel(scale_g, factor, level, coupling_ref, transfer_ref, got_ref, above_ref, sent_ref, own_ref, message_ref):
    probes = own_ref.shape[0]
    above = jnp.where(bit_of(level) == 1, above_ref[...], sent_ref[...].astype(F32))
    out = descend(scale_g, factor, got_ref[:probes], coupling_ref[0, level], transfer_ref[0, level], above)
    own_ref[...] = out
    message_ref[...] = out.astype(BF16)


def node_kernel(scale_g, factor, level, coupling_ref, transfer_ref, got_ref, above_ref, sent_ref, own_ref):
    probes = own_ref.shape[0]
    above = jnp.where(bit_of(level) == 0, above_ref[...], sent_ref[...].astype(F32))
    own_ref[...] = descend(scale_g, factor, got_ref[:probes], coupling_ref[0, level], transfer_ref[0, level], above)


def down_kernel(scale_g, factor, coupling_ref, transfer_ref, bases_ref, got_ref, above_ref, sent_ref, out_ref):
    probes = out_ref.shape[1]
    above = jnp.where(bit_of(0) == 1, above_ref[...], sent_ref[...])
    expansion = descend(scale_g, factor, got_ref[:probes], coupling_ref[0, 0], transfer_ref[0, 0], above)
    out_ref[...] = dot_wide(bases_ref[...], expansion, NT)


def tile(rows_a, rows_b, scale):
    gram = dot(rows_a, rows_b, NT)
    return halves(gram * gram * scale)


def self_kernel(scale, f_ref, x_ref, out_ref):
    high, low = tile(f_ref[...], f_ref[...], scale)
    x_high, x_low = halves(x_ref[...])
    out_ref[...] = dot(high, x_high, NN) + (dot(high, x_low, NN) + dot(low, x_high, NN))


def times(parts, x16):
    return dot(parts[0], x16, NN) + dot(parts[1], x16, NN)


def times_back(parts, xt16):
    return (dot(xt16, parts[0], NN) + dot(xt16, parts[1], NN)).T


def pair_kernel(scale, f_ref, g_ref, near_ref, x_ref, got_ref, list_ref, count_ref, out_ref, sib_ref, xt_ref, xst_ref):
    odd = lax.rem(lax.axis_index("leaf"), 2) == 1
    rows, probes = near_ref.shape
    xt_ref[...] = x_ref[...].T.astype(BF16)
    for half in range(2):
        part = got_ref[2 * probes :, half * probes : (half + 1) * probes]
        xst_ref[:, half * (rows // 2) : (half + 1) * (rows // 2)] = part.T.astype(BF16)

    @pl.when(odd)
    def _():
        parts = tile(g_ref[...], f_ref[...], scale)
        sib_ref[...] = times(parts, x_ref[...].astype(BF16))
        flag = member(list_ref, count_ref, -1)
        out_ref[...] = near_ref[...] + flag * times_back(parts, xst_ref[...])

    @pl.when(jnp.logical_not(odd))
    def _():
        out_ref[...] = near_ref[...]
        sib_ref[...] = jnp.zeros_like(sib_ref)


def chunk_kernel(scale, size, f_ref, g_ref, h_ref, flags_ref, near_ref, sib_in_ref, xt_ref, xst_ref, list_ref, count_ref, out_ref, sib_ref, back_ref):
    even = lax.rem(lax.axis_index("leaf"), 2) == 0
    width = f_ref.shape[1]
    probes = near_ref.shape[1]
    h = h_ref[:size, :width]
    xh = h_ref[:size, width:]
    at = flags_ref.shape[0] - FLAG_ROWS
    flag2 = flags_ref[at : at + 1, :probes].astype(F32)
    flag1 = flags_ref[at : at + 1, probes : 2 * probes].astype(F32)
    parts = tile(f_ref[...], h, scale)
    out_ref[...] = near_ref[...] + member(list_ref, count_ref, 2) * times(parts, xh)
    back = flag2 * times_back(parts, xt_ref[...])

    @pl.when(even)
    def _():
        cross = tile(g_ref[...], h, scale)
        sib_ref[...] = (sib_in_ref[...] + times(cross, xh)).astype(sib_ref.dtype)
        back_ref[...] = (back + flag1 * times_back(cross, xst_ref[...])).astype(BF16)

    @pl.when(jnp.logical_not(even))
    def _():
        sib_ref[...] = sib_in_ref[...].astype(sib_ref.dtype)
        back_ref[...] = back.astype(BF16)


def final_kernel(near_ref, far_ref, sib_ref, list_ref, count_ref, *refs):
    out_ref = refs[-1]
    flag = member(list_ref, count_ref, 1)
    at = 0
    for back_ref in refs[:-1]:
        rows = slice(at, at + back_ref.shape[0])
        out_ref[rows] = near_ref[rows] + far_ref[rows] + flag * sib_ref[rows].astype(F32) + back_ref[...].astype(F32)
        at += back_ref.shape[0]


def moved(array, by):
    peers = lax.axis_size("leaf")
    return lax.ppermute(array, "leaf", [(i, i + by) for i in range(peers) if 0 <= i + by < peers])


def across(array, distance, bits=()):
    senders = [i for i in range(lax.axis_size("leaf")) if all(i >> at & 1 == bit for at, bit in bits)]
    return lax.ppermute(array, "leaf", [(i, i ^ distance) for i in senders])


def partner(array, level, bits=()):
    return across(array, 1 << level, bits)


def body(features, probes, bases, transfers, couplings, near_list, near_count):
    rows, width = features.shape
    count = probes.shape[1]
    rank = bases.shape[1]
    depth = transfers.shape[1]
    scale = 1.0 / (rows * width)
    scale_g = (3.0 / rank) ** 0.5
    factors = [scale_g * 2.0 ** (-0.5 * (level + 1)) for level in range(depth)]
    shape = jax.ShapeDtypeStruct
    sizes = [rows // 2, rows // 2]

    sib_features = partner(features, 0)
    (message,) = call(
        functools.partial(leaf_kernel, factors[0]),
        [shape((2 * count + rows // 2, rank), F32)],
        [HBM] * 3,
        6 * rows * rank * count,
        bases, probes, transfers,
        scratch=[
            pltpu.VMEM((rows, rank), F32),
            pltpu.VMEM((rows, count), F32),
            pltpu.VMEM((rank, rank), F32),
            pltpu.SemaphoreType.DMA((3,)),
        ],
        limit=LOAD_LIMIT,
    )
    gots = [partner(message, 0)]
    packed = call(
        functools.partial(pack_kernel, sizes),
        [shape((size + (0 if i else FLAG_ROWS), width + count), BF16) for i, size in enumerate(sizes)],
        [VMEM, VMEM, SMEM, SMEM],
        1000,
        features, probes, near_list, near_count,
    )
    far = [moved(part, -2) for part in packed]
    own = [message]
    top = depth - 1
    for level in range(1, top + 1):
        message, *own = call(
            functools.partial(up_kernel, level, factors[level]),
            [shape((2 * count, rank), BF16), shape((count, rank), F32)] if level < top else [shape((count, rank), BF16)] * 2,
            [VMEM] * 3,
            6 * rank * rank * count,
            *own, gots[-1], transfers,
        )
        if level < top:
            gots.append(partner(message, level, SHARED[level]))
    gots.append(partner(message, top, SHARED[top]))
    terms = [across(own[0], (1 << top + 1) + extra, SHARED[top]) for extra in (0, 1 << top)]

    tile_flops = 2 * rows * rows * (width + 4 * count)
    (near,) = call(
        functools.partial(self_kernel, scale),
        [shape((rows, count), F32)],
        [VMEM, VMEM],
        tile_flops,
        features, probes,
    )
    near, sib, xt, xst = call(
        functools.partial(pair_kernel, scale),
        [shape((rows, count), F32)] * 2 + [shape((count, rows), BF16)] * 2,
        [VMEM] * 5 + [SMEM] * 2,
        tile_flops,
        features, sib_features, near, probes, gots[0], near_list, near_count,
    )
    backs = []
    for stage, (size, part) in enumerate(zip(sizes, far)):
        last = stage == len(sizes) - 1
        near, sib, back = call(
            functools.partial(chunk_kernel, scale, size),
            [shape((rows, count), F32), shape((rows, count), BF16 if last else F32), shape((size, count), BF16)],
            [VMEM] * 8 + [SMEM] * 2,
            tile_flops * 2 * size // rows,
            features, sib_features, part, far[0], near, sib, xt, xst, near_list, near_count,
        )
        backs.append(moved(back, 2))
    sib_got = partner(sib, 0)
    product_flops = 6 * count * rank * rank
    e3, e3_message = call(
        functools.partial(top_kernel, scale_g, factors[top]),
        [shape((count, rank), F32), shape((count, rank), BF16)],
        [VMEM] * 5,
        3 * product_flops,
        couplings, transfers, gots[top], *terms,
    )
    e3_sent = partner(e3_message, 2, SHARED[3])
    e2, e2_message = call(
        functools.partial(middle_kernel, scale_g, factors[2], 2),
        [shape((count, rank), F32), shape((count, rank), BF16)],
        [VMEM] * 5,
        2 * product_flops,
        couplings, transfers, gots[2], e3, e3_sent,
    )
    e2_sent = partner(e2_message, 1, SHARED[2])
    (e1,) = call(
        functools.partial(node_kernel, scale_g, factors[1], 1),
        [shape((count, rank), F32)],
        [VMEM] * 5,
        2 * product_flops,
        couplings, transfers, gots[1], e2, e2_sent,
    )
    e1_sent = partner(e1, 0, SHARED[1])
    (far_sum,) = call(
        functools.partial(down_kernel, scale_g, factors[0]),
        [shape((rows, count), F32)],
        [VMEM] * 6,
        2 * product_flops + 6 * rows * rank * count,
        couplings, transfers, bases, gots[0], e1, e1_sent,
    )
    (out,) = call(
        final_kernel,
        [shape((rows, count), F32)],
        [VMEM] * 3 + [SMEM] * 2 + [VMEM] * len(backs),
        6 * rows * count,
        near, far_sum, sib_got, near_list, near_count, *backs,
    )
    return out


def solution(mesh):
    in_specs = (
        P("leaf", None),
        P("leaf", None),
        P("leaf", None),
        P("leaf", None, None, None),
        P("leaf", None, None, None),
        P("leaf", None),
        P("leaf"),
    )
    out_specs = P("leaf", None)
    return jax.shard_map(body, mesh=mesh, in_specs=in_specs, out_specs=out_specs, check_vma=False)
```

time: 68 us -> 61.2 us (0.900)
  waiting for transfers between devices: 24 us -> 17.8 us
  Pallas kernels: 17 us -> 14.7 us
  starting transfers between devices: 24.8 us -> 26.2 us
    ppermute x7 -> x11, waiting for transfers between devices: 20.1 us -> 1.42 us  [across(): return lax.ppermute(array, 'leaf', [(i, i ^ distance) for i in senders])]
    ppermute x5 -> x4, waiting for transfers between devices: 3.88 us -> 16.4 us  [moved(): lax.ppermute(array, 'leaf', [(i, i + by) for i in range(peers) if 0 <= i...]
    ppermute x7 -> x11, starting transfers between devices: 4.71 us -> 13.5 us  [across(): return lax.ppermute(array, 'leaf', [(i, i ^ distance) for i in senders])]
    ppermute x5 -> x4, starting transfers between devices: 20.1 us -> 12.7 us  [moved(): lax.ppermute(array, 'leaf', [(i, i + by) for i in range(peers) if 0 <= i...]
    pallas_call x14, Pallas kernels: 17 us -> 14.7 us  [call(): pl.pallas_call(kernel, out_shape=outs, in_specs=specs, out_specs=[VMEM] *...]
  transfers between devices with their start and end apart: 12 -> 15, of which waited for: 3 -> 5; matrix products, arithmetic and copies ran while one was open for 0% -> 0% of each run, Pallas kernels for 23% -> 19%
where the time goes in v3:
time: 61.2 us; the launch traced here: 60.7 us
  starting transfers between devices  26.2 us (43%)
  waiting for transfers between devices  17.8 us (29%)
  Pallas kernels  14.7 us (24%)
  local copies, waits for them, and re-layouts  1.12 us (2%)
  between operations  0.97 us (2%)
    ppermute x4, waiting for transfers between devices, moved(): lax.ppermute(array, 'leaf', [(i, i + by) for i in range(peers) if 0 <= i...  16.4 us
    pallas_call x14, Pallas kernels, call(): pl.pallas_call(kernel, out_shape=outs, in_specs=specs, out_specs=[VMEM] *...  14.7 us
    ppermute x11, starting transfers between devices, across(): return lax.ppermute(array, 'leaf', [(i, i ^ distance) for i in senders])  13.5 us
    ppermute x4, starting transfers between devices, moved(): lax.ppermute(array, 'leaf', [(i, i + by) for i in range(peers) if 0 <= i...  12.7 us
    ppermute x11, waiting for transfers between devices, across(): return lax.ppermute(array, 'leaf', [(i, i ^ distance) for i in senders])  1.42 us
  transfers between devices with their start and end apart: 15, of which 5 were waited for; matrix products, arithmetic and copies ran while one was open for 0% of the time, Pallas kernels for 19%

profile of v3, /device:TPU:8, one launch (start us, length us, event | category | flops | bytes accessed | tf_op | source)
XLA Modules:
  0.0 60.7 jit_solution(6070118559813946700)
XLA Ops:
  0.0 1.1 %copy-done.3 = f32[512,128]{1,0:T(8,128)S(1)} copy-done((f32[512,128]{1,0:T(8,128)S(1)}, f32[512,128]{1,0:T(8,128)}, u32[]{:S(2)}) %copy-start.3) | copy-done | bytes 262168
  1.1 1.7 %shard_map.75.own_ref = f32[512,256]{1,0:T(8,128)S(1)} custom-call(f32[512,256]{1,0:T(8,128)} %bases_ref.1, f32[512,128]{1,0:T(8,128)S(1)} %copy-done.3, f32[1,4,256,256]{3,2,1,0:T(8,128)} %transfer_ref.13), custom_call_target="tpu_custom_call" | custom-call | flops 100663296 | bytes 2359296 | tf_op jit(solution)/shard_map/pallas_call | solution.py:57
  2.9 0.5 collective-permute-start
  3.4 1.4 %collective-permute-done.3.got_ref = f32[512,256]{1,0:T(8,128)S(1)} collective-permute-done((f32[512,256]{1,0:T(8,128)S(1)}, f32[512,256]{1,0:T(8,128)S(1)}, u32[]{:S(2)}, u32[]{:S(2)}) %collective-permute-start.3) | collective-permute-done | bytes 524320 | tf_op jit(solution)/shard_map/ppermute | solution.py:233
  4.8 0.2 shard_map.79
  5.0 0.7 %collective-permute-start.4 = (bf16[256,256]{1,0:T(8,128)(2,1)S(1)}, bf16[256,256]{1,0:T(8,128)(2,1)S(1)}, u32[]{:S(2)}, u32[]{:S(2)}) collective-permute-start(bf16[256,256]{1,0:T(8,128)(2,1)S(1)} %get-tuple-element.36), channel_id=1, source_target_pairs={{1,3},{3,1},{5,7},{7,5},{9,11},{11,9},{13,15},{15,13},{17,19},{19,... | collective-permute-start | bytes 393224 | tf_op jit(solution)/shard_map/ppermute | solution.py:233
  6.4 0.6 %shard_map.73 = (bf16[272,1152]{1,0:T(8,128)(2,1)S(1)}, bf16[256,1152]{1,0:T(8,128)(2,1)S(1)}) custom-call(bf16[512,1024]{1,0:T(8,128)(2,1)S(1)} %copy-done.2, f32[512,128]{1,0:T(8,128)S(1)} %copy-done.3, s32[1,4]{1,0:T(1,128)S(1)} %copy-done.5, s32[1]{0:T(128)S(6)} %copy.8.count_ref), custom_call_target="tpu_custom_call" | custom-call | flops 1000 | bytes 2527252 | tf_op jit(solution)/shard_map/pallas_call | solution.py:57
  7.0 4.2 %collective-permute-start.2 = (bf16[272,1152]{1,0:T(8,128)(2,1)S(1)}, bf16[272,1152]{1,0:T(8,128)(2,1)S(1)}, u32[]{:S(2)}, u32[]{:S(2)}) collective-permute-start(bf16[272,1152]{1,0:T(8,128)(2,1)S(1)} %get-tuple-element.28), channel_id=1, source_target_pairs={{2,0},{3,1},{4,2},{5,3},{6,4},{7,5},{8,6},{9,7},{10,8},{11,9},{12,... | collective-permute-start | bytes 1880072 | tf_op jit(solution)/shard_map/ppermute | solution.py:228
  11.5 0.8 %collective-permute-start.5 = (bf16[256,256]{1,0:T(8,128)(2,1)S(1)}, bf16[256,256]{1,0:T(8,128)(2,1)S(1)}, u32[]{:S(2)}, u32[]{:S(2)}) collective-permute-start(bf16[256,256]{1,0:T(8,128)(2,1)S(1)} %get-tuple-element.38), channel_id=1, source_target_pairs={{1,5},{5,1},{9,13},{13,9},{17,21},{21,17},{25,29},{29,25}} | collective-permute-start | bytes 393224 | tf_op jit(solution)/shard_map/ppermute | solution.py:233
  12.3 2.4 %collective-permute-start.1 = (bf16[256,1152]{1,0:T(8,128)(2,1)S(1)}, bf16[256,1152]{1,0:T(8,128)(2,1)S(1)}, u32[]{:S(2)}, u32[]{:S(2)}) collective-permute-start(bf16[256,1152]{1,0:T(8,128)(2,1)S(1)} %get-tuple-element.27), channel_id=1, source_target_pairs={{2,0},{3,1},{4,2},{5,3},{6,4},{7,5},{8,6},{9,7},{10,8},{11,9},{12,... | collective-permute-start | bytes 1769480 | tf_op jit(solution)/shard_map/ppermute | solution.py:228
  15.0 0.7 %collective-permute-start.6 = (bf16[128,256]{1,0:T(8,128)(2,1)S(1)}, bf16[128,256]{1,0:T(8,128)(2,1)S(1)}, u32[]{:S(2)}, u32[]{:S(2)}) collective-permute-start(bf16[128,256]{1,0:T(8,128)(2,1)S(1)} %get-tuple-element.40), channel_id=1, source_target_pairs={{5,13},{13,5},{21,29},{29,21}} | collective-permute-start | bytes 196616 | tf_op jit(solution)/shard_map/ppermute | solution.py:233
  15.7 0.7 %collective-permute-start.8 = (bf16[128,256]{1,0:T(8,128)(2,1)S(1)}, bf16[128,256]{1,0:T(8,128)(2,1)S(1)}, u32[]{:S(2)}, u32[]{:S(2)}) collective-permute-start(bf16[128,256]{1,0:T(8,128)(2,1)S(1)} %get-tuple-element.41), channel_id=1, source_target_pairs={{5,29},{13,21},{21,13},{29,5}} | collective-permute-start | bytes 196616 | tf_op jit(solution)/shard_map/ppermute | solution.py:233
  16.4 0.7 %collective-permute-start.7 = (bf16[128,256]{1,0:T(8,128)(2,1)S(1)}, bf16[128,256]{1,0:T(8,128)(2,1)S(1)}, u32[]{:S(2)}, u32[]{:S(2)}) collective-permute-start(bf16[128,256]{1,0:T(8,128)(2,1)S(1)} %get-tuple-element.41), channel_id=1, source_target_pairs={{5,21},{13,29},{21,5},{29,13}} | collective-permute-start | bytes 196616 | tf_op jit(solution)/shard_map/ppermute | solution.py:233
  17.1 0.6 %shard_map.82 = (f32[128,256]{1,0:T(8,128)S(1)}, bf16[128,256]{1,0:T(8,128)(2,1)S(1)}) custom-call(f32[1,5,256,256]{3,2,1,0:T(8,128)S(1)} %copy-done.1, f32[1,4,256,256]{3,2,1,0:T(8,128)S(1)} %copy-done, bf16[128,256]{1,0:T(8,128)(2,1)S(1)} %collective-permute-done.6.got_ref, bf16[128,256]{1,0:T(8,128)(2,1)S(1)} %collective-permute-done.7.term_ref, ...), custom_call_target="tpu_custom_call" | custom-call | flops 150994944 | bytes 2752512 | tf_op jit(solution)/shard_map/pallas_call | solution.py:57
  17.7 0.7 %collective-permute-start.9 = (bf16[128,256]{1,0:T(8,128)(2,1)S(1)}, bf16[128,256]{1,0:T(8,128)(2,1)S(1)}, u32[]{:S(2)}, u32[]{:S(2)}) collective-permute-start(bf16[128,256]{1,0:T(8,128)(2,1)S(1)} %get-tuple-element.43), channel_id=1, source_target_pairs={{5,1},{13,9},{21,17},{29,25}} | collective-permute-start | bytes 196616 | tf_op jit(solution)/shard_map/ppermute | solution.py:233
  18.4 0.4 shard_map.83
  18.8 0.7 %collective-permute-start.10 = (bf16[128,256]{1,0:T(8,128)(2,1)S(1)}, bf16[128,256]{1,0:T(8,128)(2,1)S(1)}, u32[]{:S(2)}, u32[]{:S(2)}) collective-permute-start(bf16[128,256]{1,0:T(8,128)(2,1)S(1)} %get-tuple-element.45), channel_id=1, source_target_pairs={{1,3},{5,7},{9,11},{13,15},{17,19},{21,23},{25,27},{29,31}} | collective-permute-start | bytes 196616 | tf_op jit(solution)/shard_map/ppermute | solution.py:233
  19.4 1.8 %shard_map.74.near_ref = f32[512,128]{1,0:T(8,128)S(1)} custom-call(bf16[512,1024]{1,0:T(8,128)(2,1)S(1)} %copy-done.2, f32[512,128]{1,0:T(8,128)S(1)} %copy-done.3), custom_call_target="tpu_custom_call" | custom-call | flops 805306368 | bytes 1572864 | tf_op jit(solution)/shard_map/pallas_call | solution.py:57
  21.2 0.4 shard_map.84.above_ref
  21.6 1.3 %collective-permute-start.11 = (f32[128,256]{1,0:T(8,128)S(1)}, f32[128,256]{1,0:T(8,128)S(1)}, u32[]{:S(2)}, u32[]{:S(2)}) collective-permute-start(f32[128,256]{1,0:T(8,128)S(1)} %shard_map.84.above_ref), channel_id=1, source_target_pairs={{1,0},{3,2},{5,4},{7,6},{9,8},{11,10},{13,12},{15,14},{17,16},{19,... | collective-permute-start | bytes 393224 | tf_op jit(solution)/shard_map/ppermute | solution.py:233
  22.9 0.7 %shard_map.76 = (f32[512,128]{1,0:T(8,128)S(1)}, f32[512,128]{1,0:T(8,128)S(1)}, bf16[128,512]{1,0:T(8,128)(2,1)S(1)}, bf16[128,512]{1,0:T(8,128)(2,1)S(1)}) custom-call(bf16[512,1024]{1,0:T(8,128)(2,1)S(1)} %copy-done.2, bf16[512,1024]{1,0:T(8,128)(2,1)S(1)} %collective-permute-done.g_ref, f32[512,128]{1,0:T(8,128)S(1)} %shard_map.74.near_ref, ...), custom_call_target="tpu_custom_call" | custom-call | flops 805306368 | bytes 3932180 | tf_op jit(solution)/shard_map/pallas_call | solution.py:57
  23.7 1.4 %collective-permute-done.2.h_ref.flags_ref = bf16[272,1152]{1,0:T(8,128)(2,1)S(1)} collective-permute-done((bf16[272,1152]{1,0:T(8,128)(2,1)S(1)}, bf16[272,1152]{1,0:T(8,128)(2,1)S(1)}, u32[]{:S(2)}, u32[]{:S(2)}) %collective-permute-start.2) | collective-permute-done | bytes 626720 | tf_op jit(solution)/shard_map/ppermute | solution.py:228
  25.1 2.8 %shard_map.77 = (f32[512,128]{1,0:T(8,128)S(1)}, f32[512,128]{1,0:T(8,128)S(1)}, bf16[256,128]{1,0:T(8,128)(2,1)S(1)}) custom-call(bf16[512,1024]{1,0:T(8,128)(2,1)S(1)} %copy-done.2, bf16[512,1024]{1,0:T(8,128)(2,1)S(1)} %collective-permute-done.g_ref, bf16[272,1152]{1,0:T(8,128)(2,1)S(1)} %collective-permute-done.2.h_ref.flags_ref, ...), custom_call_target="tpu_custom_call" | custom-call | flops 805306368 | bytes 4726804 | tf_op jit(solution)/shard_map/pallas_call | solution.py:57
  27.9 9.8 %collective-permute-done.1.h_ref = bf16[256,1152]{1,0:T(8,128)(2,1)S(1)} collective-permute-done((bf16[256,1152]{1,0:T(8,128)(2,1)S(1)}, bf16[256,1152]{1,0:T(8,128)(2,1)S(1)}, u32[]{:S(2)}, u32[]{:S(2)}) %collective-permute-start.1) | collective-permute-done | bytes 589856 | tf_op jit(solution)/shard_map/ppermute | solution.py:228
  37.7 2.8 %shard_map.78 = (f32[512,128]{1,0:T(8,128)S(1)}, bf16[512,128]{1,0:T(8,128)(2,1)S(1)}, bf16[256,128]{1,0:T(8,128)(2,1)S(1)}) custom-call(bf16[512,1024]{1,0:T(8,128)(2,1)S(1)} %copy-done.2, bf16[512,1024]{1,0:T(8,128)(2,1)S(1)} %collective-permute-done.g_ref, bf16[256,1152]{1,0:T(8,128)(2,1)S(1)} %collective-permute-done.1.h_ref, ...), custom_call_target="tpu_custom_call" | custom-call | flops 805306368 | bytes 4558868 | tf_op jit(solution)/shard_map/pallas_call | solution.py:57
  40.5 6.9 %collective-permute-start.12 = (bf16[512,128]{1,0:T(8,128)(2,1)S(1)}, bf16[512,128]{1,0:T(8,128)(2,1)S(1)}, u32[]{:S(2)}, u32[]{:S(2)}) collective-permute-start(bf16[512,128]{1,0:T(8,128)(2,1)S(1)} %get-tuple-element.46), channel_id=1, source_target_pairs={{0,1},{1,0},{2,3},{3,2},{4,5},{5,4},{6,7},{7,6},{8,9},{9,8},{10,11... | collective-permute-start | bytes 393224 | tf_op jit(solution)/shard_map/ppermute | solution.py:233
  47.4 4.1 %collective-permute-start.14 = (bf16[256,128]{1,0:T(8,128)(2,1)S(1)}, bf16[256,128]{1,0:T(8,128)(2,1)S(1)}, u32[]{:S(2)}, u32[]{:S(2)}) collective-permute-start(bf16[256,128]{1,0:T(8,128)(2,1)S(1)} %get-tuple-element.48), channel_id=1, source_target_pairs={{0,2},{1,3},{2,4},{3,5},{4,6},{5,7},{6,8},{7,9},{8,10},{9,11},{10,... | collective-permute-start | bytes 196616 | tf_op jit(solution)/shard_map/ppermute | solution.py:228
  51.5 1.9 %collective-permute-start.13 = (bf16[256,128]{1,0:T(8,128)(2,1)S(1)}, bf16[256,128]{1,0:T(8,128)(2,1)S(1)}, u32[]{:S(2)}, u32[]{:S(2)}) collective-permute-start(bf16[256,128]{1,0:T(8,128)(2,1)S(1)} %get-tuple-element.47), channel_id=1, source_target_pairs={{0,2},{1,3},{2,4},{3,5},{4,6},{5,7},{6,8},{7,9},{8,10},{9,11},{10,... | collective-permute-start | bytes 196616 | tf_op jit(solution)/shard_map/ppermute | solution.py:228
  53.4 0.9 %shard_map.85.far_ref = f32[512,128]{1,0:T(8,128)S(1)} custom-call(f32[1,5,256,256]{3,2,1,0:T(8,128)S(1)} %copy-done.1, f32[1,4,256,256]{3,2,1,0:T(8,128)S(1)} %copy-done, f32[512,256]{1,0:T(8,128)S(1)} %copy-done.4, f32[512,256]{1,0:T(8,128)S(1)} %collective-permute-done.3.got_ref, f32[128,256]{1,0:T(8,128)S(1)} %shard_map.84.above_ref, ...), custom_call_target="tpu_custom_call" | custom-call | flops 201326592 | bytes 3932160 | tf_op jit(solution)/shard_map/pallas_call | solution.py:57
  54.3 1.1 %collective-permute-done.14.refs_1_ = bf16[256,128]{1,0:T(8,128)(2,1)S(1)} collective-permute-done((bf16[256,128]{1,0:T(8,128)(2,1)S(1)}, bf16[256,128]{1,0:T(8,128)(2,1)S(1)}, u32[]{:S(2)}, u32[]{:S(2)}) %collective-permute-start.14) | collective-permute-done | bytes 65568 | tf_op jit(solution)/shard_map/ppermute | solution.py:228
  55.3 4.1 %collective-permute-done.13.refs_0_ = bf16[256,128]{1,0:T(8,128)(2,1)S(1)} collective-permute-done((bf16[256,128]{1,0:T(8,128)(2,1)S(1)}, bf16[256,128]{1,0:T(8,128)(2,1)S(1)}, u32[]{:S(2)}, u32[]{:S(2)}) %collective-permute-start.13) | collective-permute-done | bytes 65568 | tf_op jit(solution)/shard_map/ppermute | solution.py:228
  59.4 1.3 %shard_map.86 = f32[512,128]{1,0:T(8,128)} custom-call(f32[512,128]{1,0:T(8,128)S(1)} %get-tuple-element.35.near_ref, f32[512,128]{1,0:T(8,128)S(1)} %shard_map.85.far_ref, bf16[512,128]{1,0:T(8,128)(2,1)S(1)} %collective-permute-done.12.sib_ref, s32[1,4]{1,0:T(1,128)S(1)} %copy-done.5, s32[1]{0:T(128)S(6)} %copy.8.count_ref, ...), custom_call_target="tpu_custom_call" | custom-call | flops 393216 | bytes 1048596 | tf_op jit(solution)/shard_map/pallas_call | solution.py:57
  (24 shorter events, 0.6 us)
Async XLA Ops:
  0.0 4.8 %copy-start = (f32[1,4,256,256]{3,2,1,0:T(8,128)S(1)}, f32[1,4,256,256]{3,2,1,0:T(8,128)}, u32[]{:S(2)}) copy-start(f32[1,4,256,256]{3,2,1,0:T(8,128)} %transfer_ref.13) | copy-start | bytes 3145732
  0.0 2.9 %copy-start.2 = (bf16[512,1024]{1,0:T(8,128)(2,1)S(1)}, bf16[512,1024]{1,0:T(8,128)(2,1)}, u32[]{:S(2)}) copy-start(bf16[512,1024]{1,0:T(8,128)(2,1)} %f_ref.9) | copy-start | bytes 3145732
  0.0 1.1 %copy-start.3 = (f32[512,128]{1,0:T(8,128)S(1)}, f32[512,128]{1,0:T(8,128)}, u32[]{:S(2)}) copy-start(f32[512,128]{1,0:T(8,128)} %x_ref.5) | copy-start | bytes 786436
  2.8 3.5 %copy-start.5 = (s32[1,4]{1,0:T(1,128)S(1)}, s32[1,4]{1,0:T(1,128)}, u32[]{:S(2)}) copy-start(s32[1,4]{1,0:T(1,128)} %list_ref.9) | copy-start | bytes 52
  2.8 2.0 %collective-permute-start.3 = (f32[512,256]{1,0:T(8,128)S(1)}, f32[512,256]{1,0:T(8,128)S(1)}, u32[]{:S(2)}, u32[]{:S(2)}) collective-permute-start(f32[512,256]{1,0:T(8,128)S(1)} %shard_map.75.own_ref), channel_id=1, source_target_pairs={{0,1},{1,0},{2,3},{3,2},{4,5},{5,4},{6,7},{7,6},{8,9},{9,8},{10,11... | collective-permute-start | bytes 1572872 | tf_op jit(solution)/shard_map/ppermute | solution.py:233
  2.9 20.0 %collective-permute-start = (bf16[512,1024]{1,0:T(8,128)(2,1)S(1)}, bf16[512,1024]{1,0:T(8,128)(2,1)S(1)}, u32[]{:S(2)}, u32[]{:S(2)}) collective-permute-start(bf16[512,1024]{1,0:T(8,128)(2,1)S(1)} %copy-done.2), channel_id=1, source_target_pairs={{0,1},{1,0},{2,3},{3,2},{4,5},{5,4},{6,7},{7,6},{8,9},{9,8},{10,11... | collective-permute-start | bytes 3145736 | tf_op jit(solution)/shard_map/ppermute | solution.py:233
  5.0 6.2 %collective-permute-start.4 = (bf16[256,256]{1,0:T(8,128)(2,1)S(1)}, bf16[256,256]{1,0:T(8,128)(2,1)S(1)}, u32[]{:S(2)}, u32[]{:S(2)}) collective-permute-start(bf16[256,256]{1,0:T(8,128)(2,1)S(1)} %get-tuple-element.36), channel_id=1, source_target_pairs={{1,3},{3,1},{5,7},{7,5},{9,11},{11,9},{13,15},{15,13},{17,19},{19,... | collective-permute-start | bytes 393224 | tf_op jit(solution)/shard_map/ppermute | solution.py:233
  7.0 18.1 %collective-permute-start.2 = (bf16[272,1152]{1,0:T(8,128)(2,1)S(1)}, bf16[272,1152]{1,0:T(8,128)(2,1)S(1)}, u32[]{:S(2)}, u32[]{:S(2)}) collective-permute-start(bf16[272,1152]{1,0:T(8,128)(2,1)S(1)} %get-tuple-element.28), channel_id=1, source_target_pairs={{2,0},{3,1},{4,2},{5,3},{6,4},{7,5},{8,6},{9,7},{10,8},{11,9},{12,... | collective-permute-start | bytes 1880072 | tf_op jit(solution)/shard_map/ppermute | solution.py:228
  11.3 5.8 %copy-start.1 = (f32[1,5,256,256]{3,2,1,0:T(8,128)S(1)}, f32[1,5,256,256]{3,2,1,0:T(8,128)}, u32[]{:S(2)}) copy-start(f32[1,5,256,256]{3,2,1,0:T(8,128)} %coupling_ref.7) | copy-start | bytes 3932164
  11.5 3.3 %collective-permute-start.5 = (bf16[256,256]{1,0:T(8,128)(2,1)S(1)}, bf16[256,256]{1,0:T(8,128)(2,1)S(1)}, u32[]{:S(2)}, u32[]{:S(2)}) collective-permute-start(bf16[256,256]{1,0:T(8,128)(2,1)S(1)} %get-tuple-element.38), channel_id=1, source_target_pairs={{1,5},{5,1},{9,13},{13,9},{17,21},{21,17},{25,29},{29,25}} | collective-permute-start | bytes 393224 | tf_op jit(solution)/shard_map/ppermute | solution.py:233
  12.3 25.4 %collective-permute-start.1 = (bf16[256,1152]{1,0:T(8,128)(2,1)S(1)}, bf16[256,1152]{1,0:T(8,128)(2,1)S(1)}, u32[]{:S(2)}, u32[]{:S(2)}) collective-permute-start(bf16[256,1152]{1,0:T(8,128)(2,1)S(1)} %get-tuple-element.27), channel_id=1, source_target_pairs={{2,0},{3,1},{4,2},{5,3},{6,4},{7,5},{8,6},{9,7},{10,8},{11,9},{12,... | collective-permute-start | bytes 1769480 | tf_op jit(solution)/shard_map/ppermute | solution.py:228
  15.0 1.3 %collective-permute-start.6 = (bf16[128,256]{1,0:T(8,128)(2,1)S(1)}, bf16[128,256]{1,0:T(8,128)(2,1)S(1)}, u32[]{:S(2)}, u32[]{:S(2)}) collective-permute-start(bf16[128,256]{1,0:T(8,128)(2,1)S(1)} %get-tuple-element.40), channel_id=1, source_target_pairs={{5,13},{13,5},{21,29},{29,21}} | collective-permute-start | bytes 196616 | tf_op jit(solution)/shard_map/ppermute | solution.py:233
  15.7 1.4 %collective-permute-start.8 = (bf16[128,256]{1,0:T(8,128)(2,1)S(1)}, bf16[128,256]{1,0:T(8,128)(2,1)S(1)}, u32[]{:S(2)}, u32[]{:S(2)}) collective-permute-start(bf16[128,256]{1,0:T(8,128)(2,1)S(1)} %get-tuple-element.41), channel_id=1, source_target_pairs={{5,29},{13,21},{21,13},{29,5}} | collective-permute-start | bytes 196616 | tf_op jit(solution)/shard_map/ppermute | solution.py:233
  16.4 0.7 %collective-permute-start.7 = (bf16[128,256]{1,0:T(8,128)(2,1)S(1)}, bf16[128,256]{1,0:T(8,128)(2,1)S(1)}, u32[]{:S(2)}, u32[]{:S(2)}) collective-permute-start(bf16[128,256]{1,0:T(8,128)(2,1)S(1)} %get-tuple-element.41), channel_id=1, source_target_pairs={{5,21},{13,29},{21,5},{29,13}} | collective-permute-start | bytes 196616 | tf_op jit(solution)/shard_map/ppermute | solution.py:233
  17.7 0.7 %collective-permute-start.9 = (bf16[128,256]{1,0:T(8,128)(2,1)S(1)}, bf16[128,256]{1,0:T(8,128)(2,1)S(1)}, u32[]{:S(2)}, u32[]{:S(2)}) collective-permute-start(bf16[128,256]{1,0:T(8,128)(2,1)S(1)} %get-tuple-element.43), channel_id=1, source_target_pairs={{5,1},{13,9},{21,17},{29,25}} | collective-permute-start | bytes 196616 | tf_op jit(solution)/shard_map/ppermute | solution.py:233
  18.8 2.5 %collective-permute-start.10 = (bf16[128,256]{1,0:T(8,128)(2,1)S(1)}, bf16[128,256]{1,0:T(8,128)(2,1)S(1)}, u32[]{:S(2)}, u32[]{:S(2)}) collective-permute-start(bf16[128,256]{1,0:T(8,128)(2,1)S(1)} %get-tuple-element.45), channel_id=1, source_target_pairs={{1,3},{5,7},{9,11},{13,15},{17,19},{21,23},{25,27},{29,31}} | collective-permute-start | bytes 196616 | tf_op jit(solution)/shard_map/ppermute | solution.py:233
  21.6 31.8 %collective-permute-start.11 = (f32[128,256]{1,0:T(8,128)S(1)}, f32[128,256]{1,0:T(8,128)S(1)}, u32[]{:S(2)}, u32[]{:S(2)}) collective-permute-start(f32[128,256]{1,0:T(8,128)S(1)} %shard_map.84.above_ref), channel_id=1, source_target_pairs={{1,0},{3,2},{5,4},{7,6},{9,8},{11,10},{13,12},{15,14},{17,16},{19,... | collective-permute-start | bytes 393224 | tf_op jit(solution)/shard_map/ppermute | solution.py:233
  37.7 15.7 %copy-start.4 = (f32[512,256]{1,0:T(8,128)S(1)}, f32[512,256]{1,0:T(8,128)}, u32[]{:S(2)}) copy-start(f32[512,256]{1,0:T(8,128)} %bases_ref.1) | copy-start | bytes 1572868
  40.5 18.9 %collective-permute-start.12 = (bf16[512,128]{1,0:T(8,128)(2,1)S(1)}, bf16[512,128]{1,0:T(8,128)(2,1)S(1)}, u32[]{:S(2)}, u32[]{:S(2)}) collective-permute-start(bf16[512,128]{1,0:T(8,128)(2,1)S(1)} %get-tuple-element.46), channel_id=1, source_target_pairs={{0,1},{1,0},{2,3},{3,2},{4,5},{5,4},{6,7},{7,6},{8,9},{9,8},{10,11... | collective-permute-start | bytes 393224 | tf_op jit(solution)/shard_map/ppermute | solution.py:233
  47.4 7.9 %collective-permute-start.14 = (bf16[256,128]{1,0:T(8,128)(2,1)S(1)}, bf16[256,128]{1,0:T(8,128)(2,1)S(1)}, u32[]{:S(2)}, u32[]{:S(2)}) collective-permute-start(bf16[256,128]{1,0:T(8,128)(2,1)S(1)} %get-tuple-element.48), channel_id=1, source_target_pairs={{0,2},{1,3},{2,4},{3,5},{4,6},{5,7},{6,8},{7,9},{8,10},{9,11},{10,... | collective-permute-start | bytes 196616 | tf_op jit(solution)/shard_map/ppermute | solution.py:228
  51.5 8.0 %collective-permute-start.13 = (bf16[256,128]{1,0:T(8,128)(2,1)S(1)}, bf16[256,128]{1,0:T(8,128)(2,1)S(1)}, u32[]{:S(2)}, u32[]{:S(2)}) collective-permute-start(bf16[256,128]{1,0:T(8,128)(2,1)S(1)} %get-tuple-element.47), channel_id=1, source_target_pairs={{0,2},{1,3},{2,4},{3,5},{4,6},{5,7},{6,8},{7,9},{8,10},{9,11},{10,... | collective-permute-start | bytes 196616 | tf_op jit(solution)/shard_map/ppermute | solution.py:228

commit v4 on v3

--- a/solution.py
+++ b/solution.py
@@ -16,7 +16,7 @@
 NN = (((1,), (0,)), ((), ()))
 NT = (((1,), (1,)), ((), ()))
 TN = (((0,), (0,)), ((), ()))
-FLAG_ROWS = 16
+FLAG_ROWS = 8
 LIMIT = 16 << 20
 LOAD_LIMIT = 55500000
 SHARED = ((), ((0, 1),), ((0, 1), (1, 0)), ((0, 1), (1, 0), (2, 1)))
@@ -84,28 +84,27 @@
     message_ref[2 * probes :, probes:] = x[rows // 2 :]
 
 
-def pack_kernel(sizes, f_ref, x_ref, list_ref, count_ref, *far_refs):
-    width = f_ref.shape[1]
+def pack_kernel(first, f_ref, x_ref, list_ref, count_ref, far_ref):
+    rows, width = f_ref.shape
     probes = x_ref.shape[1]
-    first = 0
-    for size, far_ref in zip(sizes, far_refs):
-        far_ref[:size, :width] = f_ref[first : first + size]
-        far_ref[:size, width:] = x_ref[first : first + size].astype(BF16)
-        first += size
-    flags = [jnp.full((FLAG_ROWS, probes), member(list_ref, count_ref, offset), F32) for offset in (-2, -1)]
-    flags.append(jnp.zeros((FLAG_ROWS, width - probes), F32))
-    far_refs[0][sizes[0] :] = jnp.concatenate(flags, axis=1).astype(BF16)
-
-
-def up_kernel(level, factor, own_ref, got_ref, transfer_ref, message_ref, next_ref):
-    probes = next_ref.shape[0]
+    size = min(far_ref.shape[0], rows - first)
+    far_ref[:size, :width] = f_ref[first : first + size]
+    far_ref[:size, width:] = x_ref[first : first + size].astype(BF16)
+    if far_ref.shape[0] > size:
+        flags = [jnp.full((FLAG_ROWS, probes), member(list_ref, count_ref, offset), F32) for offset in (-2, -1)]
+        flags.append(jnp.zeros((FLAG_ROWS, width - probes), F32))
+        far_ref[size:] = jnp.concatenate(flags, axis=1).astype(BF16)
+
+
+def up_kernel(level, factor, own_ref, got_ref, transfer_ref, message_ref, *next_refs):
+    probes = message_ref.shape[0] if factor is None else message_ref.shape[0] // 2
     own = own_ref[probes : 2 * probes] if own_ref.shape[0] > probes else own_ref[...]
     skeleton = own + got_ref[probes : 2 * probes].astype(F32)
     message_ref[:probes] = skeleton.astype(message_ref.dtype)
-    moved = factor * dot_wide(skeleton, transfer_ref[0, level], NN)
-    if message_ref.shape[0] > probes:
+    if factor is not None:
+        moved = factor * dot_wide(skeleton, transfer_ref[0, level], NN)
         message_ref[probes:] = moved.astype(message_ref.dtype)
-    next_ref[...] = moved.astype(next_ref.dtype)
+        next_refs[0][...] = moved
 
 
 def bit_of(level):
@@ -118,11 +117,11 @@
     return update if above is None else update + factor * dot_wide(above, transfer, NT)
 
 
-def top_kernel(scale_g, factor, coupling_ref, transfer_ref, got_ref, term_ref, other_ref, own_ref, message_ref):
+def top_kernel(scale_g, factor, coupling_ref, transfer_ref, got_ref, root_ref, own_ref, message_ref):
     depth = transfer_ref.shape[1]
-    sibling = term_ref[...].astype(F32) + other_ref[...].astype(F32)
-    root = descend(scale_g, None, sibling, coupling_ref[0, depth], None, None)
-    out = descend(scale_g, factor, got_ref[...], coupling_ref[0, depth - 1], transfer_ref[0, depth - 1], root)
+    probes = own_ref.shape[0]
+    root = descend(scale_g, None, root_ref[...], coupling_ref[0, depth], None, None)
+    out = descend(scale_g, factor, got_ref[:probes], coupling_ref[0, depth - 1], transfer_ref[0, depth - 1], root)
     own_ref[...] = out
     message_ref[...] = out.astype(BF16)
 
@@ -135,15 +134,22 @@
     message_ref[...] = out.astype(BF16)
 
 
-def node_kernel(scale_g, factor, level, coupling_ref, transfer_ref, got_ref, above_ref, sent_ref, own_ref):
-    probes = own_ref.shape[0]
+def node_kernel(scale_g, factor, level, coupling_ref, transfer_ref, got_ref, above_ref, sent_ref, sib_ref, own_ref, message_ref):
+    probes, rank = own_ref.shape
+    rows = sib_ref.shape[0]
     above = jnp.where(bit_of(level) == 0, above_ref[...], sent_ref[...].astype(F32))
-    own_ref[...] = descend(scale_g, factor, got_ref[:probes], coupling_ref[0, level], transfer_ref[0, level], above)
+    out = descend(scale_g, factor, got_ref[:probes], coupling_ref[0, level], transfer_ref[0, level], above)
+    own_ref[...] = out
+    message_ref[:rows] = sib_ref[...]
+    for part in range(rank // probes):
+        message_ref[rows + part * probes : rows + (part + 1) * probes] = out[:, part * probes : (part + 1) * probes]
 
 
 def down_kernel(scale_g, factor, coupling_ref, transfer_ref, bases_ref, got_ref, above_ref, sent_ref, out_ref):
-    probes = out_ref.shape[1]
-    above = jnp.where(bit_of(0) == 1, above_ref[...], sent_ref[...])
+    rows, probes = out_ref.shape
+    rank = bases_ref.shape[1]
+    sent = [sent_ref[rows + part * probes : rows + (part + 1) * probes] for part in range(rank // probes)]
+    above = jnp.where(bit_of(0) == 1, above_ref[...], jnp.concatenate(sent, axis=1))
     expansion = descend(scale_g, factor, got_ref[:probes], coupling_ref[0, 0], transfer_ref[0, 0], above)
     out_ref[...] = dot_wide(bases_ref[...], expansion, NT)
 
@@ -188,48 +194,64 @@
         sib_ref[...] = jnp.zeros_like(sib_ref)
 
 
-def chunk_kernel(scale, size, f_ref, g_ref, h_ref, flags_ref, near_ref, sib_in_ref, xt_ref, xst_ref, list_ref, count_ref, out_ref, sib_ref, back_ref):
+def chunk_kernel(scale, size, f_ref, g_ref, even_ref, odd_ref, near_ref, sib_in_ref, xt_ref, xst_ref, list_ref, count_ref, *refs):
     even = lax.rem(lax.axis_index("leaf"), 2) == 0
     width = f_ref.shape[1]
     probes = near_ref.shape[1]
-    h = h_ref[:size, :width]
-    xh = h_ref[:size, width:]
-    at = flags_ref.shape[0] - FLAG_ROWS
-    flag2 = flags_ref[at : at + 1, :probes].astype(F32)
-    flag1 = flags_ref[at : at + 1, probes : 2 * probes].astype(F32)
-    parts = tile(f_ref[...], h, scale)
-    out_ref[...] = near_ref[...] + member(list_ref, count_ref, 2) * times(parts, xh)
-    back = flag2 * times_back(parts, xt_ref[...])
+    heads = refs[: len(refs) // 5 * 2]
+    out_ref, sib_ref, *back_refs = refs[len(heads) :]
+    mine = member(list_ref, count_ref, 2)
+
+    def put(back, cross_back):
+        if not heads:
+            back_refs[0][...] = back
+            back_refs[1][...] = jnp.zeros_like(back) if cross_back is None else cross_back
+            return
+        head = heads[0].shape[0]
+        flag2 = even_ref[size : size + 1, :probes].astype(F32)
+        flag1 = even_ref[size : size + 1, probes : 2 * probes].astype(F32)
+        back_refs[0][:head] = (flag2 * heads[0][...] + flag1 * heads[1][...]).astype(BF16)
+        total = flag2 * back
+        back_refs[0][head:] = (total if cross_back is None else total + flag1 * cross_back).astype(BF16)
 
     @pl.when(even)
     def _():
+        h = even_ref[:size, :width]
+        xh = even_ref[:size, width:]
+        parts = tile(f_ref[...], h, scale)
+        out_ref[...] = near_ref[...] + mine * times(parts, xh)
         cross = tile(g_ref[...], h, scale)
-        sib_ref[...] = (sib_in_ref[...] + times(cross, xh)).astype(sib_ref.dtype)
-        back_ref[...] = (back + flag1 * times_back(cross, xst_ref[...])).astype(BF16)
+        sib_ref[...] = sib_in_ref[...] + times(cross, xh)
+        put(times_back(parts, xt_ref[...]), times_back(cross, xst_ref[...]))
 
     @pl.when(jnp.logical_not(even))
     def _():
-        sib_ref[...] = sib_in_ref[...].astype(sib_ref.dtype)
-        back_ref[...] = back.astype(BF16)
-
-
-def final_kernel(near_ref, far_ref, sib_ref, list_ref, count_ref, *refs):
-    out_ref = refs[-1]
+        h = odd_ref[:size, :width]
+        xh = odd_ref[:size, width:]
+        parts = tile(f_ref[...], h, scale)
+        out_ref[...] = near_ref[...] + mine * times(parts, xh)
+        sib_ref[...] = sib_in_ref[...]
+        put(times_back(parts, xt_ref[...]), None)
+
+
+def final_kernel(near_ref, far_ref, sib_ref, back_ref, list_ref, count_ref, out_ref):
+    rows = out_ref.shape[0]
     flag = member(list_ref, count_ref, 1)
-    at = 0
-    for back_ref in refs[:-1]:
-        rows = slice(at, at + back_ref.shape[0])
-        out_ref[rows] = near_ref[rows] + far_ref[rows] + flag * sib_ref[rows].astype(F32) + back_ref[...].astype(F32)
-        at += back_ref.shape[0]
-
-
-def moved(array, by):
+    out_ref[...] = near_ref[...] + far_ref[...] + flag * sib_ref[:rows] + back_ref[...].astype(F32)
+
+
+def sender(index, bits):
+    return all(index >> at & 1 == bit for at, bit in bits)
+
+
+def moved(array, by, bits=()):
     peers = lax.axis_size("leaf")
-    return lax.ppermute(array, "leaf", [(i, i + by) for i in range(peers) if 0 <= i + by < peers])
+    pairs = [(i, i + by) for i in range(peers) if 0 <= i + by < peers and sender(i, bits)]
+    return lax.ppermute(array, "leaf", pairs)
 
 
 def across(array, distance, bits=()):
-    senders = [i for i in range(lax.axis_size("leaf")) if all(i >> at & 1 == bit for at, bit in bits)]
+    senders = [i for i in range(lax.axis_size("leaf")) if sender(i, bits)]
     return lax.ppermute(array, "leaf", [(i, i ^ distance) for i in senders])
 
 
@@ -264,28 +286,30 @@
         limit=LOAD_LIMIT,
     )
     gots = [partner(message, 0)]
-    packed = call(
-        functools.partial(pack_kernel, sizes),
-        [shape((size + (0 if i else FLAG_ROWS), width + count), BF16) for i, size in enumerate(sizes)],
-        [VMEM, VMEM, SMEM, SMEM],
-        1000,
-        features, probes, near_list, near_count,
-    )
-    far = [moved(part, -2) for part in packed]
+    packed = []
+    for at in range(2):
+        packed += call(
+            functools.partial(pack_kernel, sizes[0] * at),
+            [shape((sizes[at] + FLAG_ROWS * at, width + count), BF16)],
+            [VMEM, VMEM, SMEM, SMEM],
+            1000,
+            features, probes, near_list, near_count,
+        )
+    far_even = moved(packed[0], -2, ((0, 0),))
+    far_odd = moved(packed[0], -2, ((0, 1),))
+    far_last = moved(packed[1], -2)
     own = [message]
-    top = depth - 1
-    for level in range(1, top + 1):
+    for level in range(1, depth + 1):
+        last = level == depth
+        outs = [shape((count if last else 2 * count, rank), BF16), shape((count, rank), F32)]
         message, *own = call(
-            functools.partial(up_kernel, level, factors[level]),
-            [shape((2 * count, rank), BF16), shape((count, rank), F32)] if level < top else [shape((count, rank), BF16)] * 2,
+            functools.partial(up_kernel, level, None if last else factors[level]),
+            outs[:1] if last else outs,
             [VMEM] * 3,
             6 * rank * rank * count,
             *own, gots[-1], transfers,
         )
-        if level < top:
-            gots.append(partner(message, level, SHARED[level]))
-    gots.append(partner(message, top, SHARED[top]))
-    terms = [across(own[0], (1 << top + 1) + extra, SHARED[top]) for extra in (0, 1 << top)]
+        gots.append(partner(message, level, SHARED[min(level, 3)]))
 
     tile_flops = 2 * rows * rows * (width + 4 * count)
     (near,) = call(
@@ -302,25 +326,24 @@
         tile_flops,
         features, sib_features, near, probes, gots[0], near_list, near_count,
     )
-    backs = []
-    for stage, (size, part) in enumerate(zip(sizes, far)):
-        last = stage == len(sizes) - 1
-        near, sib, back = call(
+    heads = []
+    for at, (size, parts) in enumerate(zip(sizes, ((far_even, far_odd), (far_last, far_last)))):
+        back_shapes = [shape((size, count), F32)] * 2 if at == 0 else [shape((rows, count), BF16)]
+        near, sib, *heads = call(
             functools.partial(chunk_kernel, scale, size),
-            [shape((rows, count), F32), shape((rows, count), BF16 if last else F32), shape((size, count), BF16)],
-            [VMEM] * 8 + [SMEM] * 2,
+            [shape((rows, count), F32), shape((rows, count), F32), *back_shapes],
+            [VMEM] * 8 + [SMEM] * 2 + [VMEM] * len(heads),
             tile_flops * 2 * size // rows,
-            features, sib_features, part, far[0], near, sib, xt, xst, near_list, near_count,
+            features, sib_features, *parts, near, sib, xt, xst, near_list, near_count, *heads,
         )
-        backs.append(moved(back, 2))
-    sib_got = partner(sib, 0)
+    back = moved(heads[0], 2)
     product_flops = 6 * count * rank * rank
     e3, e3_message = call(
-        functools.partial(top_kernel, scale_g, factors[top]),
+        functools.partial(top_kernel, scale_g, factors[depth - 1]),
         [shape((count, rank), F32), shape((count, rank), BF16)],
-        [VMEM] * 5,
+        [VMEM] * 4,
         3 * product_flops,
-        couplings, transfers, gots[top], *terms,
+        couplings, transfers, gots[depth - 1], gots[depth],
     )
     e3_sent = partner(e3_message, 2, SHARED[3])
     e2, e2_message = call(
@@ -331,27 +354,27 @@
         couplings, transfers, gots[2], e3, e3_sent,
     )
     e2_sent = partner(e2_message, 1, SHARED[2])
-    (e1,) = call(
+    e1, sib_message = call(
         functools.partial(node_kernel, scale_g, factors[1], 1),
-        [shape((count, rank), F32)],
-        [VMEM] * 5,
+        [shape((count, rank), F32), shape((rows + rank, count), F32)],
+        [VMEM] * 6,
         2 * product_flops,
-        couplings, transfers, gots[1], e2, e2_sent,
-    )
-    e1_sent = partner(e1, 0, SHARED[1])
+        couplings, transfers, gots[1], e2, e2_sent, sib,
+    )
+    sib_got = partner(sib_message, 0)
     (far_sum,) = call(
         functools.partial(down_kernel, scale_g, factors[0]),
         [shape((rows, count), F32)],
         [VMEM] * 6,
         2 * product_flops + 6 * rows * rank * count,
-        couplings, transfers, bases, gots[0], e1, e1_sent,
+        couplings, transfers, bases, gots[0], e1, sib_got,
     )
     (out,) = call(
         final_kernel,
         [shape((rows, count), F32)],
-        [VMEM] * 3 + [SMEM] * 2 + [VMEM] * len(backs),
+        [VMEM] * 4 + [SMEM] * 2,
         6 * rows * count,
-        near, far_sum, sib_got, near_list, near_count, *backs,
+        near, far_sum, sib_got, back, near_list, near_count,
     )
     return out
 

time: 61.2 us -> 74 us (1.21)
  starting transfers between devices: 26.2 us -> 40.1 us
  waiting for transfers between devices: 17.8 us -> 16.8 us
    ppermute x11 -> x9, starting transfers between devices: 13.5 us -> 29.2 us  [across(): return lax.ppermute(array, 'leaf', [(i, i ^ distance) for i in senders])]
    ppermute x4, starting transfers between devices: 12.7 us -> 10.9 us  [moved(): return lax.ppermute(array, 'leaf', pairs)]
    ppermute x11 -> x9, waiting for transfers between devices: 1.42 us -> 0.02 us  [across(): return lax.ppermute(array, 'leaf', [(i, i ^ distance) for i in senders])]
    pallas_call x14 -> x16, Pallas kernels: 14.7 us -> 14.6 us  [call(): pl.pallas_call(kernel, out_shape=outs, in_specs=specs, out_specs=[VMEM] *...]
  transfers between devices with their start and end apart: 15 -> 13, of which waited for: 5 -> 3; matrix products, arithmetic and copies ran while one was open for 0% -> 0% of each run, Pallas kernels for 19% -> 18%
where the time goes in v4:
time: 74 us; the launch traced here: 73.6 us
  starting transfers between devices  40.1 us (54%)
  waiting for transfers between devices  16.8 us (23%)
  Pallas kernels  14.6 us (20%)
  local copies, waits for them, and re-layouts  1.06 us (1%)
  between operations  0.98 us (1%)
    ppermute x9, starting transfers between devices, across(): return lax.ppermute(array, 'leaf', [(i, i ^ distance) for i in senders])  29.2 us
    ppermute x4, waiting for transfers between devices, moved(): return lax.ppermute(array, 'leaf', pairs)  16.8 us
    pallas_call x16, Pallas kernels, call(): pl.pallas_call(kernel, out_shape=outs, in_specs=specs, out_specs=[VMEM] *...  14.6 us
    ppermute x4, starting transfers between devices, moved(): return lax.ppermute(array, 'leaf', pairs)  10.9 us
  transfers between devices with their start and end apart: 13, of which 3 were waited for; matrix products, arithmetic and copies ran while one was open for 0% of the time, Pallas kernels for 18%

profile of v4, /device:TPU:8, one launch (start us, length us, event | category | flops | bytes accessed | tf_op | source)
XLA Modules:
  0.0 73.6 jit_solution(16247303198619129880)
XLA Ops:
  0.0 1.0 %copy-done.3 = f32[512,128]{1,0:T(8,128)S(1)} copy-done((f32[512,128]{1,0:T(8,128)S(1)}, f32[512,128]{1,0:T(8,128)}, u32[]{:S(2)}) %copy-start.3) | copy-done | bytes 262168
  1.0 1.7 %shard_map.76.own_ref = f32[512,256]{1,0:T(8,128)S(1)} custom-call(f32[512,256]{1,0:T(8,128)} %bases_ref.1, f32[512,128]{1,0:T(8,128)S(1)} %copy-done.3, f32[1,4,256,256]{3,2,1,0:T(8,128)} %transfer_ref.15), custom_call_target="tpu_custom_call" | custom-call | flops 100663296 | bytes 2359296 | tf_op jit(solution)/shard_map/pallas_call | solution.py:57
  2.8 0.0 copy-start
  2.8 0.5 collective-permute-start.4
  3.9 0.6 shard_map.74
  4.5 4.2 %collective-permute-start.2 = (bf16[256,1152]{1,0:T(8,128)(2,1)S(1)}, bf16[256,1152]{1,0:T(8,128)(2,1)S(1)}, u32[]{:S(2)}, u32[]{:S(2)}) collective-permute-start(bf16[256,1152]{1,0:T(8,128)(2,1)S(1)} %shard_map.74), channel_id=1, source_target_pairs={{2,0},{4,2},{6,4},{8,6},{10,8},{12,10},{14,12},{16,14},{18,16},{20... | collective-permute-start | bytes 1769480 | tf_op jit(solution)/shard_map/ppermute | solution.py:250
  8.8 0.7 collective-permute-start.3
  9.5 0.2 shard_map.80
  9.7 0.7 collective-permute-start.5
  10.4 0.6 shard_map.73
  11.0 2.4 %collective-permute-start.1 = (bf16[264,1152]{1,0:T(8,128)(2,1)S(1)}, bf16[264,1152]{1,0:T(8,128)(2,1)S(1)}, u32[]{:S(2)}, u32[]{:S(2)}) collective-permute-start(bf16[264,1152]{1,0:T(8,128)(2,1)S(1)} %shard_map.73), channel_id=1, source_target_pairs={{2,0},{3,1},{4,2},{5,3},{6,4},{7,5},{8,6},{9,7},{10,8},{11,9},{12,... | collective-permute-start | bytes 1824776 | tf_op jit(solution)/shard_map/ppermute | solution.py:250
  13.5 0.2 shard_map.81
  13.7 0.7 collective-permute-start.6
  14.4 0.2 shard_map.82
  14.6 0.7 collective-permute-start.7
  15.3 0.8 %collective-permute-start.8 = (bf16[128,256]{1,0:T(8,128)(2,1)S(1)}, bf16[128,256]{1,0:T(8,128)(2,1)S(1)}, u32[]{:S(2)}, u32[]{:S(2)}) collective-permute-start(bf16[128,256]{1,0:T(8,128)(2,1)S(1)} %shard_map.83), channel_id=1, source_target_pairs={{5,21},{13,29},{21,5},{29,13}} | collective-permute-start | bytes 196616 | tf_op jit(solution)/shard_map/ppermute | solution.py:255
  16.1 1.8 %shard_map.75.near_ref = f32[512,128]{1,0:T(8,128)S(1)} custom-call(bf16[512,1024]{1,0:T(8,128)(2,1)S(1)} %copy-done.1, f32[512,128]{1,0:T(8,128)S(1)} %copy-done.3), custom_call_target="tpu_custom_call" | custom-call | flops 805306368 | bytes 1572864 | tf_op jit(solution)/shard_map/pallas_call | solution.py:57
  17.9 0.5 shard_map.84
  18.4 0.7 collective-permute-start.9
  19.1 0.7 shard_map.77
  19.9 2.8 %collective-permute-done.2.even_ref = bf16[256,1152]{1,0:T(8,128)(2,1)S(1)} collective-permute-done((bf16[256,1152]{1,0:T(8,128)(2,1)S(1)}, bf16[256,1152]{1,0:T(8,128)(2,1)S(1)}, u32[]{:S(2)}, u32[]{:S(2)}) %collective-permute-start.2) | collective-permute-done | bytes 589856 | tf_op jit(solution)/shard_map/ppermute | solution.py:250
  22.6 2.6 %shard_map.78 = (f32[512,128]{1,0:T(8,128)S(1)}, f32[512,128]{1,0:T(8,128)S(1)}, f32[256,128]{1,0:T(8,128)S(1)}, f32[256,128]{1,0:T(8,128)S(1)}) custom-call(bf16[512,1024]{1,0:T(8,128)(2,1)S(1)} %copy-done.1, bf16[512,1024]{1,0:T(8,128)(2,1)S(1)} %collective-permute-done.g_ref, bf16[256,1152]{1,0:T(8,128)(2,1)S(1)} %collective-permute-done.2.even_ref, ...), custom_call_target="tpu_custom_call" | custom-call | flops 805306368 | bytes 4849684 | tf_op jit(solution)/shard_map/pallas_call | solution.py:57
  25.2 0.4 shard_map.85
  25.6 0.7 collective-permute-start.10
  26.2 9.4 %collective-permute-done.1.even_ref.odd_ref = bf16[264,1152]{1,0:T(8,128)(2,1)S(1)} collective-permute-done((bf16[264,1152]{1,0:T(8,128)(2,1)S(1)}, bf16[264,1152]{1,0:T(8,128)(2,1)S(1)}, u32[]{:S(2)}, u32[]{:S(2)}) %collective-permute-start.1) | collective-permute-done | bytes 608288 | tf_op jit(solution)/shard_map/ppermute | solution.py:250
  35.6 2.6 %shard_map.79 = (f32[512,128]{1,0:T(8,128)S(1)}, f32[512,128]{1,0:T(8,128)S(1)}, bf16[512,128]{1,0:T(8,128)(2,1)S(1)}) custom-call(bf16[512,1024]{1,0:T(8,128)(2,1)S(1)} %copy-done.1, bf16[512,1024]{1,0:T(8,128)(2,1)S(1)} %collective-permute-done.g_ref, bf16[264,1152]{1,0:T(8,128)(2,1)S(1)} %collective-permute-done.1.even_ref.odd_ref, ...), custom_call_target="tpu_custom_call" | custom-call | flops 805306368 | bytes 5017620 | tf_op jit(solution)/shard_map/pallas_call | solution.py:57
  38.2 0.4 shard_map.86
  38.6 24.6 %collective-permute-start.11 = (f32[768,128]{1,0:T(8,128)S(1)}, f32[768,128]{1,0:T(8,128)S(1)}, u32[]{:S(2)}, u32[]{:S(2)}) collective-permute-start(f32[768,128]{1,0:T(8,128)S(1)} %get-tuple-element.49), channel_id=1, source_target_pairs={{0,1},{1,0},{2,3},{3,2},{4,5},{5,4},{6,7},{7,6},{8,9},{9,8},{10,11... | collective-permute-start | bytes 1179656 | tf_op jit(solution)/shard_map/ppermute | solution.py:255
  63.2 3.5 %collective-permute-start.12 = (bf16[512,128]{1,0:T(8,128)(2,1)S(1)}, bf16[512,128]{1,0:T(8,128)(2,1)S(1)}, u32[]{:S(2)}, u32[]{:S(2)}) collective-permute-start(bf16[512,128]{1,0:T(8,128)(2,1)S(1)} %get-tuple-element.50), channel_id=1, source_target_pairs={{0,2},{1,3},{2,4},{3,5},{4,6},{5,7},{6,8},{7,9},{8,10},{9,11},{10,... | collective-permute-start | bytes 393224 | tf_op jit(solution)/shard_map/ppermute | solution.py:250
  66.8 0.8 %shard_map.87.far_ref = f32[512,128]{1,0:T(8,128)S(1)} custom-call(f32[1,5,256,256]{3,2,1,0:T(8,128)S(1)} %copy-done.2, f32[1,4,256,256]{3,2,1,0:T(8,128)S(1)} %copy-done, f32[512,256]{1,0:T(8,128)S(1)} %copy-done.4, f32[512,256]{1,0:T(8,128)S(1)} %collective-permute-done.4.got_ref, f32[128,256]{1,0:T(8,128)S(1)} %get-tuple-element.48.above_ref, ...), custom_call_target="tpu_custom_call" | custom-call | flops 201326592 | bytes 4194304 | tf_op jit(solution)/shard_map/pallas_call | solution.py:57
  67.6 4.7 %collective-permute-done.12.back_ref = bf16[512,128]{1,0:T(8,128)(2,1)S(1)} collective-permute-done((bf16[512,128]{1,0:T(8,128)(2,1)S(1)}, bf16[512,128]{1,0:T(8,128)(2,1)S(1)}, u32[]{:S(2)}, u32[]{:S(2)}) %collective-permute-start.12) | collective-permute-done | bytes 131104 | tf_op jit(solution)/shard_map/ppermute | solution.py:250
  72.3 1.3 %shard_map.88 = f32[512,128]{1,0:T(8,128)} custom-call(f32[512,128]{1,0:T(8,128)S(1)} %get-tuple-element.36.near_ref, f32[512,128]{1,0:T(8,128)S(1)} %shard_map.87.far_ref, f32[768,128]{1,0:T(8,128)S(1)} %collective-permute-done.11.sent_ref.sib_ref, bf16[512,128]{1,0:T(8,128)(2,1)S(1)} %collective-permute-done.12.back_ref, s32[1,4]{1,0:T(1,128)S(1)} %copy-done.5, ...), custom_call_target="tpu_custom_call" | custom-call | flops 393216 | bytes 1310740 | tf_op jit(solution)/shard_map/pallas_call | solution.py:57
  (22 shorter events, 0.1 us)
Async XLA Ops:
  0.0 3.9 %copy-start.1 = (bf16[512,1024]{1,0:T(8,128)(2,1)S(1)}, bf16[512,1024]{1,0:T(8,128)(2,1)}, u32[]{:S(2)}) copy-start(bf16[512,1024]{1,0:T(8,128)(2,1)} %f_ref.11) | copy-start | bytes 3145732
  0.0 19.1 %collective-permute-start = (bf16[512,1024]{1,0:T(8,128)(2,1)}, bf16[512,1024]{1,0:T(8,128)(2,1)S(1)}, u32[]{:S(2)}, u32[]{:S(2)}) collective-permute-start(bf16[512,1024]{1,0:T(8,128)(2,1)} %f_ref.11), channel_id=1, source_target_pairs={{0,1},{1,0},{2,3},{3,2},{4,5},{5,4},{6,7},{7,6},{8,9},{9,8},{10,11... | collective-permute-start | bytes 3145736 | tf_op jit(solution)/shard_map/ppermute | solution.py:255
  0.0 1.0 %copy-start.3 = (f32[512,128]{1,0:T(8,128)S(1)}, f32[512,128]{1,0:T(8,128)}, u32[]{:S(2)}) copy-start(f32[512,128]{1,0:T(8,128)} %x_ref.7) | copy-start | bytes 786436
  1.0 2.9 %copy-start.5 = (s32[1,4]{1,0:T(1,128)S(1)}, s32[1,4]{1,0:T(1,128)}, u32[]{:S(2)}) copy-start(s32[1,4]{1,0:T(1,128)} %list_ref.11) | copy-start | bytes 52
  2.8 6.7 %copy-start = (f32[1,4,256,256]{3,2,1,0:T(8,128)S(1)}, f32[1,4,256,256]{3,2,1,0:T(8,128)}, u32[]{:S(2)}) copy-start(f32[1,4,256,256]{3,2,1,0:T(8,128)} %transfer_ref.15) | copy-start | bytes 3145732
  2.8 6.7 %collective-permute-start.4 = (f32[512,256]{1,0:T(8,128)S(1)}, f32[512,256]{1,0:T(8,128)S(1)}, u32[]{:S(2)}, u32[]{:S(2)}) collective-permute-start(f32[512,256]{1,0:T(8,128)S(1)} %shard_map.76.own_ref), channel_id=1, source_target_pairs={{0,1},{1,0},{2,3},{3,2},{4,5},{5,4},{6,7},{7,6},{8,9},{9,8},{10,11... | collective-permute-start | bytes 1572872 | tf_op jit(solution)/shard_map/ppermute | solution.py:255
  4.5 18.1 %collective-permute-start.2 = (bf16[256,1152]{1,0:T(8,128)(2,1)S(1)}, bf16[256,1152]{1,0:T(8,128)(2,1)S(1)}, u32[]{:S(2)}, u32[]{:S(2)}) collective-permute-start(bf16[256,1152]{1,0:T(8,128)(2,1)S(1)} %shard_map.74), channel_id=1, source_target_pairs={{2,0},{4,2},{6,4},{8,6},{10,8},{12,10},{14,12},{16,14},{18,16},{20... | collective-permute-start | bytes 1769480 | tf_op jit(solution)/shard_map/ppermute | solution.py:250
  8.8 13.8 %collective-permute-start.3 = (bf16[256,1152]{1,0:T(8,128)(2,1)S(1)}, bf16[256,1152]{1,0:T(8,128)(2,1)S(1)}, u32[]{:S(2)}, u32[]{:S(2)}) collective-permute-start(bf16[256,1152]{1,0:T(8,128)(2,1)S(1)} %shard_map.74), channel_id=1, source_target_pairs={{3,1},{5,3},{7,5},{9,7},{11,9},{13,11},{15,13},{17,15},{19,17},{21... | collective-permute-start | bytes 1769480 | tf_op jit(solution)/shard_map/ppermute | solution.py:250
  9.7 3.7 %collective-permute-start.5 = (bf16[256,256]{1,0:T(8,128)(2,1)S(1)}, bf16[256,256]{1,0:T(8,128)(2,1)S(1)}, u32[]{:S(2)}, u32[]{:S(2)}) collective-permute-start(bf16[256,256]{1,0:T(8,128)(2,1)S(1)} %get-tuple-element.37), channel_id=1, source_target_pairs={{1,3},{3,1},{5,7},{7,5},{9,11},{11,9},{13,15},{15,13},{17,19},{19,... | collective-permute-start | bytes 393224 | tf_op jit(solution)/shard_map/ppermute | solution.py:255
  11.0 24.7 %collective-permute-start.1 = (bf16[264,1152]{1,0:T(8,128)(2,1)S(1)}, bf16[264,1152]{1,0:T(8,128)(2,1)S(1)}, u32[]{:S(2)}, u32[]{:S(2)}) collective-permute-start(bf16[264,1152]{1,0:T(8,128)(2,1)S(1)} %shard_map.73), channel_id=1, source_target_pairs={{2,0},{3,1},{4,2},{5,3},{6,4},{7,5},{8,6},{9,7},{10,8},{11,9},{12,... | collective-permute-start | bytes 1824776 | tf_op jit(solution)/shard_map/ppermute | solution.py:250
  13.7 0.7 collective-permute-start.6
  14.6 0.7 collective-permute-start.7
  15.3 2.6 %copy-start.2 = (f32[1,5,256,256]{3,2,1,0:T(8,128)S(1)}, f32[1,5,256,256]{3,2,1,0:T(8,128)}, u32[]{:S(2)}) copy-start(f32[1,5,256,256]{3,2,1,0:T(8,128)} %coupling_ref.7) | copy-start | bytes 3932164
  15.3 2.6 %collective-permute-start.8 = (bf16[128,256]{1,0:T(8,128)(2,1)S(1)}, bf16[128,256]{1,0:T(8,128)(2,1)S(1)}, u32[]{:S(2)}, u32[]{:S(2)}) collective-permute-start(bf16[128,256]{1,0:T(8,128)(2,1)S(1)} %shard_map.83), channel_id=1, source_target_pairs={{5,21},{13,29},{21,5},{29,13}} | collective-permute-start | bytes 196616 | tf_op jit(solution)/shard_map/ppermute | solution.py:255
  18.4 6.7 %collective-permute-start.9 = (bf16[128,256]{1,0:T(8,128)(2,1)S(1)}, bf16[128,256]{1,0:T(8,128)(2,1)S(1)}, u32[]{:S(2)}, u32[]{:S(2)}) collective-permute-start(bf16[128,256]{1,0:T(8,128)(2,1)S(1)} %get-tuple-element.44), channel_id=1, source_target_pairs={{5,1},{13,9},{21,17},{29,25}} | collective-permute-start | bytes 196616 | tf_op jit(solution)/shard_map/ppermute | solution.py:255
  25.6 12.6 %collective-permute-start.10 = (bf16[128,256]{1,0:T(8,128)(2,1)S(1)}, bf16[128,256]{1,0:T(8,128)(2,1)S(1)}, u32[]{:S(2)}, u32[]{:S(2)}) collective-permute-start(bf16[128,256]{1,0:T(8,128)(2,1)S(1)} %get-tuple-element.46), channel_id=1, source_target_pairs={{1,3},{5,7},{9,11},{13,15},{17,19},{21,23},{25,27},{29,31}} | collective-permute-start | bytes 196616 | tf_op jit(solution)/shard_map/ppermute | solution.py:255
  38.2 28.5 %copy-start.4 = (f32[512,256]{1,0:T(8,128)S(1)}, f32[512,256]{1,0:T(8,128)}, u32[]{:S(2)}) copy-start(f32[512,256]{1,0:T(8,128)} %bases_ref.1) | copy-start | bytes 1572868
  38.6 28.1 %collective-permute-start.11 = (f32[768,128]{1,0:T(8,128)S(1)}, f32[768,128]{1,0:T(8,128)S(1)}, u32[]{:S(2)}, u32[]{:S(2)}) collective-permute-start(f32[768,128]{1,0:T(8,128)S(1)} %get-tuple-element.49), channel_id=1, source_target_pairs={{0,1},{1,0},{2,3},{3,2},{4,5},{5,4},{6,7},{7,6},{8,9},{9,8},{10,11... | collective-permute-start | bytes 1179656 | tf_op jit(solution)/shard_map/ppermute | solution.py:255
  63.2 9.1 %collective-permute-start.12 = (bf16[512,128]{1,0:T(8,128)(2,1)S(1)}, bf16[512,128]{1,0:T(8,128)(2,1)S(1)}, u32[]{:S(2)}, u32[]{:S(2)}) collective-permute-start(bf16[512,128]{1,0:T(8,128)(2,1)S(1)} %get-tuple-element.50), channel_id=1, source_target_pairs={{0,2},{1,3},{2,4},{3,5},{4,6},{5,7},{6,8},{7,9},{8,10},{9,11},{10,... | collective-permute-start | bytes 393224 | tf_op jit(solution)/shard_map/ppermute | solution.py:250

commit v5 on v4

--- a/solution.py
+++ b/solution.py
@@ -18,7 +18,7 @@
 TN = (((0,), (0,)), ((), ()))
 FLAG_ROWS = 8
 LIMIT = 16 << 20
-LOAD_LIMIT = 55500000
+LOAD_LIMIT = 55400000
 SHARED = ((), ((0, 1),), ((0, 1), (1, 0)), ((0, 1), (1, 0), (2, 1)))
 
 
@@ -46,7 +46,7 @@
     index = lax.axis_index("leaf")
     found = jnp.float32(0.0)
     for slot in range(list_ref.shape[1]):
-        hit = (list_ref[0, slot] == index + offset) & (slot < count_ref[0])
+        hit = (list_ref[0, slot] == index + offset) & (slot < count_ref[0, 0])
         found = jnp.where(hit, jnp.float32(1.0), found)
     return found
 
@@ -65,16 +65,18 @@
     )(*args)
 
 
-def leaf_kernel(c1, bases_hbm, x_hbm, transfers_hbm, message_ref, bases_ref, x_ref, transfer_ref, sems):
+def load_kernel(bases_hbm, transfers_hbm, bases_ref, transfer_ref, sems):
     copies = [
-        pltpu.make_async_copy(x_hbm, x_ref, sems.at[0]),
-        pltpu.make_async_copy(bases_hbm, bases_ref, sems.at[1]),
-        pltpu.make_async_copy(transfers_hbm.at[0, 0], transfer_ref, sems.at[2]),
+        pltpu.make_async_copy(bases_hbm, bases_ref, sems.at[0]),
+        pltpu.make_async_copy(transfers_hbm.at[0, 0], transfer_ref, sems.at[1]),
     ]
     for copy in copies:
         copy.start()
     for copy in copies:
         copy.wait()
+
+
+def leaf_kernel(c1, bases_ref, x_ref, transfer_ref, message_ref):
     x = x_ref[...]
     rows, probes = x.shape
     skeleton = dot_wide(x, bases_ref[...], TN)
@@ -84,13 +86,15 @@
     message_ref[2 * probes :, probes:] = x[rows // 2 :]
 
 
-def pack_kernel(first, f_ref, x_ref, list_ref, count_ref, far_ref):
+def pack_kernel(first, f_ref, x_ref, *refs):
+    far_ref = refs[-1]
     rows, width = f_ref.shape
     probes = x_ref.shape[1]
     size = min(far_ref.shape[0], rows - first)
     far_ref[:size, :width] = f_ref[first : first + size]
     far_ref[:size, width:] = x_ref[first : first + size].astype(BF16)
     if far_ref.shape[0] > size:
+        list_ref, count_ref = refs[:2]
         flags = [jnp.full((FLAG_ROWS, probes), member(list_ref, count_ref, offset), F32) for offset in (-2, -1)]
         flags.append(jnp.zeros((FLAG_ROWS, width - probes), F32))
         far_ref[size:] = jnp.concatenate(flags, axis=1).astype(BF16)
@@ -134,22 +138,28 @@
     message_ref[...] = out.astype(BF16)
 
 
-def node_kernel(scale_g, factor, level, coupling_ref, transfer_ref, got_ref, above_ref, sent_ref, sib_ref, own_ref, message_ref):
+def node_kernel(scale_g, factor, level, coupling_ref, transfer_ref, got_ref, above_ref, sent_ref, cross_ref, pair_ref, own_ref, message_ref):
     probes, rank = own_ref.shape
-    rows = sib_ref.shape[0]
+    at = 2 * cross_ref.shape[0]
+    message_ref[: at // 2] = cross_ref[...]
+    message_ref[at // 2 : at] = pair_ref[...]
     above = jnp.where(bit_of(level) == 0, above_ref[...], sent_ref[...].astype(F32))
     out = descend(scale_g, factor, got_ref[:probes], coupling_ref[0, level], transfer_ref[0, level], above)
     own_ref[...] = out
-    message_ref[:rows] = sib_ref[...]
-    for part in range(rank // probes):
-        message_ref[rows + part * probes : rows + (part + 1) * probes] = out[:, part * probes : (part + 1) * probes]
+    for part in halves(out):
+        for first in range(0, rank, probes):
+            message_ref[at : at + probes] = part[:, first : first + probes]
+            at += probes
 
 
 def down_kernel(scale_g, factor, coupling_ref, transfer_ref, bases_ref, got_ref, above_ref, sent_ref, out_ref):
     rows, probes = out_ref.shape
     rank = bases_ref.shape[1]
-    sent = [sent_ref[rows + part * probes : rows + (part + 1) * probes] for part in range(rank // probes)]
-    above = jnp.where(bit_of(0) == 1, above_ref[...], jnp.concatenate(sent, axis=1))
+    high, low = [
+        jnp.concatenate([sent_ref[at + first : at + first + probes] for first in range(0, rank, probes)], axis=1).astype(F32)
+        for at in (2 * rows, 2 * rows + rank)
+    ]
+    above = jnp.where(bit_of(0) == 1, above_ref[...], high + low)
     expansion = descend(scale_g, factor, got_ref[:probes], coupling_ref[0, 0], transfer_ref[0, 0], above)
     out_ref[...] = dot_wide(bases_ref[...], expansion, NT)
 
@@ -173,32 +183,32 @@
     return (dot(xt16, parts[0], NN) + dot(xt16, parts[1], NN)).T
 
 
-def pair_kernel(scale, f_ref, g_ref, near_ref, x_ref, got_ref, list_ref, count_ref, out_ref, sib_ref, xt_ref, xst_ref):
-    odd = lax.rem(lax.axis_index("leaf"), 2) == 1
+def pair_kernel(scale, f_ref, g_ref, near_ref, x_ref, got_ref, list_ref, count_ref, out_ref, pair_ref, xt_ref, xst_ref):
+    even = bit_of(0) == 0
     rows, probes = near_ref.shape
     xt_ref[...] = x_ref[...].T.astype(BF16)
-    for half in range(2):
-        part = got_ref[2 * probes :, half * probes : (half + 1) * probes]
+    halves_of = [got_ref[2 * probes :, half * probes : (half + 1) * probes] for half in range(2)]
+    for half, part in enumerate(halves_of):
         xst_ref[:, half * (rows // 2) : (half + 1) * (rows // 2)] = part.T.astype(BF16)
 
-    @pl.when(odd)
+    @pl.when(even)
     def _():
-        parts = tile(g_ref[...], f_ref[...], scale)
-        sib_ref[...] = times(parts, x_ref[...].astype(BF16))
-        flag = member(list_ref, count_ref, -1)
-        out_ref[...] = near_ref[...] + flag * times_back(parts, xst_ref[...])
-
-    @pl.when(jnp.logical_not(odd))
+        parts = tile(f_ref[...], g_ref[...], scale)
+        flag = member(list_ref, count_ref, 1)
+        out_ref[...] = near_ref[...] + flag * times(parts, jnp.concatenate(halves_of, axis=0).astype(BF16))
+        pair_ref[...] = times_back(parts, xt_ref[...]).astype(BF16)
+
+    @pl.when(jnp.logical_not(even))
     def _():
         out_ref[...] = near_ref[...]
-        sib_ref[...] = jnp.zeros_like(sib_ref)
-
-
-def chunk_kernel(scale, size, f_ref, g_ref, even_ref, odd_ref, near_ref, sib_in_ref, xt_ref, xst_ref, list_ref, count_ref, *refs):
+        pair_ref[...] = jnp.zeros_like(pair_ref)
+
+
+def chunk_kernel(scale, size, f_ref, g_ref, far_ref, near_ref, xt_ref, xst_ref, list_ref, count_ref, *refs):
     even = lax.rem(lax.axis_index("leaf"), 2) == 0
     width = f_ref.shape[1]
     probes = near_ref.shape[1]
-    heads = refs[: len(refs) // 5 * 2]
+    heads = refs[: len(refs) // 5 * 3]
     out_ref, sib_ref, *back_refs = refs[len(heads) :]
     mine = member(list_ref, count_ref, 2)
 
@@ -207,47 +217,52 @@
             back_refs[0][...] = back
             back_refs[1][...] = jnp.zeros_like(back) if cross_back is None else cross_back
             return
-        head = heads[0].shape[0]
-        flag2 = even_ref[size : size + 1, :probes].astype(F32)
-        flag1 = even_ref[size : size + 1, probes : 2 * probes].astype(F32)
-        back_refs[0][:head] = (flag2 * heads[0][...] + flag1 * heads[1][...]).astype(BF16)
+        head = heads[1].shape[0]
+        flag2 = far_ref[size : size + 1, :probes].astype(F32)
+        flag1 = far_ref[size : size + 1, probes : 2 * probes].astype(F32)
+        back_refs[0][:head] = (flag2 * heads[1][...] + flag1 * heads[2][...]).astype(BF16)
         total = flag2 * back
         back_refs[0][head:] = (total if cross_back is None else total + flag1 * cross_back).astype(BF16)
 
     @pl.when(even)
     def _():
-        h = even_ref[:size, :width]
-        xh = even_ref[:size, width:]
+        h = far_ref[:size, :width]
+        xh = far_ref[:size, width:]
         parts = tile(f_ref[...], h, scale)
         out_ref[...] = near_ref[...] + mine * times(parts, xh)
         cross = tile(g_ref[...], h, scale)
-        sib_ref[...] = sib_in_ref[...] + times(cross, xh)
+        sib = times(cross, xh)
+        sib_ref[...] = (sib + heads[0][...] if heads else sib).astype(sib_ref.dtype)
         put(times_back(parts, xt_ref[...]), times_back(cross, xst_ref[...]))
 
     @pl.when(jnp.logical_not(even))
     def _():
-        h = odd_ref[:size, :width]
-        xh = odd_ref[:size, width:]
+        h = far_ref[:size, :width]
+        xh = far_ref[:size, width:]
         parts = tile(f_ref[...], h, scale)
         out_ref[...] = near_ref[...] + mine * times(parts, xh)
-        sib_ref[...] = sib_in_ref[...]
+        sib_ref[...] = jnp.zeros_like(sib_ref)
         put(times_back(parts, xt_ref[...]), None)
 
 
 def final_kernel(near_ref, far_ref, sib_ref, back_ref, list_ref, count_ref, out_ref):
     rows = out_ref.shape[0]
-    flag = member(list_ref, count_ref, 1)
-    out_ref[...] = near_ref[...] + far_ref[...] + flag * sib_ref[:rows] + back_ref[...].astype(F32)
+    after, before = member(list_ref, count_ref, 1), member(list_ref, count_ref, -1)
+    sib = after * sib_ref[:rows].astype(F32) + before * sib_ref[rows : 2 * rows].astype(F32)
+    out_ref[...] = near_ref[...] + far_ref[...] + sib + back_ref[...].astype(F32)
 
 
 def sender(index, bits):
     return all(index >> at & 1 == bit for at, bit in bits)
 
 
-def moved(array, by, bits=()):
+def moved(array, by, wrap=True):
     peers = lax.axis_size("leaf")
-    pairs = [(i, i + by) for i in range(peers) if 0 <= i + by < peers and sender(i, bits)]
-    return lax.ppermute(array, "leaf", pairs)
+    return lax.ppermute(array, "leaf", [(i, (i + by) % peers) for i in range(peers) if wrap or 0 <= i + by < peers])
+
+
+def level1_partner(index):
+    return index ^ (2 if index & 1 else 8 if index & 2 else 4)
 
 
 def across(array, distance, bits=()):
@@ -261,6 +276,7 @@
 
 def body(features, probes, bases, transfers, couplings, near_list, near_count):
     rows, width = features.shape
+    near_count = near_count.reshape(1, 1)
     count = probes.shape[1]
     rank = bases.shape[1]
     depth = transfers.shape[1]
@@ -271,33 +287,34 @@
     sizes = [rows // 2, rows // 2]
 
     sib_features = partner(features, 0)
+    bases_v, transfer0 = call(
+        load_kernel,
+        [shape((rows, rank), F32), shape((rank, rank), F32)],
+        [HBM] * 2,
+        1000,
+        bases, transfers,
+        scratch=[pltpu.SemaphoreType.DMA((2,))],
+        limit=LOAD_LIMIT,
+    )
     (message,) = call(
         functools.partial(leaf_kernel, factors[0]),
         [shape((2 * count + rows // 2, rank), F32)],
-        [HBM] * 3,
+        [VMEM] * 3,
         6 * rows * rank * count,
-        bases, probes, transfers,
-        scratch=[
-            pltpu.VMEM((rows, rank), F32),
-            pltpu.VMEM((rows, count), F32),
-            pltpu.VMEM((rank, rank), F32),
-            pltpu.SemaphoreType.DMA((3,)),
-        ],
-        limit=LOAD_LIMIT,
+        bases_v, probes, transfer0,
     )
     gots = [partner(message, 0)]
     packed = []
-    for at in range(2):
+    for at, lists in enumerate(([], [near_list, near_count])):
         packed += call(
             functools.partial(pack_kernel, sizes[0] * at),
             [shape((sizes[at] + FLAG_ROWS * at, width + count), BF16)],
-            [VMEM, VMEM, SMEM, SMEM],
+            [VMEM, VMEM] + [SMEM] * len(lists),
             1000,
-            features, probes, near_list, near_count,
+            features, probes, *lists,
         )
-    far_even = moved(packed[0], -2, ((0, 0),))
-    far_odd = moved(packed[0], -2, ((0, 1),))
-    far_last = moved(packed[1], -2)
+    far_first = moved(packed[0], -2)
+    far_last = moved(packed[1], -2, wrap=False)
     own = [message]
     for level in range(1, depth + 1):
         last = level == depth
@@ -309,7 +326,11 @@
             6 * rank * rank * count,
             *own, gots[-1], transfers,
         )
-        gots.append(partner(message, level, SHARED[min(level, 3)]))
+        if level == 1:
+            whole = [(i, level1_partner(i)) for i in range(lax.axis_size("leaf"))]
+            gots.append(lax.ppermute(message, "leaf", whole))
+        else:
+            gots.append(partner(message, level, SHARED[min(level, 3)]))
 
     tile_flops = 2 * rows * rows * (width + 4 * count)
     (near,) = call(
@@ -319,24 +340,25 @@
         tile_flops,
         features, probes,
     )
-    near, sib, xt, xst = call(
+    near, pair, xt, xst = call(
         functools.partial(pair_kernel, scale),
-        [shape((rows, count), F32)] * 2 + [shape((count, rows), BF16)] * 2,
+        [shape((rows, count), F32), shape((rows, count), BF16)] + [shape((count, rows), BF16)] * 2,
         [VMEM] * 5 + [SMEM] * 2,
         tile_flops,
         features, sib_features, near, probes, gots[0], near_list, near_count,
     )
     heads = []
-    for at, (size, parts) in enumerate(zip(sizes, ((far_even, far_odd), (far_last, far_last)))):
+    for at, (size, part) in enumerate(zip(sizes, (far_first, far_last))):
         back_shapes = [shape((size, count), F32)] * 2 if at == 0 else [shape((rows, count), BF16)]
-        near, sib, *heads = call(
+        near, *heads = call(
             functools.partial(chunk_kernel, scale, size),
-            [shape((rows, count), F32), shape((rows, count), F32), *back_shapes],
-            [VMEM] * 8 + [SMEM] * 2 + [VMEM] * len(heads),
+            [shape((rows, count), F32), shape((rows, count), BF16 if at else F32), *back_shapes],
+            [VMEM] * 6 + [SMEM] * 2 + [VMEM] * len(heads),
             tile_flops * 2 * size // rows,
-            features, sib_features, *parts, near, sib, xt, xst, near_list, near_count, *heads,
+            features, sib_features, part, near, xt, xst, near_list, near_count, *heads,
         )
-    back = moved(heads[0], 2)
+    cross, back = heads
+    back = moved(back, 2, wrap=False)
     product_flops = 6 * count * rank * rank
     e3, e3_message = call(
         functools.partial(top_kernel, scale_g, factors[depth - 1]),
@@ -356,10 +378,10 @@
     e2_sent = partner(e2_message, 1, SHARED[2])
     e1, sib_message = call(
         functools.partial(node_kernel, scale_g, factors[1], 1),
-        [shape((count, rank), F32), shape((rows + rank, count), F32)],
-        [VMEM] * 6,
+        [shape((count, rank), F32), shape((2 * rows + 2 * rank, count), BF16)],
+        [VMEM] * 7,
         2 * product_flops,
-        couplings, transfers, gots[1], e2, e2_sent, sib,
+        couplings, transfers, gots[1], e2, e2_sent, cross, pair,
     )
     sib_got = partner(sib_message, 0)
     (far_sum,) = call(
@@ -367,7 +389,7 @@
         [shape((rows, count), F32)],
         [VMEM] * 6,
         2 * product_flops + 6 * rows * rank * count,
-        couplings, transfers, bases, gots[0], e1, sib_got,
+        couplings, transfers, bases_v, gots[0], e1, sib_got,
     )
     (out,) = call(
         final_kernel,

time: 74 us -> 69.2 us (0.935)
  waiting for transfers between devices: 16.8 us -> 13.8 us
  starting transfers between devices: 40.1 us -> 38.6 us
  local copies, waits for them, and re-layouts: 1.06 us -> 0.05 us
  Pallas kernels: 14.6 us -> 15.4 us
    ppermute x4, waiting for transfers between devices: 16.8 us -> 13.8 us  [the longest x3 13.8 us: moved(): lax.ppermute(array, 'leaf', [(i, (i + by) % peers) for i in range(peers)...]
    ppermute x9 -> x8, starting transfers between devices: 29.2 us -> 27.7 us  [across(): return lax.ppermute(array, 'leaf', [(i, i ^ distance) for i in senders])]
    unnamed x12 -> x10, local copies, waits for them, and re-layouts: 1.06 us -> 0.05 us
    pallas_call x16 -> x17, Pallas kernels: 14.6 us -> 15.4 us  [call(): pl.pallas_call(kernel, out_shape=outs, in_specs=specs, out_specs=[VMEM] *...]
  transfers between devices with their start and end apart: 13 -> 12, of which waited for: 3 -> 2; matrix products, arithmetic and copies ran while one was open for 0% -> 0% of each run, Pallas kernels for 18% -> 20%
where the time goes in v5:
time: 69.2 us; the launch traced here: 68.9 us
  starting transfers between devices  38.6 us (56%)
  Pallas kernels  15.4 us (22%)
  waiting for transfers between devices  13.8 us (20%)
  between operations  0.94 us (1%)
    ppermute x8, starting transfers between devices, across(): return lax.ppermute(array, 'leaf', [(i, i ^ distance) for i in senders])  27.7 us
    pallas_call x17, Pallas kernels, call(): pl.pallas_call(kernel, out_shape=outs, in_specs=specs, out_specs=[VMEM] *...  15.4 us
    ppermute x3, waiting for transfers between devices, moved(): lax.ppermute(array, 'leaf', [(i, (i + by) % peers) for i in range(peers)...  13.8 us
    ppermute x3, starting transfers between devices, moved(): lax.ppermute(array, 'leaf', [(i, (i + by) % peers) for i in range(peers)...  10.2 us
  transfers between devices with their start and end apart: 12, of which 2 were waited for; matrix products, arithmetic and copies ran while one was open for 0% of the time, Pallas kernels for 20%

profile of v5, /device:TPU:8, one launch (start us, length us, event | category | flops | bytes accessed | tf_op | source)
XLA Modules:
  0.0 68.9 jit_solution(17782416827332598342)
XLA Ops:
  0.0 1.2 %shard_map.76 = (f32[512,256]{1,0:T(8,128)S(1)}, f32[256,256]{1,0:T(8,128)S(1)}) custom-call(f32[512,256]{1,0:T(8,128)} %bases_hbm.1, f32[1,4,256,256]{3,2,1,0:T(8,128)} %transfer_ref.15), custom_call_target="tpu_custom_call" | custom-call | flops 1000 | bytes 2359296 | tf_op jit(solution)/shard_map/pallas_call | solution.py:57
  1.2 0.0 copy-done.3
  1.3 0.5 shard_map.77.own_ref
  1.8 0.0 copy-start
  1.8 0.4 collective-permute-start.3
  2.3 0.0 copy-start.4
  2.4 2.4 %collective-permute-start.2 = (bf16[256,1152]{1,0:T(8,128)(2,1)S(1)}, bf16[256,1152]{1,0:T(8,128)(2,1)S(1)}, u32[]{:S(2)}, u32[]{:S(2)}) collective-permute-start(bf16[256,1152]{1,0:T(8,128)(2,1)S(1)} %shard_map.74), channel_id=1, source_target_pairs={{0,30},{1,31},{2,0},{3,1},{4,2},{5,3},{6,4},{7,5},{8,6},{9,7},{10,... | collective-permute-start | bytes 1769480 | tf_op jit(solution)/shard_map/ppermute | solution.py:261
  4.7 0.2 shard_map.81
  5.0 0.7 collective-permute-start.4
  6.3 0.6 shard_map.73
  6.9 4.3 %collective-permute-start.1 = (bf16[264,1152]{1,0:T(8,128)(2,1)S(1)}, bf16[264,1152]{1,0:T(8,128)(2,1)S(1)}, u32[]{:S(2)}, u32[]{:S(2)}) collective-permute-start(bf16[264,1152]{1,0:T(8,128)(2,1)S(1)} %shard_map.73), channel_id=1, source_target_pairs={{2,0},{3,1},{4,2},{5,3},{6,4},{7,5},{8,6},{9,7},{10,8},{11,9},{12,... | collective-permute-start | bytes 1824776 | tf_op jit(solution)/shard_map/ppermute | solution.py:261
  11.2 0.2 shard_map.82
  11.4 0.7 collective-permute-start.5
  12.1 0.2 shard_map.83
  12.4 0.7 collective-permute-start.6
  13.1 0.0 copy-start.2
  13.1 0.8 %collective-permute-start.7 = (bf16[128,256]{1,0:T(8,128)(2,1)S(1)}, bf16[128,256]{1,0:T(8,128)(2,1)S(1)}, u32[]{:S(2)}, u32[]{:S(2)}) collective-permute-start(bf16[128,256]{1,0:T(8,128)(2,1)S(1)} %shard_map.84), channel_id=1, source_target_pairs={{5,21},{13,29},{21,5},{29,13}} | collective-permute-start | bytes 196616 | tf_op jit(solution)/shard_map/ppermute | solution.py:270
  13.9 1.8 %shard_map.75.near_ref = f32[512,128]{1,0:T(8,128)S(1)} custom-call(bf16[512,1024]{1,0:T(8,128)(2,1)S(1)} %copy-done.1, f32[512,128]{1,0:T(8,128)S(1)} %copy-done.3), custom_call_target="tpu_custom_call" | custom-call | flops 805306368 | bytes 1572864 | tf_op jit(solution)/shard_map/pallas_call | solution.py:57
  15.7 0.5 shard_map.85
  16.2 0.7 collective-permute-start.8
  16.9 2.0 %shard_map.78 = (f32[512,128]{1,0:T(8,128)S(1)}, bf16[512,128]{1,0:T(8,128)(2,1)S(1)}, bf16[128,512]{1,0:T(8,128)(2,1)S(1)}, bf16[128,512]{1,0:T(8,128)(2,1)S(1)}) custom-call(bf16[512,1024]{1,0:T(8,128)(2,1)S(1)} %copy-done.1, bf16[512,1024]{1,0:T(8,128)(2,1)S(1)} %collective-permute-done.g_ref, f32[512,128]{1,0:T(8,128)S(1)} %shard_map.75.near_ref, ...), custom_call_target="tpu_custom_call" | custom-call | flops 805306368 | bytes 3801108 | tf_op jit(solution)/shard_map/pallas_call | solution.py:57
  18.9 2.6 %shard_map.79 = (f32[512,128]{1,0:T(8,128)S(1)}, f32[512,128]{1,0:T(8,128)S(1)}, f32[256,128]{1,0:T(8,128)S(1)}, f32[256,128]{1,0:T(8,128)S(1)}) custom-call(bf16[512,1024]{1,0:T(8,128)(2,1)S(1)} %copy-done.1, bf16[512,1024]{1,0:T(8,128)(2,1)S(1)} %collective-permute-done.g_ref, bf16[256,1152]{1,0:T(8,128)(2,1)S(1)} %collective-permute-done.2.far_ref, ...), custom_call_target="tpu_custom_call" | custom-call | flops 805306368 | bytes 3997716 | tf_op jit(solution)/shard_map/pallas_call | solution.py:57
  21.5 0.4 shard_map.86
  21.8 0.7 collective-permute-start.9
  22.5 9.1 %collective-permute-done.1.far_ref = bf16[264,1152]{1,0:T(8,128)(2,1)S(1)} collective-permute-done((bf16[264,1152]{1,0:T(8,128)(2,1)S(1)}, bf16[264,1152]{1,0:T(8,128)(2,1)S(1)}, u32[]{:S(2)}, u32[]{:S(2)}) %collective-permute-start.1) | collective-permute-done | bytes 608288 | tf_op jit(solution)/shard_map/ppermute | solution.py:261
  31.6 2.6 %shard_map.80 = (f32[512,128]{1,0:T(8,128)S(1)}, bf16[512,128]{1,0:T(8,128)(2,1)S(1)}, bf16[512,128]{1,0:T(8,128)(2,1)S(1)}) custom-call(bf16[512,1024]{1,0:T(8,128)(2,1)S(1)} %copy-done.1, bf16[512,1024]{1,0:T(8,128)(2,1)S(1)} %collective-permute-done.g_ref, bf16[264,1152]{1,0:T(8,128)(2,1)S(1)} %collective-permute-done.1.far_ref, ...), custom_call_target="tpu_custom_call" | custom-call | flops 805306368 | bytes 4278292 | tf_op jit(solution)/shard_map/pallas_call | solution.py:57
  34.2 0.4 shard_map.87
  34.6 23.8 %collective-permute-start.10 = (bf16[1536,128]{1,0:T(8,128)(2,1)S(1)}, bf16[1536,128]{1,0:T(8,128)(2,1)S(1)}, u32[]{:S(2)}, u32[]{:S(2)}) collective-permute-start(bf16[1536,128]{1,0:T(8,128)(2,1)S(1)} %get-tuple-element.53), channel_id=1, source_target_pairs={{0,1},{1,0},{2,3},{3,2},{4,5},{5,4},{6,7},{7,6},{8,9},{9,8},{10,11... | collective-permute-start | bytes 1179656 | tf_op jit(solution)/shard_map/ppermute | solution.py:270
  58.4 3.6 %collective-permute-start.11 = (bf16[512,128]{1,0:T(8,128)(2,1)S(1)}, bf16[512,128]{1,0:T(8,128)(2,1)S(1)}, u32[]{:S(2)}, u32[]{:S(2)}) collective-permute-start(bf16[512,128]{1,0:T(8,128)(2,1)S(1)} %get-tuple-element.54), channel_id=1, source_target_pairs={{0,2},{1,3},{2,4},{3,5},{4,6},{5,7},{6,8},{7,9},{8,10},{9,11},{10,... | collective-permute-start | bytes 393224 | tf_op jit(solution)/shard_map/ppermute | solution.py:261
  62.0 0.9 %shard_map.88.far_ref = f32[512,128]{1,0:T(8,128)S(1)} custom-call(f32[1,5,256,256]{3,2,1,0:T(8,128)S(1)} %copy-done.2, f32[1,4,256,256]{3,2,1,0:T(8,128)S(1)} %copy-done, f32[512,256]{1,0:T(8,128)S(1)} %get-tuple-element.30.bases_ref, f32[512,256]{1,0:T(8,128)S(1)} %collective-permute-done.3.got_ref, f32[128,256]{1,0:T(8,128)S(1)} %get-tuple-element.52.above_ref, ...), custom_call_target="tpu_custom_call" | custom-call | flops 201326592 | bytes 4194304 | tf_op jit(solution)/shard_map/pallas_call | solution.py:57
  62.9 4.7 %collective-permute-done.11.back_ref = bf16[512,128]{1,0:T(8,128)(2,1)S(1)} collective-permute-done((bf16[512,128]{1,0:T(8,128)(2,1)S(1)}, bf16[512,128]{1,0:T(8,128)(2,1)S(1)}, u32[]{:S(2)}, u32[]{:S(2)}) %collective-permute-start.11) | collective-permute-done | bytes 131104 | tf_op jit(solution)/shard_map/ppermute | solution.py:261
  67.6 1.3 %shard_map.89 = f32[512,128]{1,0:T(8,128)} custom-call(f32[512,128]{1,0:T(8,128)S(1)} %get-tuple-element.39.near_ref, f32[512,128]{1,0:T(8,128)S(1)} %shard_map.88.far_ref, bf16[1536,128]{1,0:T(8,128)(2,1)S(1)} %collective-permute-done.10.sent_ref.sib_ref, bf16[512,128]{1,0:T(8,128)(2,1)S(1)} %collective-permute-done.11.back_ref, s32[1,4]{1,0:T(1,128)S(1)} %copy-done.4, ...), custom_call_target="tpu_custom_call" | custom-call | flops 393216 | bytes 1310740 | tf_op jit(solution)/shard_map/pallas_call | solution.py:57
  (19 shorter events, 0.1 us)
Async XLA Ops:
  0.0 2.3 %copy-start.1 = (bf16[512,1024]{1,0:T(8,128)(2,1)S(1)}, bf16[512,1024]{1,0:T(8,128)(2,1)}, u32[]{:S(2)}) copy-start(bf16[512,1024]{1,0:T(8,128)(2,1)} %f_ref.11) | copy-start | bytes 3145732
  0.0 1.3 %copy-start.3 = (f32[512,128]{1,0:T(8,128)S(1)}, f32[512,128]{1,0:T(8,128)}, u32[]{:S(2)}) copy-start(f32[512,128]{1,0:T(8,128)} %x_ref.9) | copy-start | bytes 786436
  0.0 16.9 %collective-permute-start = (bf16[512,1024]{1,0:T(8,128)(2,1)}, bf16[512,1024]{1,0:T(8,128)(2,1)S(1)}, u32[]{:S(2)}, u32[]{:S(2)}) collective-permute-start(bf16[512,1024]{1,0:T(8,128)(2,1)} %f_ref.11), channel_id=1, source_target_pairs={{0,1},{1,0},{2,3},{3,2},{4,5},{5,4},{6,7},{7,6},{8,9},{9,8},{10,11... | collective-permute-start | bytes 3145736 | tf_op jit(solution)/shard_map/ppermute | solution.py:270
  1.8 2.9 %copy-start = (f32[1,4,256,256]{3,2,1,0:T(8,128)S(1)}, f32[1,4,256,256]{3,2,1,0:T(8,128)}, u32[]{:S(2)}) copy-start(f32[1,4,256,256]{3,2,1,0:T(8,128)} %transfer_ref.15) | copy-start | bytes 3145732
  1.8 2.9 %collective-permute-start.3 = (f32[512,256]{1,0:T(8,128)S(1)}, f32[512,256]{1,0:T(8,128)S(1)}, u32[]{:S(2)}, u32[]{:S(2)}) collective-permute-start(f32[512,256]{1,0:T(8,128)S(1)} %shard_map.77.own_ref), channel_id=1, source_target_pairs={{0,1},{1,0},{2,3},{3,2},{4,5},{5,4},{6,7},{7,6},{8,9},{9,8},{10,11... | collective-permute-start | bytes 1572872 | tf_op jit(solution)/shard_map/ppermute | solution.py:270
  2.3 4.0 %copy-start.4 = (s32[1,4]{1,0:T(1,128)S(1)}, s32[1,4]{1,0:T(1,128)}, u32[]{:S(2)}) copy-start(s32[1,4]{1,0:T(1,128)} %list_ref.7) | copy-start | bytes 52
  2.4 16.5 %collective-permute-start.2 = (bf16[256,1152]{1,0:T(8,128)(2,1)S(1)}, bf16[256,1152]{1,0:T(8,128)(2,1)S(1)}, u32[]{:S(2)}, u32[]{:S(2)}) collective-permute-start(bf16[256,1152]{1,0:T(8,128)(2,1)S(1)} %shard_map.74), channel_id=1, source_target_pairs={{0,30},{1,31},{2,0},{3,1},{4,2},{5,3},{6,4},{7,5},{8,6},{9,7},{10,... | collective-permute-start | bytes 1769480 | tf_op jit(solution)/shard_map/ppermute | solution.py:261
  5.0 6.2 %collective-permute-start.4 = (bf16[256,256]{1,0:T(8,128)(2,1)S(1)}, bf16[256,256]{1,0:T(8,128)(2,1)S(1)}, u32[]{:S(2)}, u32[]{:S(2)}) collective-permute-start(bf16[256,256]{1,0:T(8,128)(2,1)S(1)} %get-tuple-element.40), channel_id=1, source_target_pairs={{0,4},{1,3},{2,10},{3,1},{4,0},{5,7},{6,14},{7,5},{8,12},{9,11},{1... | collective-permute-start | bytes 393224 | tf_op jit(solution)/shard_map/ppermute | solution.py:331
  6.9 24.7 %collective-permute-start.1 = (bf16[264,1152]{1,0:T(8,128)(2,1)S(1)}, bf16[264,1152]{1,0:T(8,128)(2,1)S(1)}, u32[]{:S(2)}, u32[]{:S(2)}) collective-permute-start(bf16[264,1152]{1,0:T(8,128)(2,1)S(1)} %shard_map.73), channel_id=1, source_target_pairs={{2,0},{3,1},{4,2},{5,3},{6,4},{7,5},{8,6},{9,7},{10,8},{11,9},{12,... | collective-permute-start | bytes 1824776 | tf_op jit(solution)/shard_map/ppermute | solution.py:261
  11.4 0.7 collective-permute-start.5
  12.4 0.7 collective-permute-start.6
  13.1 2.6 %copy-start.2 = (f32[1,5,256,256]{3,2,1,0:T(8,128)S(1)}, f32[1,5,256,256]{3,2,1,0:T(8,128)}, u32[]{:S(2)}) copy-start(f32[1,5,256,256]{3,2,1,0:T(8,128)} %coupling_ref.7) | copy-start | bytes 3932164
  13.1 2.6 %collective-permute-start.7 = (bf16[128,256]{1,0:T(8,128)(2,1)S(1)}, bf16[128,256]{1,0:T(8,128)(2,1)S(1)}, u32[]{:S(2)}, u32[]{:S(2)}) collective-permute-start(bf16[128,256]{1,0:T(8,128)(2,1)S(1)} %shard_map.84), channel_id=1, source_target_pairs={{5,21},{13,29},{21,5},{29,13}} | collective-permute-start | bytes 196616 | tf_op jit(solution)/shard_map/ppermute | solution.py:270
  16.2 5.2 %collective-permute-start.8 = (bf16[128,256]{1,0:T(8,128)(2,1)S(1)}, bf16[128,256]{1,0:T(8,128)(2,1)S(1)}, u32[]{:S(2)}, u32[]{:S(2)}) collective-permute-start(bf16[128,256]{1,0:T(8,128)(2,1)S(1)} %get-tuple-element.47), channel_id=1, source_target_pairs={{5,1},{13,9},{21,17},{29,25}} | collective-permute-start | bytes 196616 | tf_op jit(solution)/shard_map/ppermute | solution.py:270
  21.8 12.4 %collective-permute-start.9 = (bf16[128,256]{1,0:T(8,128)(2,1)S(1)}, bf16[128,256]{1,0:T(8,128)(2,1)S(1)}, u32[]{:S(2)}, u32[]{:S(2)}) collective-permute-start(bf16[128,256]{1,0:T(8,128)(2,1)S(1)} %get-tuple-element.49), channel_id=1, source_target_pairs={{1,3},{5,7},{9,11},{13,15},{17,19},{21,23},{25,27},{29,31}} | collective-permute-start | bytes 196616 | tf_op jit(solution)/shard_map/ppermute | solution.py:270
  34.6 27.4 %collective-permute-start.10 = (bf16[1536,128]{1,0:T(8,128)(2,1)S(1)}, bf16[1536,128]{1,0:T(8,128)(2,1)S(1)}, u32[]{:S(2)}, u32[]{:S(2)}) collective-permute-start(bf16[1536,128]{1,0:T(8,128)(2,1)S(1)} %get-tuple-element.53), channel_id=1, source_target_pairs={{0,1},{1,0},{2,3},{3,2},{4,5},{5,4},{6,7},{7,6},{8,9},{9,8},{10,11... | collective-permute-start | bytes 1179656 | tf_op jit(solution)/shard_map/ppermute | solution.py:270
  58.4 9.1 %collective-permute-start.11 = (bf16[512,128]{1,0:T(8,128)(2,1)S(1)}, bf16[512,128]{1,0:T(8,128)(2,1)S(1)}, u32[]{:S(2)}, u32[]{:S(2)}) collective-permute-start(bf16[512,128]{1,0:T(8,128)(2,1)S(1)} %get-tuple-element.54), channel_id=1, source_target_pairs={{0,2},{1,3},{2,4},{3,5},{4,6},{5,7},{6,8},{7,9},{8,10},{9,11},{10,... | collective-permute-start | bytes 393224 | tf_op jit(solution)/shard_map/ppermute | solution.py:261

commit v6 on v5

--- a/solution.py
+++ b/solution.py
@@ -17,6 +17,7 @@
 NT = (((1,), (1,)), ((), ()))
 TN = (((0,), (0,)), ((), ()))
 FLAG_ROWS = 8
+OFFSETS = (-2, -1, 1, 2)
 LIMIT = 16 << 20
 LOAD_LIMIT = 55400000
 SHARED = ((), ((0, 1),), ((0, 1), (1, 0)), ((0, 1), (1, 0), (2, 1)))
@@ -87,17 +88,26 @@
 
 
 def pack_kernel(first, f_ref, x_ref, *refs):
-    far_ref = refs[-1]
     rows, width = f_ref.shape
     probes = x_ref.shape[1]
-    size = min(far_ref.shape[0], rows - first)
-    far_ref[:size, :width] = f_ref[first : first + size]
-    far_ref[:size, width:] = x_ref[first : first + size].astype(BF16)
-    if far_ref.shape[0] > size:
-        list_ref, count_ref = refs[:2]
+    if len(refs) == 1:
+        far_ref = refs[0]
+        size = far_ref.shape[0]
+    else:
+        list_ref, count_ref, far_ref, flags_ref = refs
+        size = rows - first
         flags = [jnp.full((FLAG_ROWS, probes), member(list_ref, count_ref, offset), F32) for offset in (-2, -1)]
         flags.append(jnp.zeros((FLAG_ROWS, width - probes), F32))
         far_ref[size:] = jnp.concatenate(flags, axis=1).astype(BF16)
+        for row, offset in enumerate(OFFSETS):
+            flags_ref[row : row + 1] = jnp.full((1, probes), member(list_ref, count_ref, offset), F32)
+    far_ref[:size, :width] = f_ref[first : first + size]
+    far_ref[:size, width:] = x_ref[first : first + size].astype(BF16)
+
+
+def flag_of(flags_ref, offset):
+    row = OFFSETS.index(offset)
+    return flags_ref[row : row + 1]
 
 
 def up_kernel(level, factor, own_ref, got_ref, transfer_ref, message_ref, *next_refs):
@@ -183,7 +193,7 @@
     return (dot(xt16, parts[0], NN) + dot(xt16, parts[1], NN)).T
 
 
-def pair_kernel(scale, f_ref, g_ref, near_ref, x_ref, got_ref, list_ref, count_ref, out_ref, pair_ref, xt_ref, xst_ref):
+def pair_kernel(scale, f_ref, g_ref, near_ref, x_ref, got_ref, flags_ref, out_ref, pair_ref, xt_ref, xst_ref):
     even = bit_of(0) == 0
     rows, probes = near_ref.shape
     xt_ref[...] = x_ref[...].T.astype(BF16)
@@ -194,7 +204,7 @@
     @pl.when(even)
     def _():
         parts = tile(f_ref[...], g_ref[...], scale)
-        flag = member(list_ref, count_ref, 1)
+        flag = flag_of(flags_ref, 1)
         out_ref[...] = near_ref[...] + flag * times(parts, jnp.concatenate(halves_of, axis=0).astype(BF16))
         pair_ref[...] = times_back(parts, xt_ref[...]).astype(BF16)
 
@@ -204,13 +214,13 @@
         pair_ref[...] = jnp.zeros_like(pair_ref)
 
 
-def chunk_kernel(scale, size, f_ref, g_ref, far_ref, near_ref, xt_ref, xst_ref, list_ref, count_ref, *refs):
+def chunk_kernel(scale, size, f_ref, g_ref, far_ref, near_ref, xt_ref, xst_ref, flags_ref, *refs):
     even = lax.rem(lax.axis_index("leaf"), 2) == 0
     width = f_ref.shape[1]
     probes = near_ref.shape[1]
     heads = refs[: len(refs) // 5 * 3]
     out_ref, sib_ref, *back_refs = refs[len(heads) :]
-    mine = member(list_ref, count_ref, 2)
+    mine = flag_of(flags_ref, 2)
 
     def put(back, cross_back):
         if not heads:
@@ -245,9 +255,9 @@
         put(times_back(parts, xt_ref[...]), None)
 
 
-def final_kernel(near_ref, far_ref, sib_ref, back_ref, list_ref, count_ref, out_ref):
+def final_kernel(near_ref, far_ref, sib_ref, back_ref, flags_ref, out_ref):
     rows = out_ref.shape[0]
-    after, before = member(list_ref, count_ref, 1), member(list_ref, count_ref, -1)
+    after, before = flag_of(flags_ref, 1), flag_of(flags_ref, -1)
     sib = after * sib_ref[:rows].astype(F32) + before * sib_ref[rows : 2 * rows].astype(F32)
     out_ref[...] = near_ref[...] + far_ref[...] + sib + back_ref[...].astype(F32)
 
@@ -308,11 +318,12 @@
     for at, lists in enumerate(([], [near_list, near_count])):
         packed += call(
             functools.partial(pack_kernel, sizes[0] * at),
-            [shape((sizes[at] + FLAG_ROWS * at, width + count), BF16)],
+            [shape((sizes[at] + FLAG_ROWS * at, width + count), BF16)] + [shape((FLAG_ROWS, count), F32)] * at,
             [VMEM, VMEM] + [SMEM] * len(lists),
             1000,
             features, probes, *lists,
         )
+    flags = packed.pop()
     far_first = moved(packed[0], -2)
     far_last = moved(packed[1], -2, wrap=False)
     own = [message]
@@ -343,9 +354,9 @@
     near, pair, xt, xst = call(
         functools.partial(pair_kernel, scale),
         [shape((rows, count), F32), shape((rows, count), BF16)] + [shape((count, rows), BF16)] * 2,
-        [VMEM] * 5 + [SMEM] * 2,
+        [VMEM] * 6,
         tile_flops,
-        features, sib_features, near, probes, gots[0], near_list, near_count,
+        features, sib_features, near, probes, gots[0], flags,
     )
     heads = []
     for at, (size, part) in enumerate(zip(sizes, (far_first, far_last))):
@@ -353,9 +364,9 @@
         near, *heads = call(
             functools.partial(chunk_kernel, scale, size),
             [shape((rows, count), F32), shape((rows, count), BF16 if at else F32), *back_shapes],
-            [VMEM] * 6 + [SMEM] * 2 + [VMEM] * len(heads),
+            [VMEM] * (7 + len(heads)),
             tile_flops * 2 * size // rows,
-            features, sib_features, part, near, xt, xst, near_list, near_count, *heads,
+            features, sib_features, part, near, xt, xst, flags, *heads,
         )
     cross, back = heads
     back = moved(back, 2, wrap=False)
@@ -394,9 +405,9 @@
     (out,) = call(
         final_kernel,
         [shape((rows, count), F32)],
-        [VMEM] * 4 + [SMEM] * 2,
+        [VMEM] * 5,
         6 * rows * count,
-        near, far_sum, sib_got, back, near_list, near_count,
+        near, far_sum, sib_got, back, flags,
     )
     return out
 

time: 69.2 us -> 68.2 us (0.986)
  Pallas kernels: 15.4 us -> 13.2 us
  waiting for transfers between devices: 13.8 us -> 14.5 us
    pallas_call x17, Pallas kernels: 15.4 us -> 13.2 us  [call(): pl.pallas_call(kernel, out_shape=outs, in_specs=specs, out_specs=[VMEM] *...]
    ppermute x3, waiting for transfers between devices: 13.8 us -> 14.5 us  [moved(): lax.ppermute(array, 'leaf', [(i, (i + by) % peers) for i in range(peers)...]
  transfers between devices with their start and end apart: 12 -> 12, of which waited for: 2 -> 3; matrix products, arithmetic and copies ran while one was open for 0% -> 0% of each run, Pallas kernels for 20% -> 18%
where the time goes in v6:
time: 68.2 us; the launch traced here: 68 us
  starting transfers between devices  39.2 us (57%)
  waiting for transfers between devices  14.5 us (21%)
  Pallas kernels  13.2 us (19%)
  between operations  0.93 us (1%)
    ppermute x8, starting transfers between devices, across(): return lax.ppermute(array, 'leaf', [(i, i ^ distance) for i in senders])  27.9 us
    ppermute x3, waiting for transfers between devices, moved(): lax.ppermute(array, 'leaf', [(i, (i + by) % peers) for i in range(peers)...  14.5 us
    pallas_call x17, Pallas kernels, call(): pl.pallas_call(kernel, out_shape=outs, in_specs=specs, out_specs=[VMEM] *...  13.2 us
    ppermute x3, starting transfers between devices, moved(): lax.ppermute(array, 'leaf', [(i, (i + by) % peers) for i in range(peers)...  10.6 us
  transfers between devices with their start and end apart: 12, of which 3 were waited for; matrix products, arithmetic and copies ran while one was open for 0% of the time, Pallas kernels for 18%

profile of v6, /device:TPU:8, one launch (start us, length us, event | category | flops | bytes accessed | tf_op | source)
XLA Modules:
  0.0 68.0 jit_solution(4441461627320573273)
XLA Ops:
  0.0 1.2 %shard_map.76 = (f32[512,256]{1,0:T(8,128)S(1)}, f32[256,256]{1,0:T(8,128)S(1)}) custom-call(f32[512,256]{1,0:T(8,128)} %bases_hbm.1, f32[1,4,256,256]{3,2,1,0:T(8,128)} %transfer_ref.15), custom_call_target="tpu_custom_call" | custom-call | flops 1000 | bytes 2359296 | tf_op jit(solution)/shard_map/pallas_call | solution.py:58
  1.2 0.0 copy-done.3
  1.3 0.5 shard_map.77.own_ref
  1.8 0.0 copy-start
  1.8 0.4 collective-permute-start.3
  2.3 0.0 copy-start.4
  2.4 2.4 %collective-permute-start.2 = (bf16[256,1152]{1,0:T(8,128)(2,1)S(1)}, bf16[256,1152]{1,0:T(8,128)(2,1)S(1)}, u32[]{:S(2)}, u32[]{:S(2)}) collective-permute-start(bf16[256,1152]{1,0:T(8,128)(2,1)S(1)} %shard_map.74), channel_id=1, source_target_pairs={{0,30},{1,31},{2,0},{3,1},{4,2},{5,3},{6,4},{7,5},{8,6},{9,7},{10,... | collective-permute-start | bytes 1769480 | tf_op jit(solution)/shard_map/ppermute | solution.py:271
  4.7 0.2 shard_map.81
  5.0 0.7 %collective-permute-start.4 = (bf16[256,256]{1,0:T(8,128)(2,1)S(1)}, bf16[256,256]{1,0:T(8,128)(2,1)S(1)}, u32[]{:S(2)}, u32[]{:S(2)}) collective-permute-start(bf16[256,256]{1,0:T(8,128)(2,1)S(1)} %get-tuple-element.44), channel_id=1, source_target_pairs={{0,4},{1,3},{2,10},{3,1},{4,0},{5,7},{6,14},{7,5},{8,12},{9,11},{1... | collective-permute-start | bytes 393224 | tf_op jit(solution)/shard_map/ppermute | solution.py:342
  6.3 0.6 shard_map.73
  6.9 4.3 %collective-permute-start.1 = (bf16[264,1152]{1,0:T(8,128)(2,1)S(1)}, bf16[264,1152]{1,0:T(8,128)(2,1)S(1)}, u32[]{:S(2)}, u32[]{:S(2)}) collective-permute-start(bf16[264,1152]{1,0:T(8,128)(2,1)S(1)} %get-tuple-element.32), channel_id=1, source_target_pairs={{2,0},{3,1},{4,2},{5,3},{6,4},{7,5},{8,6},{9,7},{10,8},{11,9},{12,... | collective-permute-start | bytes 1824776 | tf_op jit(solution)/shard_map/ppermute | solution.py:271
  11.2 0.2 shard_map.82
  11.4 0.7 collective-permute-start.5
  12.1 0.2 shard_map.83
  12.4 0.7 collective-permute-start.6
  13.1 0.8 %collective-permute-start.7 = (bf16[128,256]{1,0:T(8,128)(2,1)S(1)}, bf16[128,256]{1,0:T(8,128)(2,1)S(1)}, u32[]{:S(2)}, u32[]{:S(2)}) collective-permute-start(bf16[128,256]{1,0:T(8,128)(2,1)S(1)} %shard_map.84), channel_id=1, source_target_pairs={{5,21},{13,29},{21,5},{29,13}} | collective-permute-start | bytes 196616 | tf_op jit(solution)/shard_map/ppermute | solution.py:280
  13.9 1.8 %shard_map.75.near_ref = f32[512,128]{1,0:T(8,128)S(1)} custom-call(bf16[512,1024]{1,0:T(8,128)(2,1)S(1)} %copy-done.1, f32[512,128]{1,0:T(8,128)S(1)} %copy-done.3), custom_call_target="tpu_custom_call" | custom-call | flops 805306368 | bytes 1572864 | tf_op jit(solution)/shard_map/pallas_call | solution.py:58
  15.7 0.5 shard_map.85
  16.2 0.7 collective-permute-start.8
  16.9 1.4 %shard_map.78 = (f32[512,128]{1,0:T(8,128)S(1)}, bf16[512,128]{1,0:T(8,128)(2,1)S(1)}, bf16[128,512]{1,0:T(8,128)(2,1)S(1)}, bf16[128,512]{1,0:T(8,128)(2,1)S(1)}) custom-call(bf16[512,1024]{1,0:T(8,128)(2,1)S(1)} %copy-done.1, bf16[512,1024]{1,0:T(8,128)(2,1)S(1)} %collective-permute-done.g_ref, f32[512,128]{1,0:T(8,128)S(1)} %shard_map.75.near_ref, ...), custom_call_target="tpu_custom_call" | custom-call | flops 805306368 | bytes 3805184 | tf_op jit(solution)/shard_map/pallas_call | solution.py:58
  18.3 0.3 collective-permute-done.2.far_ref
  18.6 2.0 %shard_map.79 = (f32[512,128]{1,0:T(8,128)S(1)}, f32[512,128]{1,0:T(8,128)S(1)}, f32[256,128]{1,0:T(8,128)S(1)}, f32[256,128]{1,0:T(8,128)S(1)}) custom-call(bf16[512,1024]{1,0:T(8,128)(2,1)S(1)} %copy-done.1, bf16[512,1024]{1,0:T(8,128)(2,1)S(1)} %collective-permute-done.g_ref, bf16[256,1152]{1,0:T(8,128)(2,1)S(1)} %collective-permute-done.2.far_ref, ...), custom_call_target="tpu_custom_call" | custom-call | flops 805306368 | bytes 4001792 | tf_op jit(solution)/shard_map/pallas_call | solution.py:58
  20.6 0.4 shard_map.86
  21.0 0.7 collective-permute-start.9
  21.7 10.0 %collective-permute-done.1.far_ref = bf16[264,1152]{1,0:T(8,128)(2,1)S(1)} collective-permute-done((bf16[264,1152]{1,0:T(8,128)(2,1)S(1)}, bf16[264,1152]{1,0:T(8,128)(2,1)S(1)}, u32[]{:S(2)}, u32[]{:S(2)}) %collective-permute-start.1) | collective-permute-done | bytes 608288 | tf_op jit(solution)/shard_map/ppermute | solution.py:271
  31.6 2.0 %shard_map.80 = (f32[512,128]{1,0:T(8,128)S(1)}, bf16[512,128]{1,0:T(8,128)(2,1)S(1)}, bf16[512,128]{1,0:T(8,128)(2,1)S(1)}) custom-call(bf16[512,1024]{1,0:T(8,128)(2,1)S(1)} %copy-done.1, bf16[512,1024]{1,0:T(8,128)(2,1)S(1)} %collective-permute-done.g_ref, bf16[264,1152]{1,0:T(8,128)(2,1)S(1)} %collective-permute-done.1.far_ref, ...), custom_call_target="tpu_custom_call" | custom-call | flops 805306368 | bytes 4282368 | tf_op jit(solution)/shard_map/pallas_call | solution.py:58
  33.7 0.4 shard_map.87
  34.1 24.0 %collective-permute-start.10 = (bf16[1536,128]{1,0:T(8,128)(2,1)S(1)}, bf16[1536,128]{1,0:T(8,128)(2,1)S(1)}, u32[]{:S(2)}, u32[]{:S(2)}) collective-permute-start(bf16[1536,128]{1,0:T(8,128)(2,1)S(1)} %get-tuple-element.57), channel_id=1, source_target_pairs={{0,1},{1,0},{2,3},{3,2},{4,5},{5,4},{6,7},{7,6},{8,9},{9,8},{10,11... | collective-permute-start | bytes 1179656 | tf_op jit(solution)/shard_map/ppermute | solution.py:280
  58.0 4.0 %collective-permute-start.11 = (bf16[512,128]{1,0:T(8,128)(2,1)S(1)}, bf16[512,128]{1,0:T(8,128)(2,1)S(1)}, u32[]{:S(2)}, u32[]{:S(2)}) collective-permute-start(bf16[512,128]{1,0:T(8,128)(2,1)S(1)} %get-tuple-element.58), channel_id=1, source_target_pairs={{0,2},{1,3},{2,4},{3,5},{4,6},{5,7},{6,8},{7,9},{8,10},{9,11},{10,... | collective-permute-start | bytes 393224 | tf_op jit(solution)/shard_map/ppermute | solution.py:271
  62.0 0.9 %shard_map.88.far_ref = f32[512,128]{1,0:T(8,128)S(1)} custom-call(f32[1,5,256,256]{3,2,1,0:T(8,128)S(1)} %copy-done.2, f32[1,4,256,256]{3,2,1,0:T(8,128)S(1)} %copy-done, f32[512,256]{1,0:T(8,128)S(1)} %get-tuple-element.33.bases_ref, f32[512,256]{1,0:T(8,128)S(1)} %collective-permute-done.3.got_ref, f32[128,256]{1,0:T(8,128)S(1)} %get-tuple-element.56.above_ref, ...), custom_call_target="tpu_custom_call" | custom-call | flops 201326592 | bytes 4194304 | tf_op jit(solution)/shard_map/pallas_call | solution.py:58
  62.9 4.3 %collective-permute-done.11.back_ref = bf16[512,128]{1,0:T(8,128)(2,1)S(1)} collective-permute-done((bf16[512,128]{1,0:T(8,128)(2,1)S(1)}, bf16[512,128]{1,0:T(8,128)(2,1)S(1)}, u32[]{:S(2)}, u32[]{:S(2)}) %collective-permute-start.11) | collective-permute-done | bytes 131104 | tf_op jit(solution)/shard_map/ppermute | solution.py:271
  67.2 0.8 %shard_map.89 = f32[512,128]{1,0:T(8,128)} custom-call(f32[512,128]{1,0:T(8,128)S(1)} %get-tuple-element.43.near_ref, f32[512,128]{1,0:T(8,128)S(1)} %shard_map.88.far_ref, bf16[1536,128]{1,0:T(8,128)(2,1)S(1)} %collective-permute-done.10.sent_ref.sib_ref, bf16[512,128]{1,0:T(8,128)(2,1)S(1)} %collective-permute-done.11.back_ref, ...), custom_call_target="tpu_custom_call" | custom-call | flops 393216 | bytes 1314816 | tf_op jit(solution)/shard_map/pallas_call | solution.py:58
  (19 shorter events, 0.1 us)
Async XLA Ops:
  0.0 2.3 %copy-start.1 = (bf16[512,1024]{1,0:T(8,128)(2,1)S(1)}, bf16[512,1024]{1,0:T(8,128)(2,1)}, u32[]{:S(2)}) copy-start(bf16[512,1024]{1,0:T(8,128)(2,1)} %f_ref.11) | copy-start | bytes 3145732
  0.0 1.3 %copy-start.3 = (f32[512,128]{1,0:T(8,128)S(1)}, f32[512,128]{1,0:T(8,128)}, u32[]{:S(2)}) copy-start(f32[512,128]{1,0:T(8,128)} %x_ref.9) | copy-start | bytes 786436
  0.0 16.9 %collective-permute-start = (bf16[512,1024]{1,0:T(8,128)(2,1)}, bf16[512,1024]{1,0:T(8,128)(2,1)S(1)}, u32[]{:S(2)}, u32[]{:S(2)}) collective-permute-start(bf16[512,1024]{1,0:T(8,128)(2,1)} %f_ref.11), channel_id=1, source_target_pairs={{0,1},{1,0},{2,3},{3,2},{4,5},{5,4},{6,7},{7,6},{8,9},{9,8},{10,11... | collective-permute-start | bytes 3145736 | tf_op jit(solution)/shard_map/ppermute | solution.py:280
  1.8 2.9 %copy-start = (f32[1,4,256,256]{3,2,1,0:T(8,128)S(1)}, f32[1,4,256,256]{3,2,1,0:T(8,128)}, u32[]{:S(2)}) copy-start(f32[1,4,256,256]{3,2,1,0:T(8,128)} %transfer_ref.15) | copy-start | bytes 3145732
  1.8 2.9 %collective-permute-start.3 = (f32[512,256]{1,0:T(8,128)S(1)}, f32[512,256]{1,0:T(8,128)S(1)}, u32[]{:S(2)}, u32[]{:S(2)}) collective-permute-start(f32[512,256]{1,0:T(8,128)S(1)} %shard_map.77.own_ref), channel_id=1, source_target_pairs={{0,1},{1,0},{2,3},{3,2},{4,5},{5,4},{6,7},{7,6},{8,9},{9,8},{10,11... | collective-permute-start | bytes 1572872 | tf_op jit(solution)/shard_map/ppermute | solution.py:280
  2.3 4.0 %copy-start.4 = (s32[1,4]{1,0:T(1,128)S(1)}, s32[1,4]{1,0:T(1,128)}, u32[]{:S(2)}) copy-start(s32[1,4]{1,0:T(1,128)} %refs_0_.1) | copy-start | bytes 52
  2.4 16.3 %collective-permute-start.2 = (bf16[256,1152]{1,0:T(8,128)(2,1)S(1)}, bf16[256,1152]{1,0:T(8,128)(2,1)S(1)}, u32[]{:S(2)}, u32[]{:S(2)}) collective-permute-start(bf16[256,1152]{1,0:T(8,128)(2,1)S(1)} %shard_map.74), channel_id=1, source_target_pairs={{0,30},{1,31},{2,0},{3,1},{4,2},{5,3},{6,4},{7,5},{8,6},{9,7},{10,... | collective-permute-start | bytes 1769480 | tf_op jit(solution)/shard_map/ppermute | solution.py:271
  5.0 6.2 %collective-permute-start.4 = (bf16[256,256]{1,0:T(8,128)(2,1)S(1)}, bf16[256,256]{1,0:T(8,128)(2,1)S(1)}, u32[]{:S(2)}, u32[]{:S(2)}) collective-permute-start(bf16[256,256]{1,0:T(8,128)(2,1)S(1)} %get-tuple-element.44), channel_id=1, source_target_pairs={{0,4},{1,3},{2,10},{3,1},{4,0},{5,7},{6,14},{7,5},{8,12},{9,11},{1... | collective-permute-start | bytes 393224 | tf_op jit(solution)/shard_map/ppermute | solution.py:342
  6.9 24.7 %collective-permute-start.1 = (bf16[264,1152]{1,0:T(8,128)(2,1)S(1)}, bf16[264,1152]{1,0:T(8,128)(2,1)S(1)}, u32[]{:S(2)}, u32[]{:S(2)}) collective-permute-start(bf16[264,1152]{1,0:T(8,128)(2,1)S(1)} %get-tuple-element.32), channel_id=1, source_target_pairs={{2,0},{3,1},{4,2},{5,3},{6,4},{7,5},{8,6},{9,7},{10,8},{11,9},{12,... | collective-permute-start | bytes 1824776 | tf_op jit(solution)/shard_map/ppermute | solution.py:271
  11.4 0.7 collective-permute-start.5
  12.4 0.7 collective-permute-start.6
  13.1 2.6 %copy-start.2 = (f32[1,5,256,256]{3,2,1,0:T(8,128)S(1)}, f32[1,5,256,256]{3,2,1,0:T(8,128)}, u32[]{:S(2)}) copy-start(f32[1,5,256,256]{3,2,1,0:T(8,128)} %coupling_ref.7) | copy-start | bytes 3932164
  13.1 2.6 %collective-permute-start.7 = (bf16[128,256]{1,0:T(8,128)(2,1)S(1)}, bf16[128,256]{1,0:T(8,128)(2,1)S(1)}, u32[]{:S(2)}, u32[]{:S(2)}) collective-permute-start(bf16[128,256]{1,0:T(8,128)(2,1)S(1)} %shard_map.84), channel_id=1, source_target_pairs={{5,21},{13,29},{21,5},{29,13}} | collective-permute-start | bytes 196616 | tf_op jit(solution)/shard_map/ppermute | solution.py:280
  16.2 4.4 %collective-permute-start.8 = (bf16[128,256]{1,0:T(8,128)(2,1)S(1)}, bf16[128,256]{1,0:T(8,128)(2,1)S(1)}, u32[]{:S(2)}, u32[]{:S(2)}) collective-permute-start(bf16[128,256]{1,0:T(8,128)(2,1)S(1)} %get-tuple-element.51), channel_id=1, source_target_pairs={{5,1},{13,9},{21,17},{29,25}} | collective-permute-start | bytes 196616 | tf_op jit(solution)/shard_map/ppermute | solution.py:280
  21.0 12.7 %collective-permute-start.9 = (bf16[128,256]{1,0:T(8,128)(2,1)S(1)}, bf16[128,256]{1,0:T(8,128)(2,1)S(1)}, u32[]{:S(2)}, u32[]{:S(2)}) collective-permute-start(bf16[128,256]{1,0:T(8,128)(2,1)S(1)} %get-tuple-element.53), channel_id=1, source_target_pairs={{1,3},{5,7},{9,11},{13,15},{17,19},{21,23},{25,27},{29,31}} | collective-permute-start | bytes 196616 | tf_op jit(solution)/shard_map/ppermute | solution.py:280
  34.1 27.9 %collective-permute-start.10 = (bf16[1536,128]{1,0:T(8,128)(2,1)S(1)}, bf16[1536,128]{1,0:T(8,128)(2,1)S(1)}, u32[]{:S(2)}, u32[]{:S(2)}) collective-permute-start(bf16[1536,128]{1,0:T(8,128)(2,1)S(1)} %get-tuple-element.57), channel_id=1, source_target_pairs={{0,1},{1,0},{2,3},{3,2},{4,5},{5,4},{6,7},{7,6},{8,9},{9,8},{10,11... | collective-permute-start | bytes 1179656 | tf_op jit(solution)/shard_map/ppermute | solution.py:280
  58.0 9.1 %collective-permute-start.11 = (bf16[512,128]{1,0:T(8,128)(2,1)S(1)}, bf16[512,128]{1,0:T(8,128)(2,1)S(1)}, u32[]{:S(2)}, u32[]{:S(2)}) collective-permute-start(bf16[512,128]{1,0:T(8,128)(2,1)S(1)} %get-tuple-element.58), channel_id=1, source_target_pairs={{0,2},{1,3},{2,4},{3,5},{4,6},{5,7},{6,8},{7,9},{8,10},{9,11},{10,... | collective-permute-start | bytes 393224 | tf_op jit(solution)/shard_map/ppermute | solution.py:271

commit v7 on v6

--- a/solution.py
+++ b/solution.py
@@ -10,7 +10,6 @@
 BF16 = jnp.bfloat16
 F32 = jnp.float32
 VMEM = pl.BlockSpec(memory_space=pltpu.VMEM)
-SMEM = pl.BlockSpec(memory_space=pltpu.SMEM)
 HBM = pl.BlockSpec(memory_space=pltpu.HBM)
 ANY = pl.BlockSpec(memory_space=pl.ANY)
 NN = (((1,), (0,)), ((), ()))
@@ -43,13 +42,10 @@
     return dot(a16, b_high, dims) + dot(a16, b_low, dims)
 
 
-def member(list_ref, count_ref, offset):
-    index = lax.axis_index("leaf")
-    found = jnp.float32(0.0)
-    for slot in range(list_ref.shape[1]):
-        hit = (list_ref[0, slot] == index + offset) & (slot < count_ref[0, 0])
-        found = jnp.where(hit, jnp.float32(1.0), found)
-    return found
+def member(near_list, near_count, offset):
+    slots = lax.broadcasted_iota(jnp.int32, near_list.shape, 1)
+    hits = (near_list == lax.axis_index("leaf") + offset) & (slots < near_count)
+    return jnp.max(jnp.where(hits, jnp.float32(1.0), jnp.float32(0.0)), axis=1, keepdims=True)
 
 
 def call(kernel, outs, specs, flops, *args, scratch=(), limit=LIMIT):
@@ -79,12 +75,10 @@
 
 def leaf_kernel(c1, bases_ref, x_ref, transfer_ref, message_ref):
     x = x_ref[...]
-    rows, probes = x.shape
+    probes = x.shape[1]
     skeleton = dot_wide(x, bases_ref[...], TN)
     message_ref[:probes] = skeleton
-    message_ref[probes : 2 * probes] = c1 * dot_wide(skeleton, transfer_ref[...], NN)
-    message_ref[2 * probes :, :probes] = x[: rows // 2]
-    message_ref[2 * probes :, probes:] = x[rows // 2 :]
+    message_ref[probes:] = c1 * dot_wide(skeleton, transfer_ref[...], NN)
 
 
 def pack_kernel(first, f_ref, x_ref, *refs):
@@ -94,13 +88,16 @@
         far_ref = refs[0]
         size = far_ref.shape[0]
     else:
-        list_ref, count_ref, far_ref, flags_ref = refs
+        list_ref, far_ref, flags_ref, x16_ref = refs
         size = rows - first
-        flags = [jnp.full((FLAG_ROWS, probes), member(list_ref, count_ref, offset), F32) for offset in (-2, -1)]
+        slots = list_ref.shape[1] - 1
+        found = [member(list_ref[:, :slots], list_ref[:, slots:], offset) for offset in OFFSETS]
+        flags = [jnp.broadcast_to(flag, (FLAG_ROWS, probes)) for flag in found[:2]]
         flags.append(jnp.zeros((FLAG_ROWS, width - probes), F32))
         far_ref[size:] = jnp.concatenate(flags, axis=1).astype(BF16)
-        for row, offset in enumerate(OFFSETS):
-            flags_ref[row : row + 1] = jnp.full((1, probes), member(list_ref, count_ref, offset), F32)
+        for row, flag in enumerate(found):
+            flags_ref[row : row + 1] = jnp.broadcast_to(flag, (1, probes))
+        x16_ref[...] = x_ref[...].astype(BF16)
     far_ref[:size, :width] = f_ref[first : first + size]
     far_ref[:size, width:] = x_ref[first : first + size].astype(BF16)
 
@@ -193,19 +190,16 @@
     return (dot(xt16, parts[0], NN) + dot(xt16, parts[1], NN)).T
 
 
-def pair_kernel(scale, f_ref, g_ref, near_ref, x_ref, got_ref, flags_ref, out_ref, pair_ref, xt_ref, xst_ref):
+def pair_kernel(scale, f_ref, g_ref, near_ref, x_ref, xs_ref, flags_ref, out_ref, pair_ref, xt_ref, xst_ref):
     even = bit_of(0) == 0
-    rows, probes = near_ref.shape
-    xt_ref[...] = x_ref[...].T.astype(BF16)
-    halves_of = [got_ref[2 * probes :, half * probes : (half + 1) * probes] for half in range(2)]
-    for half, part in enumerate(halves_of):
-        xst_ref[:, half * (rows // 2) : (half + 1) * (rows // 2)] = part.T.astype(BF16)
+    xt_ref[...] = x_ref[...].T
+    xst_ref[...] = xs_ref[...].T
 
     @pl.when(even)
     def _():
         parts = tile(f_ref[...], g_ref[...], scale)
         flag = flag_of(flags_ref, 1)
-        out_ref[...] = near_ref[...] + flag * times(parts, jnp.concatenate(halves_of, axis=0).astype(BF16))
+        out_ref[...] = near_ref[...] + flag * times(parts, xs_ref[...])
         pair_ref[...] = times_back(parts, xt_ref[...]).astype(BF16)
 
     @pl.when(jnp.logical_not(even))
@@ -286,7 +280,7 @@
 
 def body(features, probes, bases, transfers, couplings, near_list, near_count):
     rows, width = features.shape
-    near_count = near_count.reshape(1, 1)
+    lists = jnp.concatenate([near_list, near_count.reshape(1, 1)], axis=1)
     count = probes.shape[1]
     rank = bases.shape[1]
     depth = transfers.shape[1]
@@ -294,7 +288,7 @@
     scale_g = (3.0 / rank) ** 0.5
     factors = [scale_g * 2.0 ** (-0.5 * (level + 1)) for level in range(depth)]
     shape = jax.ShapeDtypeStruct
-    sizes = [rows // 2, rows // 2]
+    sizes = [rows * 6 // 8, rows * (8 - 6) // 8]
 
     sib_features = partner(features, 0)
     bases_v, transfer0 = call(
@@ -308,22 +302,24 @@
     )
     (message,) = call(
         functools.partial(leaf_kernel, factors[0]),
-        [shape((2 * count + rows // 2, rank), F32)],
+        [shape((2 * count, rank), F32)],
         [VMEM] * 3,
         6 * rows * rank * count,
         bases_v, probes, transfer0,
     )
     gots = [partner(message, 0)]
     packed = []
-    for at, lists in enumerate(([], [near_list, near_count])):
+    for at, more in enumerate(([], [lists])):
         packed += call(
             functools.partial(pack_kernel, sizes[0] * at),
-            [shape((sizes[at] + FLAG_ROWS * at, width + count), BF16)] + [shape((FLAG_ROWS, count), F32)] * at,
-            [VMEM, VMEM] + [SMEM] * len(lists),
+            [shape((sizes[at] + FLAG_ROWS * at, width + count), BF16)]
+            + [shape((FLAG_ROWS, count), F32), shape((rows, count), BF16)][: 2 * at],
+            [VMEM] * (2 + len(more)),
             1000,
-            features, probes, *lists,
+            features, probes, *more,
         )
-    flags = packed.pop()
+    *packed, flags, own_x = packed
+    sib_x = partner(own_x, 0)
     far_first = moved(packed[0], -2)
     far_last = moved(packed[1], -2, wrap=False)
     own = [message]
@@ -356,7 +352,7 @@
         [shape((rows, count), F32), shape((rows, count), BF16)] + [shape((count, rows), BF16)] * 2,
         [VMEM] * 6,
         tile_flops,
-        features, sib_features, near, probes, gots[0], flags,
+        features, sib_features, near, own_x, sib_x, flags,
     )
     heads = []
     for at, (size, part) in enumerate(zip(sizes, (far_first, far_last))):

time: 68.2 us -> 65.1 us (0.955)
  the two profiles are of different devices: /device:TPU:8 before, /device:TPU:12 now
where the time goes in v7:
time: 65.1 us; the launch traced here: 64.9 us
  starting transfers between devices  40.2 us (62%)
  Pallas kernels  12.7 us (20%)
  waiting for transfers between devices  10.8 us (17%)
  between operations  0.94 us (1%)
    ppermute x9, starting transfers between devices, across(): return lax.ppermute(array, 'leaf', [(i, i ^ distance) for i in senders])  33.1 us
    pallas_call x17, Pallas kernels, call(): pl.pallas_call(kernel, out_shape=outs, in_specs=specs, out_specs=[VMEM] *...  12.7 us
    ppermute x3, waiting for transfers between devices, moved(): lax.ppermute(array, 'leaf', [(i, (i + by) % peers) for i in range(peers)...  7.26 us
    ppermute x3, starting transfers between devices, moved(): lax.ppermute(array, 'leaf', [(i, (i + by) % peers) for i in range(peers)...  5.64 us
    ppermute x1, waiting for transfers between devices, body(): gots.append(lax.ppermute(message, 'leaf', whole))  3.56 us
    ppermute x1, starting transfers between devices, body(): gots.append(lax.ppermute(message, 'leaf', whole))  1.47 us
  transfers between devices with their start and end apart: 13, of which 3 were waited for; matrix products, arithmetic and copies ran while one was open for 0% of the time, Pallas kernels for 18%

profile of v7, /device:TPU:12, one launch (start us, length us, event | category | flops | bytes accessed | tf_op | source)
XLA Modules:
  0.0 64.9 jit_solution(3244822609569798364)
XLA Ops:
  0.0 1.2 %shard_map.79 = (f32[512,256]{1,0:T(8,128)S(1)}, f32[256,256]{1,0:T(8,128)S(1)}) custom-call(f32[512,256]{1,0:T(8,128)} %bases_hbm.1, f32[1,4,256,256]{3,2,1,0:T(8,128)} %transfer_ref.15), custom_call_target="tpu_custom_call" | custom-call | flops 1000 | bytes 2359296 | tf_op jit(solution)/shard_map/pallas_call | solution.py:54
  1.3 0.5 shard_map.80.own_ref
  1.8 0.4 collective-permute-start.4
  2.3 0.1 shard_map.74
  2.4 1.5 %collective-permute-start.2 = (bf16[384,1152]{1,0:T(8,128)(2,1)S(1)}, bf16[384,1152]{1,0:T(8,128)(2,1)S(1)}, u32[]{:S(2)}, u32[]{:S(2)}) collective-permute-start(bf16[384,1152]{1,0:T(8,128)(2,1)S(1)} %shard_map.74), channel_id=1, source_target_pairs={{0,30},{1,31},{2,0},{3,1},{4,2},{5,3},{6,4},{7,5},{8,6},{9,7},{10,... | collective-permute-start | bytes 2654216 | tf_op jit(solution)/shard_map/ppermute | solution.py:265
  3.9 0.2 shard_map.81
  4.1 1.5 %collective-permute-start.5 = (bf16[256,256]{1,0:T(8,128)(2,1)S(1)}, bf16[256,256]{1,0:T(8,128)(2,1)S(1)}, u32[]{:S(2)}, u32[]{:S(2)}) collective-permute-start(bf16[256,256]{1,0:T(8,128)(2,1)S(1)} %get-tuple-element.46), channel_id=1, source_target_pairs={{0,4},{1,3},{2,10},{3,1},{4,0},{5,7},{6,14},{7,5},{8,12},{9,11},{1... | collective-permute-start | bytes 393224 | tf_op jit(solution)/shard_map/ppermute | solution.py:338
  5.6 3.6 %collective-permute-done.5.got_ref = bf16[256,256]{1,0:T(8,128)(2,1)S(1)} collective-permute-done((bf16[256,256]{1,0:T(8,128)(2,1)S(1)}, bf16[256,256]{1,0:T(8,128)(2,1)S(1)}, u32[]{:S(2)}, u32[]{:S(2)}) %collective-permute-start.5) | collective-permute-done | bytes 131104 | tf_op jit(solution)/shard_map/ppermute | solution.py:338
  9.1 0.2 shard_map.82
  9.3 0.7 %collective-permute-start.6 = (bf16[256,256]{1,0:T(8,128)(2,1)S(1)}, bf16[256,256]{1,0:T(8,128)(2,1)S(1)}, u32[]{:S(2)}, u32[]{:S(2)}) collective-permute-start(bf16[256,256]{1,0:T(8,128)(2,1)S(1)} %get-tuple-element.48), channel_id=1, source_target_pairs={{1,5},{5,1},{9,13},{13,9},{17,21},{21,17},{25,29},{29,25}} | collective-permute-start | bytes 393224 | tf_op jit(solution)/shard_map/ppermute | solution.py:274
  10.0 0.2 shard_map.83
  10.3 0.7 %collective-permute-start.7 = (bf16[256,256]{1,0:T(8,128)(2,1)S(1)}, bf16[256,256]{1,0:T(8,128)(2,1)S(1)}, u32[]{:S(2)}, u32[]{:S(2)}) collective-permute-start(bf16[256,256]{1,0:T(8,128)(2,1)S(1)} %get-tuple-element.50), channel_id=1, source_target_pairs={{5,13},{13,5},{21,29},{29,21}} | collective-permute-start | bytes 393224 | tf_op jit(solution)/shard_map/ppermute | solution.py:274
  11.6 0.8 %collective-permute-start.8 = (bf16[128,256]{1,0:T(8,128)(2,1)S(1)}, bf16[128,256]{1,0:T(8,128)(2,1)S(1)}, u32[]{:S(2)}, u32[]{:S(2)}) collective-permute-start(bf16[128,256]{1,0:T(8,128)(2,1)S(1)} %shard_map.84), channel_id=1, source_target_pairs={{5,21},{13,29},{21,5},{29,13}} | collective-permute-start | bytes 196616 | tf_op jit(solution)/shard_map/ppermute | solution.py:274
  12.5 0.1 pad_add_fusion.refs_0_
  12.5 0.2 shard_map.73
  12.7 29.1 %collective-permute-start.3 = (bf16[512,128]{1,0:T(8,128)(2,1)S(1)}, bf16[512,128]{1,0:T(8,128)(2,1)S(1)}, u32[]{:S(2)}, u32[]{:S(2)}) collective-permute-start(bf16[512,128]{1,0:T(8,128)(2,1)S(1)} %get-tuple-element.34.x_ref), channel_id=1, source_target_pairs={{0,1},{1,0},{2,3},{3,2},{4,5},{5,4},{6,7},{7,6},{8,9},{9,8},{10,11... | collective-permute-start | bytes 393224 | tf_op jit(solution)/shard_map/ppermute | solution.py:274
  41.8 1.9 %collective-permute-start.1 = (bf16[136,1152]{1,0:T(8,128)(2,1)S(1)}, bf16[136,1152]{1,0:T(8,128)(2,1)S(1)}, u32[]{:S(2)}, u32[]{:S(2)}) collective-permute-start(bf16[136,1152]{1,0:T(8,128)(2,1)S(1)} %get-tuple-element.33), channel_id=1, source_target_pairs={{2,0},{3,1},{4,2},{5,3},{6,4},{7,5},{8,6},{9,7},{10,8},{11,9},{12,... | collective-permute-start | bytes 940040 | tf_op jit(solution)/shard_map/ppermute | solution.py:265
  43.8 0.5 shard_map.85
  44.3 0.7 %collective-permute-start.9 = (bf16[128,256]{1,0:T(8,128)(2,1)S(1)}, bf16[128,256]{1,0:T(8,128)(2,1)S(1)}, u32[]{:S(2)}, u32[]{:S(2)}) collective-permute-start(bf16[128,256]{1,0:T(8,128)(2,1)S(1)} %get-tuple-element.53), channel_id=1, source_target_pairs={{5,1},{13,9},{21,17},{29,25}} | collective-permute-start | bytes 196616 | tf_op jit(solution)/shard_map/ppermute | solution.py:274
  44.9 1.8 %shard_map.75.near_ref = f32[512,128]{1,0:T(8,128)S(1)} custom-call(bf16[512,1024]{1,0:T(8,128)(2,1)S(1)} %copy-done.2, f32[512,128]{1,0:T(8,128)S(1)} %copy-done.3), custom_call_target="tpu_custom_call" | custom-call | flops 805306368 | bytes 1572864 | tf_op jit(solution)/shard_map/pallas_call | solution.py:54
  46.7 0.4 shard_map.86
  47.1 0.7 %collective-permute-start.10 = (bf16[128,256]{1,0:T(8,128)(2,1)S(1)}, bf16[128,256]{1,0:T(8,128)(2,1)S(1)}, u32[]{:S(2)}, u32[]{:S(2)}) collective-permute-start(bf16[128,256]{1,0:T(8,128)(2,1)S(1)} %get-tuple-element.55), channel_id=1, source_target_pairs={{1,3},{5,7},{9,11},{13,15},{17,19},{21,23},{25,27},{29,31}} | collective-permute-start | bytes 196616 | tf_op jit(solution)/shard_map/ppermute | solution.py:274
  47.8 1.4 %shard_map.76 = (f32[512,128]{1,0:T(8,128)S(1)}, bf16[512,128]{1,0:T(8,128)(2,1)S(1)}, bf16[128,512]{1,0:T(8,128)(2,1)S(1)}, bf16[128,512]{1,0:T(8,128)(2,1)S(1)}) custom-call(bf16[512,1024]{1,0:T(8,128)(2,1)S(1)} %copy-done.2, bf16[512,1024]{1,0:T(8,128)(2,1)S(1)} %collective-permute-done.g_ref, f32[512,128]{1,0:T(8,128)S(1)} %shard_map.75.near_ref, ...), custom_call_target="tpu_custom_call" | custom-call | flops 805306368 | bytes 3280896 | tf_op jit(solution)/shard_map/pallas_call | solution.py:54
  49.2 2.1 %shard_map.77 = (f32[512,128]{1,0:T(8,128)S(1)}, f32[512,128]{1,0:T(8,128)S(1)}, f32[384,128]{1,0:T(8,128)S(1)}, f32[384,128]{1,0:T(8,128)S(1)}) custom-call(bf16[512,1024]{1,0:T(8,128)(2,1)S(1)} %copy-done.2, bf16[512,1024]{1,0:T(8,128)(2,1)S(1)} %collective-permute-done.g_ref, bf16[384,1152]{1,0:T(8,128)(2,1)S(1)} %collective-permute-done.2.far_ref, ...), custom_call_target="tpu_custom_call" | custom-call | flops 1207959552 | bytes 4427776 | tf_op jit(solution)/shard_map/pallas_call | solution.py:54
  51.3 1.7 %collective-permute-done.1.far_ref = bf16[136,1152]{1,0:T(8,128)(2,1)S(1)} collective-permute-done((bf16[136,1152]{1,0:T(8,128)(2,1)S(1)}, bf16[136,1152]{1,0:T(8,128)(2,1)S(1)}, u32[]{:S(2)}, u32[]{:S(2)}) %collective-permute-start.1) | collective-permute-done | bytes 313376 | tf_op jit(solution)/shard_map/ppermute | solution.py:265
  53.0 1.8 %shard_map.78 = (f32[512,128]{1,0:T(8,128)S(1)}, bf16[512,128]{1,0:T(8,128)(2,1)S(1)}, bf16[512,128]{1,0:T(8,128)(2,1)S(1)}) custom-call(bf16[512,1024]{1,0:T(8,128)(2,1)S(1)} %copy-done.2, bf16[512,1024]{1,0:T(8,128)(2,1)S(1)} %collective-permute-done.g_ref, bf16[136,1152]{1,0:T(8,128)(2,1)S(1)} %collective-permute-done.1.far_ref, ...), custom_call_target="tpu_custom_call" | custom-call | flops 402653184 | bytes 4118528 | tf_op jit(solution)/shard_map/pallas_call | solution.py:54
  54.9 0.4 shard_map.87
  55.3 0.1 collective-permute-start.11
  55.4 2.2 %collective-permute-start.12 = (bf16[512,128]{1,0:T(8,128)(2,1)S(1)}, bf16[512,128]{1,0:T(8,128)(2,1)S(1)}, u32[]{:S(2)}, u32[]{:S(2)}) collective-permute-start(bf16[512,128]{1,0:T(8,128)(2,1)S(1)} %get-tuple-element.60), channel_id=1, source_target_pairs={{0,2},{1,3},{2,4},{3,5},{4,6},{5,7},{6,8},{7,9},{8,10},{9,11},{10,... | collective-permute-start | bytes 393224 | tf_op jit(solution)/shard_map/ppermute | solution.py:265
  57.6 0.9 %shard_map.88.far_ref = f32[512,128]{1,0:T(8,128)S(1)} custom-call(f32[1,5,256,256]{3,2,1,0:T(8,128)S(1)} %copy-done.1, f32[1,4,256,256]{3,2,1,0:T(8,128)S(1)} %copy-done, f32[512,256]{1,0:T(8,128)S(1)} %get-tuple-element.44.bases_ref, f32[256,256]{1,0:T(8,128)S(1)} %collective-permute-done.4.got_ref, f32[128,256]{1,0:T(8,128)S(1)} %get-tuple-element.58.above_ref, ...), custom_call_target="tpu_custom_call" | custom-call | flops 201326592 | bytes 3932160 | tf_op jit(solution)/shard_map/pallas_call | solution.py:54
  58.5 5.6 %collective-permute-done.12.back_ref = bf16[512,128]{1,0:T(8,128)(2,1)S(1)} collective-permute-done((bf16[512,128]{1,0:T(8,128)(2,1)S(1)}, bf16[512,128]{1,0:T(8,128)(2,1)S(1)}, u32[]{:S(2)}, u32[]{:S(2)}) %collective-permute-start.12) | collective-permute-done | bytes 131104 | tf_op jit(solution)/shard_map/ppermute | solution.py:265
  64.1 0.8 %shard_map.89 = f32[512,128]{1,0:T(8,128)} custom-call(f32[512,128]{1,0:T(8,128)S(1)} %get-tuple-element.43.near_ref, f32[512,128]{1,0:T(8,128)S(1)} %shard_map.88.far_ref, bf16[1536,128]{1,0:T(8,128)(2,1)S(1)} %collective-permute-done.11.sent_ref.sib_ref, bf16[512,128]{1,0:T(8,128)(2,1)S(1)} %collective-permute-done.12.back_ref, ...), custom_call_target="tpu_custom_call" | custom-call | flops 393216 | bytes 1314816 | tf_op jit(solution)/shard_map/pallas_call | solution.py:54
  (22 shorter events, 0.1 us)
Async XLA Ops:
  0.0 2.3 %copy-start.2 = (bf16[512,1024]{1,0:T(8,128)(2,1)S(1)}, bf16[512,1024]{1,0:T(8,128)(2,1)}, u32[]{:S(2)}) copy-start(bf16[512,1024]{1,0:T(8,128)(2,1)} %f_ref.11) | copy-start | bytes 3145732
  0.0 1.3 %copy-start.3 = (f32[512,128]{1,0:T(8,128)S(1)}, f32[512,128]{1,0:T(8,128)}, u32[]{:S(2)}) copy-start(f32[512,128]{1,0:T(8,128)} %x_ref.7) | copy-start | bytes 786436
  0.0 47.8 %collective-permute-start = (bf16[512,1024]{1,0:T(8,128)(2,1)}, bf16[512,1024]{1,0:T(8,128)(2,1)S(1)}, u32[]{:S(2)}, u32[]{:S(2)}) collective-permute-start(bf16[512,1024]{1,0:T(8,128)(2,1)} %f_ref.11), channel_id=1, source_target_pairs={{0,1},{1,0},{2,3},{3,2},{4,5},{5,4},{6,7},{7,6},{8,9},{9,8},{10,11... | collective-permute-start | bytes 3145736 | tf_op jit(solution)/shard_map/ppermute | solution.py:274
  1.8 2.0 %copy-start = (f32[1,4,256,256]{3,2,1,0:T(8,128)S(1)}, f32[1,4,256,256]{3,2,1,0:T(8,128)}, u32[]{:S(2)}) copy-start(f32[1,4,256,256]{3,2,1,0:T(8,128)} %transfer_ref.15) | copy-start | bytes 3145732
  1.8 2.0 %collective-permute-start.4 = (f32[256,256]{1,0:T(8,128)S(1)}, f32[256,256]{1,0:T(8,128)S(1)}, u32[]{:S(2)}, u32[]{:S(2)}) collective-permute-start(f32[256,256]{1,0:T(8,128)S(1)} %shard_map.80.own_ref), channel_id=1, source_target_pairs={{0,1},{1,0},{2,3},{3,2},{4,5},{5,4},{6,7},{7,6},{8,9},{9,8},{10,11... | collective-permute-start | bytes 786440 | tf_op jit(solution)/shard_map/ppermute | solution.py:274
  2.4 46.9 %collective-permute-start.2 = (bf16[384,1152]{1,0:T(8,128)(2,1)S(1)}, bf16[384,1152]{1,0:T(8,128)(2,1)S(1)}, u32[]{:S(2)}, u32[]{:S(2)}) collective-permute-start(bf16[384,1152]{1,0:T(8,128)(2,1)S(1)} %shard_map.74), channel_id=1, source_target_pairs={{0,30},{1,31},{2,0},{3,1},{4,2},{5,3},{6,4},{7,5},{8,6},{9,7},{10,... | collective-permute-start | bytes 2654216 | tf_op jit(solution)/shard_map/ppermute | solution.py:265
  4.1 5.0 %collective-permute-start.5 = (bf16[256,256]{1,0:T(8,128)(2,1)S(1)}, bf16[256,256]{1,0:T(8,128)(2,1)S(1)}, u32[]{:S(2)}, u32[]{:S(2)}) collective-permute-start(bf16[256,256]{1,0:T(8,128)(2,1)S(1)} %get-tuple-element.46), channel_id=1, source_target_pairs={{0,4},{1,3},{2,10},{3,1},{4,0},{5,7},{6,14},{7,5},{8,12},{9,11},{1... | collective-permute-start | bytes 393224 | tf_op jit(solution)/shard_map/ppermute | solution.py:338
  9.3 0.7 %collective-permute-start.6 = (bf16[256,256]{1,0:T(8,128)(2,1)S(1)}, bf16[256,256]{1,0:T(8,128)(2,1)S(1)}, u32[]{:S(2)}, u32[]{:S(2)}) collective-permute-start(bf16[256,256]{1,0:T(8,128)(2,1)S(1)} %get-tuple-element.48), channel_id=1, source_target_pairs={{1,5},{5,1},{9,13},{13,9},{17,21},{21,17},{25,29},{29,25}} | collective-permute-start | bytes 393224 | tf_op jit(solution)/shard_map/ppermute | solution.py:274
  10.0 2.4 %copy-start.4 = (s32[1,4]{1,0:T(1,128)S(1)}, s32[1,4]{1,0:T(1,128)}, u32[]{:S(2)}) copy-start(s32[1,4]{1,0:T(1,128)} %param.12) | copy-start | bytes 52
  10.3 1.3 %collective-permute-start.7 = (bf16[256,256]{1,0:T(8,128)(2,1)S(1)}, bf16[256,256]{1,0:T(8,128)(2,1)S(1)}, u32[]{:S(2)}, u32[]{:S(2)}) collective-permute-start(bf16[256,256]{1,0:T(8,128)(2,1)S(1)} %get-tuple-element.50), channel_id=1, source_target_pairs={{5,13},{13,5},{21,29},{29,21}} | collective-permute-start | bytes 393224 | tf_op jit(solution)/shard_map/ppermute | solution.py:274
  11.6 32.1 %copy-start.1 = (f32[1,5,256,256]{3,2,1,0:T(8,128)S(1)}, f32[1,5,256,256]{3,2,1,0:T(8,128)}, u32[]{:S(2)}) copy-start(f32[1,5,256,256]{3,2,1,0:T(8,128)} %coupling_ref.7) | copy-start | bytes 3932164
  11.6 32.1 %collective-permute-start.8 = (bf16[128,256]{1,0:T(8,128)(2,1)S(1)}, bf16[128,256]{1,0:T(8,128)(2,1)S(1)}, u32[]{:S(2)}, u32[]{:S(2)}) collective-permute-start(bf16[128,256]{1,0:T(8,128)(2,1)S(1)} %shard_map.84), channel_id=1, source_target_pairs={{5,21},{13,29},{21,5},{29,13}} | collective-permute-start | bytes 196616 | tf_op jit(solution)/shard_map/ppermute | solution.py:274
  12.7 35.1 %collective-permute-start.3 = (bf16[512,128]{1,0:T(8,128)(2,1)S(1)}, bf16[512,128]{1,0:T(8,128)(2,1)S(1)}, u32[]{:S(2)}, u32[]{:S(2)}) collective-permute-start(bf16[512,128]{1,0:T(8,128)(2,1)S(1)} %get-tuple-element.34.x_ref), channel_id=1, source_target_pairs={{0,1},{1,0},{2,3},{3,2},{4,5},{5,4},{6,7},{7,6},{8,9},{9,8},{10,11... | collective-permute-start | bytes 393224 | tf_op jit(solution)/shard_map/ppermute | solution.py:274
  41.8 11.2 %collective-permute-start.1 = (bf16[136,1152]{1,0:T(8,128)(2,1)S(1)}, bf16[136,1152]{1,0:T(8,128)(2,1)S(1)}, u32[]{:S(2)}, u32[]{:S(2)}) collective-permute-start(bf16[136,1152]{1,0:T(8,128)(2,1)S(1)} %get-tuple-element.33), channel_id=1, source_target_pairs={{2,0},{3,1},{4,2},{5,3},{6,4},{7,5},{8,6},{9,7},{10,8},{11,9},{12,... | collective-permute-start | bytes 940040 | tf_op jit(solution)/shard_map/ppermute | solution.py:265
  44.3 2.5 %collective-permute-start.9 = (bf16[128,256]{1,0:T(8,128)(2,1)S(1)}, bf16[128,256]{1,0:T(8,128)(2,1)S(1)}, u32[]{:S(2)}, u32[]{:S(2)}) collective-permute-start(bf16[128,256]{1,0:T(8,128)(2,1)S(1)} %get-tuple-element.53), channel_id=1, source_target_pairs={{5,1},{13,9},{21,17},{29,25}} | collective-permute-start | bytes 196616 | tf_op jit(solution)/shard_map/ppermute | solution.py:274
  47.1 7.8 %collective-permute-start.10 = (bf16[128,256]{1,0:T(8,128)(2,1)S(1)}, bf16[128,256]{1,0:T(8,128)(2,1)S(1)}, u32[]{:S(2)}, u32[]{:S(2)}) collective-permute-start(bf16[128,256]{1,0:T(8,128)(2,1)S(1)} %get-tuple-element.55), channel_id=1, source_target_pairs={{1,3},{5,7},{9,11},{13,15},{17,19},{21,23},{25,27},{29,31}} | collective-permute-start | bytes 196616 | tf_op jit(solution)/shard_map/ppermute | solution.py:274
  55.3 2.3 %collective-permute-start.11 = (bf16[1536,128]{1,0:T(8,128)(2,1)S(1)}, bf16[1536,128]{1,0:T(8,128)(2,1)S(1)}, u32[]{:S(2)}, u32[]{:S(2)}) collective-permute-start(bf16[1536,128]{1,0:T(8,128)(2,1)S(1)} %get-tuple-element.59), channel_id=1, source_target_pairs={{0,1},{1,0},{2,3},{3,2},{4,5},{5,4},{6,7},{7,6},{8,9},{9,8},{10,11... | collective-permute-start | bytes 1179656 | tf_op jit(solution)/shard_map/ppermute | solution.py:274
  55.4 8.7 %collective-permute-start.12 = (bf16[512,128]{1,0:T(8,128)(2,1)S(1)}, bf16[512,128]{1,0:T(8,128)(2,1)S(1)}, u32[]{:S(2)}, u32[]{:S(2)}) collective-permute-start(bf16[512,128]{1,0:T(8,128)(2,1)S(1)} %get-tuple-element.60), channel_id=1, source_target_pairs={{0,2},{1,3},{2,4},{3,5},{4,6},{5,7},{6,8},{7,9},{8,10},{9,11},{10,... | collective-permute-start | bytes 393224 | tf_op jit(solution)/shard_map/ppermute | solution.py:265

commit v8 on v7

--- a/solution.py
+++ b/solution.py
@@ -159,7 +159,7 @@
             at += probes
 
 
-def down_kernel(scale_g, factor, coupling_ref, transfer_ref, bases_ref, got_ref, above_ref, sent_ref, out_ref):
+def down_kernel(scale_g, factor, coupling_ref, transfer_ref, bases_ref, got_ref, above_ref, sent_ref, near_ref, flags_ref, out_ref):
     rows, probes = out_ref.shape
     rank = bases_ref.shape[1]
     high, low = [
@@ -168,7 +168,9 @@
     ]
     above = jnp.where(bit_of(0) == 1, above_ref[...], high + low)
     expansion = descend(scale_g, factor, got_ref[:probes], coupling_ref[0, 0], transfer_ref[0, 0], above)
-    out_ref[...] = dot_wide(bases_ref[...], expansion, NT)
+    after, before = flag_of(flags_ref, 1), flag_of(flags_ref, -1)
+    sib = after * sent_ref[:rows].astype(F32) + before * sent_ref[rows : 2 * rows].astype(F32)
+    out_ref[...] = near_ref[...] + sib + dot_wide(bases_ref[...], expansion, NT)
 
 
 def tile(rows_a, rows_b, scale):
@@ -249,11 +251,8 @@
         put(times_back(parts, xt_ref[...]), None)
 
 
-def final_kernel(near_ref, far_ref, sib_ref, back_ref, flags_ref, out_ref):
-    rows = out_ref.shape[0]
-    after, before = flag_of(flags_ref, 1), flag_of(flags_ref, -1)
-    sib = after * sib_ref[:rows].astype(F32) + before * sib_ref[rows : 2 * rows].astype(F32)
-    out_ref[...] = near_ref[...] + far_ref[...] + sib + back_ref[...].astype(F32)
+def final_kernel(sum_ref, back_ref, out_ref):
+    out_ref[...] = sum_ref[...] + back_ref[...].astype(F32)
 
 
 def sender(index, bits):
@@ -266,7 +265,7 @@
 
 
 def level1_partner(index):
-    return index ^ (2 if index & 1 else 8 if index & 2 else 4)
+    return index ^ (2 if index & 1 else 4)
 
 
 def across(array, distance, bits=()):
@@ -394,16 +393,16 @@
     (far_sum,) = call(
         functools.partial(down_kernel, scale_g, factors[0]),
         [shape((rows, count), F32)],
-        [VMEM] * 6,
+        [VMEM] * 8,
         2 * product_flops + 6 * rows * rank * count,
-        couplings, transfers, bases_v, gots[0], e1, sib_got,
+        couplings, transfers, bases_v, gots[0], e1, sib_got, near, flags,
     )
     (out,) = call(
         final_kernel,
         [shape((rows, count), F32)],
-        [VMEM] * 5,
+        [VMEM] * 2,
         6 * rows * count,
-        near, far_sum, sib_got, back, flags,
+        far_sum, back,
     )
     return out
 

time: 65.1 us -> 65.1 us (level)
  no operation moved by 1% of the time
where the time goes in v8:
time: 65.1 us; the launch traced here: 64.8 us
  starting transfers between devices  40.2 us (62%)
  Pallas kernels  12.7 us (20%)
  waiting for transfers between devices  10.8 us (17%)
  between operations  0.94 us (1%)
    ppermute x9, starting transfers between devices, across(): return lax.ppermute(array, 'leaf', [(i, i ^ distance) for i in senders])  33.1 us
    pallas_call x17, Pallas kernels, call(): pl.pallas_call(kernel, out_shape=outs, in_specs=specs, out_specs=[VMEM] *...  12.7 us
    ppermute x3, waiting for transfers between devices, moved(): lax.ppermute(array, 'leaf', [(i, (i + by) % peers) for i in range(peers)...  7.24 us
    ppermute x3, starting transfers between devices, moved(): lax.ppermute(array, 'leaf', [(i, (i + by) % peers) for i in range(peers)...  5.64 us
    ppermute x1, waiting for transfers between devices, body(): gots.append(lax.ppermute(message, 'leaf', whole))  3.56 us
    ppermute x1, starting transfers between devices, body(): gots.append(lax.ppermute(message, 'leaf', whole))  1.47 us
  transfers between devices with their start and end apart: 13, of which 3 were waited for; matrix products, arithmetic and copies ran while one was open for 0% of the time, Pallas kernels for 18%

profile of v8, /device:TPU:12, one launch (start us, length us, event | category | flops | bytes accessed | tf_op | source)
XLA Modules:
  0.0 64.8 jit_solution(4789672891087966162)
XLA Ops:
  0.0 1.2 %shard_map.73 = (f32[512,256]{1,0:T(8,128)S(1)}, f32[256,256]{1,0:T(8,128)S(1)}) custom-call(f32[512,256]{1,0:T(8,128)} %bases_hbm.1, f32[1,4,256,256]{3,2,1,0:T(8,128)} %transfer_ref.15), custom_call_target="tpu_custom_call" | custom-call | flops 1000 | bytes 2359296 | tf_op jit(solution)/shard_map/pallas_call | solution.py:54
  1.3 0.5 shard_map.74.own_ref
  1.8 0.4 collective-permute-start
  2.3 0.1 shard_map.82
  2.4 1.5 %collective-permute-start.9 = (bf16[384,1152]{1,0:T(8,128)(2,1)S(1)}, bf16[384,1152]{1,0:T(8,128)(2,1)S(1)}, u32[]{:S(2)}, u32[]{:S(2)}) collective-permute-start(bf16[384,1152]{1,0:T(8,128)(2,1)S(1)} %shard_map.82), channel_id=1, source_target_pairs={{0,30},{1,31},{2,0},{3,1},{4,2},{5,3},{6,4},{7,5},{8,6},{9,7},{10,... | collective-permute-start | bytes 2654216 | tf_op jit(solution)/shard_map/ppermute | solution.py:264
  3.9 0.2 shard_map.75
  4.1 1.5 %collective-permute-start.1 = (bf16[256,256]{1,0:T(8,128)(2,1)S(1)}, bf16[256,256]{1,0:T(8,128)(2,1)S(1)}, u32[]{:S(2)}, u32[]{:S(2)}) collective-permute-start(bf16[256,256]{1,0:T(8,128)(2,1)S(1)} %get-tuple-element.35), channel_id=1, source_target_pairs={{0,4},{1,3},{2,6},{3,1},{4,0},{5,7},{6,2},{7,5},{8,12},{9,11},{10,... | collective-permute-start | bytes 393224 | tf_op jit(solution)/shard_map/ppermute | solution.py:337
  5.6 3.6 %collective-permute-done.1.got_ref = bf16[256,256]{1,0:T(8,128)(2,1)S(1)} collective-permute-done((bf16[256,256]{1,0:T(8,128)(2,1)S(1)}, bf16[256,256]{1,0:T(8,128)(2,1)S(1)}, u32[]{:S(2)}, u32[]{:S(2)}) %collective-permute-start.1) | collective-permute-done | bytes 131104 | tf_op jit(solution)/shard_map/ppermute | solution.py:337
  9.1 0.2 shard_map.76
  9.3 0.7 %collective-permute-start.2 = (bf16[256,256]{1,0:T(8,128)(2,1)S(1)}, bf16[256,256]{1,0:T(8,128)(2,1)S(1)}, u32[]{:S(2)}, u32[]{:S(2)}) collective-permute-start(bf16[256,256]{1,0:T(8,128)(2,1)S(1)} %get-tuple-element.37), channel_id=1, source_target_pairs={{1,5},{5,1},{9,13},{13,9},{17,21},{21,17},{25,29},{29,25}} | collective-permute-start | bytes 393224 | tf_op jit(solution)/shard_map/ppermute | solution.py:273
  10.0 0.2 shard_map.77
  10.3 0.7 %collective-permute-start.3 = (bf16[256,256]{1,0:T(8,128)(2,1)S(1)}, bf16[256,256]{1,0:T(8,128)(2,1)S(1)}, u32[]{:S(2)}, u32[]{:S(2)}) collective-permute-start(bf16[256,256]{1,0:T(8,128)(2,1)S(1)} %get-tuple-element.39), channel_id=1, source_target_pairs={{5,13},{13,5},{21,29},{29,21}} | collective-permute-start | bytes 393224 | tf_op jit(solution)/shard_map/ppermute | solution.py:273
  11.6 0.8 %collective-permute-start.4 = (bf16[128,256]{1,0:T(8,128)(2,1)S(1)}, bf16[128,256]{1,0:T(8,128)(2,1)S(1)}, u32[]{:S(2)}, u32[]{:S(2)}) collective-permute-start(bf16[128,256]{1,0:T(8,128)(2,1)S(1)} %shard_map.78), channel_id=1, source_target_pairs={{5,21},{13,29},{21,5},{29,13}} | collective-permute-start | bytes 196616 | tf_op jit(solution)/shard_map/ppermute | solution.py:273
  12.5 0.1 pad_add_fusion.refs_0_
  12.5 0.2 shard_map.81
  12.7 29.1 %collective-permute-start.10 = (bf16[512,128]{1,0:T(8,128)(2,1)S(1)}, bf16[512,128]{1,0:T(8,128)(2,1)S(1)}, u32[]{:S(2)}, u32[]{:S(2)}) collective-permute-start(bf16[512,128]{1,0:T(8,128)(2,1)S(1)} %get-tuple-element.46.x_ref), channel_id=1, source_target_pairs={{0,1},{1,0},{2,3},{3,2},{4,5},{5,4},{6,7},{7,6},{8,9},{9,8},{10,11... | collective-permute-start | bytes 393224 | tf_op jit(solution)/shard_map/ppermute | solution.py:273
  41.8 1.9 %collective-permute-start.8 = (bf16[136,1152]{1,0:T(8,128)(2,1)S(1)}, bf16[136,1152]{1,0:T(8,128)(2,1)S(1)}, u32[]{:S(2)}, u32[]{:S(2)}) collective-permute-start(bf16[136,1152]{1,0:T(8,128)(2,1)S(1)} %get-tuple-element.45), channel_id=1, source_target_pairs={{2,0},{3,1},{4,2},{5,3},{6,4},{7,5},{8,6},{9,7},{10,8},{11,9},{12,... | collective-permute-start | bytes 940040 | tf_op jit(solution)/shard_map/ppermute | solution.py:264
  43.8 0.5 shard_map.79
  44.3 0.7 %collective-permute-start.5 = (bf16[128,256]{1,0:T(8,128)(2,1)S(1)}, bf16[128,256]{1,0:T(8,128)(2,1)S(1)}, u32[]{:S(2)}, u32[]{:S(2)}) collective-permute-start(bf16[128,256]{1,0:T(8,128)(2,1)S(1)} %get-tuple-element.42), channel_id=1, source_target_pairs={{5,1},{13,9},{21,17},{29,25}} | collective-permute-start | bytes 196616 | tf_op jit(solution)/shard_map/ppermute | solution.py:273
  44.9 1.8 %shard_map.83.near_ref = f32[512,128]{1,0:T(8,128)S(1)} custom-call(bf16[512,1024]{1,0:T(8,128)(2,1)S(1)} %copy-done.2, f32[512,128]{1,0:T(8,128)S(1)} %copy-done.3), custom_call_target="tpu_custom_call" | custom-call | flops 805306368 | bytes 1572864 | tf_op jit(solution)/shard_map/pallas_call | solution.py:54
  46.7 0.4 shard_map.80
  47.1 0.7 %collective-permute-start.6 = (bf16[128,256]{1,0:T(8,128)(2,1)S(1)}, bf16[128,256]{1,0:T(8,128)(2,1)S(1)}, u32[]{:S(2)}, u32[]{:S(2)}) collective-permute-start(bf16[128,256]{1,0:T(8,128)(2,1)S(1)} %get-tuple-element.44), channel_id=1, source_target_pairs={{1,3},{5,7},{9,11},{13,15},{17,19},{21,23},{25,27},{29,31}} | collective-permute-start | bytes 196616 | tf_op jit(solution)/shard_map/ppermute | solution.py:273
  47.8 1.4 %shard_map.84 = (f32[512,128]{1,0:T(8,128)S(1)}, bf16[512,128]{1,0:T(8,128)(2,1)S(1)}, bf16[128,512]{1,0:T(8,128)(2,1)S(1)}, bf16[128,512]{1,0:T(8,128)(2,1)S(1)}) custom-call(bf16[512,1024]{1,0:T(8,128)(2,1)S(1)} %copy-done.2, bf16[512,1024]{1,0:T(8,128)(2,1)S(1)} %collective-permute-done.7.g_ref, f32[512,128]{1,0:T(8,128)S(1)} %shard_map.83.near_ref, ...), custom_call_target="tpu_custom_call" | custom-call | flops 805306368 | bytes 3280896 | tf_op jit(solution)/shard_map/pallas_call | solution.py:54
  49.2 2.1 %shard_map.85 = (f32[512,128]{1,0:T(8,128)S(1)}, f32[512,128]{1,0:T(8,128)S(1)}, f32[384,128]{1,0:T(8,128)S(1)}, f32[384,128]{1,0:T(8,128)S(1)}) custom-call(bf16[512,1024]{1,0:T(8,128)(2,1)S(1)} %copy-done.2, bf16[512,1024]{1,0:T(8,128)(2,1)S(1)} %collective-permute-done.7.g_ref, bf16[384,1152]{1,0:T(8,128)(2,1)S(1)} %collective-permute-done.9.far_ref, ...), custom_call_target="tpu_custom_call" | custom-call | flops 1207959552 | bytes 4427776 | tf_op jit(solution)/shard_map/pallas_call | solution.py:54
  51.3 1.7 %collective-permute-done.8.far_ref = bf16[136,1152]{1,0:T(8,128)(2,1)S(1)} collective-permute-done((bf16[136,1152]{1,0:T(8,128)(2,1)S(1)}, bf16[136,1152]{1,0:T(8,128)(2,1)S(1)}, u32[]{:S(2)}, u32[]{:S(2)}) %collective-permute-start.8) | collective-permute-done | bytes 313376 | tf_op jit(solution)/shard_map/ppermute | solution.py:264
  53.0 1.8 %shard_map.86 = (f32[512,128]{1,0:T(8,128)S(1)}, bf16[512,128]{1,0:T(8,128)(2,1)S(1)}, bf16[512,128]{1,0:T(8,128)(2,1)S(1)}) custom-call(bf16[512,1024]{1,0:T(8,128)(2,1)S(1)} %copy-done.2, bf16[512,1024]{1,0:T(8,128)(2,1)S(1)} %collective-permute-done.7.g_ref, bf16[136,1152]{1,0:T(8,128)(2,1)S(1)} %collective-permute-done.8.far_ref, ...), custom_call_target="tpu_custom_call" | custom-call | flops 402653184 | bytes 4118528 | tf_op jit(solution)/shard_map/pallas_call | solution.py:54
  54.9 0.4 shard_map.87
  55.3 0.1 collective-permute-start.11
  55.4 2.2 %collective-permute-start.12 = (bf16[512,128]{1,0:T(8,128)(2,1)S(1)}, bf16[512,128]{1,0:T(8,128)(2,1)S(1)}, u32[]{:S(2)}, u32[]{:S(2)}) collective-permute-start(bf16[512,128]{1,0:T(8,128)(2,1)S(1)} %get-tuple-element.60), channel_id=1, source_target_pairs={{0,2},{1,3},{2,4},{3,5},{4,6},{5,7},{6,8},{7,9},{8,10},{9,11},{10,... | collective-permute-start | bytes 393224 | tf_op jit(solution)/shard_map/ppermute | solution.py:264
  57.6 0.9 %shard_map.88.sum_ref = f32[512,128]{1,0:T(8,128)S(1)} custom-call(f32[1,5,256,256]{3,2,1,0:T(8,128)S(1)} %copy-done.1, f32[1,4,256,256]{3,2,1,0:T(8,128)S(1)} %copy-done, f32[512,256]{1,0:T(8,128)S(1)} %get-tuple-element.33.bases_ref, f32[256,256]{1,0:T(8,128)S(1)} %collective-permute-done.got_ref, f32[128,256]{1,0:T(8,128)S(1)} %get-tuple-element.57.above_ref, ...), custom_call_target="tpu_custom_call" | custom-call | flops 201326592 | bytes 4198400 | tf_op jit(solution)/shard_map/pallas_call | solution.py:54
  58.5 5.5 %collective-permute-done.12.back_ref = bf16[512,128]{1,0:T(8,128)(2,1)S(1)} collective-permute-done((bf16[512,128]{1,0:T(8,128)(2,1)S(1)}, bf16[512,128]{1,0:T(8,128)(2,1)S(1)}, u32[]{:S(2)}, u32[]{:S(2)}) %collective-permute-start.12) | collective-permute-done | bytes 131104 | tf_op jit(solution)/shard_map/ppermute | solution.py:264
  64.1 0.7 %shard_map.89 = f32[512,128]{1,0:T(8,128)} custom-call(f32[512,128]{1,0:T(8,128)S(1)} %shard_map.88.sum_ref, bf16[512,128]{1,0:T(8,128)(2,1)S(1)} %collective-permute-done.12.back_ref), custom_call_target="tpu_custom_call" | custom-call | flops 393216 | bytes 655360 | tf_op jit(solution)/shard_map/pallas_call | solution.py:54
  (22 shorter events, 0.1 us)
Async XLA Ops:
  0.0 2.3 %copy-start.2 = (bf16[512,1024]{1,0:T(8,128)(2,1)S(1)}, bf16[512,1024]{1,0:T(8,128)(2,1)}, u32[]{:S(2)}) copy-start(bf16[512,1024]{1,0:T(8,128)(2,1)} %f_ref.11) | copy-start | bytes 3145732
  0.0 1.3 %copy-start.3 = (f32[512,128]{1,0:T(8,128)S(1)}, f32[512,128]{1,0:T(8,128)}, u32[]{:S(2)}) copy-start(f32[512,128]{1,0:T(8,128)} %x_ref.7) | copy-start | bytes 786436
  0.0 47.8 %collective-permute-start.7 = (bf16[512,1024]{1,0:T(8,128)(2,1)}, bf16[512,1024]{1,0:T(8,128)(2,1)S(1)}, u32[]{:S(2)}, u32[]{:S(2)}) collective-permute-start(bf16[512,1024]{1,0:T(8,128)(2,1)} %f_ref.11), channel_id=1, source_target_pairs={{0,1},{1,0},{2,3},{3,2},{4,5},{5,4},{6,7},{7,6},{8,9},{9,8},{10,11... | collective-permute-start | bytes 3145736 | tf_op jit(solution)/shard_map/ppermute | solution.py:273
  1.8 2.0 %copy-start = (f32[1,4,256,256]{3,2,1,0:T(8,128)S(1)}, f32[1,4,256,256]{3,2,1,0:T(8,128)}, u32[]{:S(2)}) copy-start(f32[1,4,256,256]{3,2,1,0:T(8,128)} %transfer_ref.15) | copy-start | bytes 3145732
  1.8 2.0 %collective-permute-start = (f32[256,256]{1,0:T(8,128)S(1)}, f32[256,256]{1,0:T(8,128)S(1)}, u32[]{:S(2)}, u32[]{:S(2)}) collective-permute-start(f32[256,256]{1,0:T(8,128)S(1)} %shard_map.74.own_ref), channel_id=1, source_target_pairs={{0,1},{1,0},{2,3},{3,2},{4,5},{5,4},{6,7},{7,6},{8,9},{9,8},{10,11... | collective-permute-start | bytes 786440 | tf_op jit(solution)/shard_map/ppermute | solution.py:273
  2.4 46.9 %collective-permute-start.9 = (bf16[384,1152]{1,0:T(8,128)(2,1)S(1)}, bf16[384,1152]{1,0:T(8,128)(2,1)S(1)}, u32[]{:S(2)}, u32[]{:S(2)}) collective-permute-start(bf16[384,1152]{1,0:T(8,128)(2,1)S(1)} %shard_map.82), channel_id=1, source_target_pairs={{0,30},{1,31},{2,0},{3,1},{4,2},{5,3},{6,4},{7,5},{8,6},{9,7},{10,... | collective-permute-start | bytes 2654216 | tf_op jit(solution)/shard_map/ppermute | solution.py:264
  4.1 5.0 %collective-permute-start.1 = (bf16[256,256]{1,0:T(8,128)(2,1)S(1)}, bf16[256,256]{1,0:T(8,128)(2,1)S(1)}, u32[]{:S(2)}, u32[]{:S(2)}) collective-permute-start(bf16[256,256]{1,0:T(8,128)(2,1)S(1)} %get-tuple-element.35), channel_id=1, source_target_pairs={{0,4},{1,3},{2,6},{3,1},{4,0},{5,7},{6,2},{7,5},{8,12},{9,11},{10,... | collective-permute-start | bytes 393224 | tf_op jit(solution)/shard_map/ppermute | solution.py:337
  9.3 0.7 %collective-permute-start.2 = (bf16[256,256]{1,0:T(8,128)(2,1)S(1)}, bf16[256,256]{1,0:T(8,128)(2,1)S(1)}, u32[]{:S(2)}, u32[]{:S(2)}) collective-permute-start(bf16[256,256]{1,0:T(8,128)(2,1)S(1)} %get-tuple-element.37), channel_id=1, source_target_pairs={{1,5},{5,1},{9,13},{13,9},{17,21},{21,17},{25,29},{29,25}} | collective-permute-start | bytes 393224 | tf_op jit(solution)/shard_map/ppermute | solution.py:273
  10.0 2.4 %copy-start.4 = (s32[1,4]{1,0:T(1,128)S(1)}, s32[1,4]{1,0:T(1,128)}, u32[]{:S(2)}) copy-start(s32[1,4]{1,0:T(1,128)} %param.12) | copy-start | bytes 52
  10.3 1.3 %collective-permute-start.3 = (bf16[256,256]{1,0:T(8,128)(2,1)S(1)}, bf16[256,256]{1,0:T(8,128)(2,1)S(1)}, u32[]{:S(2)}, u32[]{:S(2)}) collective-permute-start(bf16[256,256]{1,0:T(8,128)(2,1)S(1)} %get-tuple-element.39), channel_id=1, source_target_pairs={{5,13},{13,5},{21,29},{29,21}} | collective-permute-start | bytes 393224 | tf_op jit(solution)/shard_map/ppermute | solution.py:273
  11.6 32.1 %copy-start.1 = (f32[1,5,256,256]{3,2,1,0:T(8,128)S(1)}, f32[1,5,256,256]{3,2,1,0:T(8,128)}, u32[]{:S(2)}) copy-start(f32[1,5,256,256]{3,2,1,0:T(8,128)} %coupling_ref.7) | copy-start | bytes 3932164
  11.6 32.1 %collective-permute-start.4 = (bf16[128,256]{1,0:T(8,128)(2,1)S(1)}, bf16[128,256]{1,0:T(8,128)(2,1)S(1)}, u32[]{:S(2)}, u32[]{:S(2)}) collective-permute-start(bf16[128,256]{1,0:T(8,128)(2,1)S(1)} %shard_map.78), channel_id=1, source_target_pairs={{5,21},{13,29},{21,5},{29,13}} | collective-permute-start | bytes 196616 | tf_op jit(solution)/shard_map/ppermute | solution.py:273
  12.7 35.1 %collective-permute-start.10 = (bf16[512,128]{1,0:T(8,128)(2,1)S(1)}, bf16[512,128]{1,0:T(8,128)(2,1)S(1)}, u32[]{:S(2)}, u32[]{:S(2)}) collective-permute-start(bf16[512,128]{1,0:T(8,128)(2,1)S(1)} %get-tuple-element.46.x_ref), channel_id=1, source_target_pairs={{0,1},{1,0},{2,3},{3,2},{4,5},{5,4},{6,7},{7,6},{8,9},{9,8},{10,11... | collective-permute-start | bytes 393224 | tf_op jit(solution)/shard_map/ppermute | solution.py:273
  41.8 11.2 %collective-permute-start.8 = (bf16[136,1152]{1,0:T(8,128)(2,1)S(1)}, bf16[136,1152]{1,0:T(8,128)(2,1)S(1)}, u32[]{:S(2)}, u32[]{:S(2)}) collective-permute-start(bf16[136,1152]{1,0:T(8,128)(2,1)S(1)} %get-tuple-element.45), channel_id=1, source_target_pairs={{2,0},{3,1},{4,2},{5,3},{6,4},{7,5},{8,6},{9,7},{10,8},{11,9},{12,... | collective-permute-start | bytes 940040 | tf_op jit(solution)/shard_map/ppermute | solution.py:264
  44.3 2.5 %collective-permute-start.5 = (bf16[128,256]{1,0:T(8,128)(2,1)S(1)}, bf16[128,256]{1,0:T(8,128)(2,1)S(1)}, u32[]{:S(2)}, u32[]{:S(2)}) collective-permute-start(bf16[128,256]{1,0:T(8,128)(2,1)S(1)} %get-tuple-element.42), channel_id=1, source_target_pairs={{5,1},{13,9},{21,17},{29,25}} | collective-permute-start | bytes 196616 | tf_op jit(solution)/shard_map/ppermute | solution.py:273
  47.1 7.8 %collective-permute-start.6 = (bf16[128,256]{1,0:T(8,128)(2,1)S(1)}, bf16[128,256]{1,0:T(8,128)(2,1)S(1)}, u32[]{:S(2)}, u32[]{:S(2)}) collective-permute-start(bf16[128,256]{1,0:T(8,128)(2,1)S(1)} %get-tuple-element.44), channel_id=1, source_target_pairs={{1,3},{5,7},{9,11},{13,15},{17,19},{21,23},{25,27},{29,31}} | collective-permute-start | bytes 196616 | tf_op jit(solution)/shard_map/ppermute | solution.py:273
  55.3 2.3 %collective-permute-start.11 = (bf16[1536,128]{1,0:T(8,128)(2,1)S(1)}, bf16[1536,128]{1,0:T(8,128)(2,1)S(1)}, u32[]{:S(2)}, u32[]{:S(2)}) collective-permute-start(bf16[1536,128]{1,0:T(8,128)(2,1)S(1)} %get-tuple-element.58), channel_id=1, source_target_pairs={{0,1},{1,0},{2,3},{3,2},{4,5},{5,4},{6,7},{7,6},{8,9},{9,8},{10,11... | collective-permute-start | bytes 1179656 | tf_op jit(solution)/shard_map/ppermute | solution.py:273
  55.4 8.7 %collective-permute-start.12 = (bf16[512,128]{1,0:T(8,128)(2,1)S(1)}, bf16[512,128]{1,0:T(8,128)(2,1)S(1)}, u32[]{:S(2)}, u32[]{:S(2)}) collective-permute-start(bf16[512,128]{1,0:T(8,128)(2,1)S(1)} %get-tuple-element.60), channel_id=1, source_target_pairs={{0,2},{1,3},{2,4},{3,5},{4,6},{5,7},{6,8},{7,9},{8,10},{9,11},{10,... | collective-permute-start | bytes 393224 | tf_op jit(solution)/shard_map/ppermute | solution.py:264
